TPU v7x, 32 devices: a whole 2x2x4 slice. The times are simulated.
32 devices in a mesh: row: 16 (over z, y, x), col: 2 (over core).
Axes of the slice: x: 2, y: 2, z: 4, core: 2. Of those that a mesh axis runs over, the one named last changes fastest.
Arguments:
- tokens: bfloat16 [16400, 1024], P('row', 'col'), may hold values from -6 to 6
- norm1_gain: bfloat16 [1024], P('row'), may hold values from 0.099609375 to 1.8984375
- norm1_bias: bfloat16 [1024], P('row'), may hold values from -1.75 to 1.75
- qkv_weight: bfloat16 [1024, 3, 1024], P('row', None, 'col'), may hold values from -0.1875 to 0.1875
- query_bias: bfloat16 [1024], P('col'), may hold values from -1.75 to 1.75
- value_bias: bfloat16 [1024], P('col'), may hold values from -0.3125 to 0.3125
- proj_weight: bfloat16 [1024, 1024], P('col', 'row'), may hold values from -6 to 6
- proj_bias: bfloat16 [1024], P('row'), may hold values from -1.75 to 1.75
- norm2_gain: bfloat16 [1024], P('row'), may hold values from 0.099609375 to 1.8984375
- norm2_bias: bfloat16 [1024], P('row'), may hold values from -1.75 to 1.75
- gate_weight: bfloat16 [1024, 2730], P('row', 'col'), may hold values from -0.1875 to 0.1875
- gate_bias: bfloat16 [2730], P('col'), may hold values from -1.75 to 1.75
- up_weight: bfloat16 [1024, 2730], P('row', 'col'), may hold values from -0.1875 to 0.1875
- up_bias: bfloat16 [2730], P('col'), may hold values from -1.75 to 1.75
- inner_gain: bfloat16 [2730], P('col'), may hold values from 0.099609375 to 1.8984375
- inner_bias: bfloat16 [2730], P('col'), may hold values from -1.75 to 1.75
- down_weight: bfloat16 [2730, 1024], P('col', 'row'), may hold values from -0.109375 to 0.109375
- down_bias: bfloat16 [1024], P('row'), may hold values from -1.75 to 1.75
- cotangent: bfloat16 [16400, 1024], P('row', 'col'), may hold values from -6 to 6
Outputs:
- layer_out: bfloat16 [16400, 1024], P('row', 'col')
- input_grad: bfloat16 [16400, 1024], P('row', 'col')
- norm1_gain_grad: float32 [1024], P('row')
- norm1_bias_grad: float32 [1024], P('row')
- qkv_weight_grad: float32 [1024, 3, 1024], P('row', None, 'col')
- query_bias_grad: float32 [1024], P('col')
- value_bias_grad: float32 [1024], P('col')
- proj_weight_grad: float32 [1024, 1024], P('col', 'row')
- proj_bias_grad: float32 [1024], P('row')
- norm2_gain_grad: float32 [1024], P('row')
- norm2_bias_grad: float32 [1024], P('row')
- gate_weight_grad: float32 [1024, 2730], P('row', 'col')
- gate_bias_grad: float32 [2730], P('col')
- up_weight_grad: float32 [1024, 2730], P('row', 'col')
- up_bias_grad: float32 [2730], P('col')
- inner_gain_grad: float32 [2730], P('col')
- inner_bias_grad: float32 [2730], P('col')
- down_weight_grad: float32 [2730, 1024], P('col', 'row')
- down_bias_grad: float32 [1024], P('row')
All inputs are finite; a program needn't handle non-finite values.
Results may differ from a plain program's by a relative error of at most 0.023.
Values may be sent and summed in bfloat16 or wider, within the bound.
A program may use at most 192 MiB of HBM per device.

v0:
```python
import functools
import math

import jax
import jax.numpy as jnp
from jax import lax
from jax.sharding import PartitionSpec as P


HD = 64
FF = 2730
GRID = 32
SEQ = 1025


EPSILON = 1e-06


def norm_forward(values, norm_gain, norm_shift):
    row_mean = jnp.mean(values, axis=-1, keepdims=True)
    centred = values - row_mean
    variance = jnp.mean(centred * centred, axis=-1, keepdims=True)
    inv_std = lax.rsqrt(variance + EPSILON)
    normed = centred * inv_std
    return (normed * norm_gain + norm_shift, normed, inv_std)


def norm_backward(upstream, normed, inv_std, norm_gain):
    scaled = upstream * norm_gain
    first_mean = jnp.mean(scaled, axis=-1, keepdims=True)
    second_mean = jnp.mean(scaled * normed, axis=-1, keepdims=True)
    delta = inv_std * (scaled - first_mean - normed * second_mean)
    return (delta, jnp.sum(upstream * normed, axis=0), jnp.sum(upstream, axis=0))


def rotary_tables(length, seq_len, grid_side, head_size):
    quarter = head_size // 4
    position = jnp.arange(length, dtype=jnp.int32) % seq_len
    patch_index = jnp.maximum(position - 1, 0)
    inside = (position > 0).astype(jnp.float32)
    row_pos = (patch_index // grid_side).astype(jnp.float32) * inside
    col_pos = (patch_index % grid_side).astype(jnp.float32) * inside
    frequency = jnp.exp(-math.log(10000.0) * jnp.arange(quarter, dtype=jnp.float32) / quarter)
    row_angle = row_pos[:, None] * frequency[None, :]
    col_angle = col_pos[:, None] * frequency[None, :]
    angles = jnp.concatenate([row_angle, row_angle, col_angle, col_angle], axis=1)
    return (jnp.cos(angles), jnp.sin(angles))


def rotate(values):
    pieces = jnp.split(values, 4, axis=-1)
    return jnp.concatenate([-pieces[1], pieces[0], -pieces[3], pieces[2]], axis=-1)


def rotate_transposed(values):
    pieces = jnp.split(values, 4, axis=-1)
    return jnp.concatenate([pieces[1], -pieces[0], pieces[3], -pieces[2]], axis=-1)


def apply_rotary(values, cosine_table, sine_table):
    return values * cosine_table[:, None, :] + rotate(values) * sine_table[:, None, :]


def rotary_back(grads, cosine_table, sine_table):
    return grads * cosine_table[:, None, :] + rotate_transposed(grads * sine_table[:, None, :])


def own_half(vector, column, half_width):
    return lax.dynamic_slice_in_dim(vector, column * half_width, half_width, axis=vector.ndim - 1)


def swap_columns(values):
    return lax.ppermute(values, "col", [(0, 1), (1, 0)])


def share_columns(partial_sums):
    half = partial_sums.shape[1] // 2
    column = lax.axis_index("col")
    own = lax.dynamic_slice_in_dim(partial_sums, column * half, half, axis=1)
    other = lax.dynamic_slice_in_dim(partial_sums, (1 - column) * half, half, axis=1)
    return own + swap_columns(other.astype(jnp.bfloat16)).astype(jnp.float32)


def join_columns(partial_sums):
    narrow = partial_sums.astype(jnp.bfloat16)
    return narrow.astype(jnp.float32) + swap_columns(narrow).astype(jnp.float32)


def gather_columns(values):
    other = swap_columns(values)
    first = lax.axis_index("col") == 0
    return jnp.concatenate(
        [jnp.where(first, values, other), jnp.where(first, other, values)], axis=1
    )


def hidden_totals(row_sums):
    return tuple(part + swap_columns(part) for part in row_sums)


def lane_round(width):
    return -(-width // 128) * 128


def pack(pieces):
    offsets = []
    padded = []
    position = 0
    for piece in pieces:
        width = lane_round(piece.shape[1])
        offsets.append(position)
        padded.append(jnp.pad(piece, ((0, 0), (0, width - piece.shape[1]))))
        position += width
    return jnp.concatenate(padded, axis=1), offsets


def spread(vector, rows_local, row_count):
    cols = -(-vector.shape[0] // rows_local)
    block = jnp.pad(vector, (0, rows_local * cols - vector.shape[0])).reshape(rows_local, cols)
    return jnp.tile(block, (row_count, 1))


def body(
    row_count,
    tokens,
    norm1_gain,
    norm1_bias,
    qkv_weight,
    query_bias,
    value_bias,
    proj_weight,
    proj_bias,
    norm2_gain,
    norm2_bias,
    gate_weight,
    gate_bias,
    up_weight,
    up_bias,
    inner_gain,
    inner_bias,
    down_weight,
    down_bias,
    cotangent,
):
    single = jnp.float32
    narrow = jnp.bfloat16
    local_rows = tokens.shape[0]
    half_width = tokens.shape[1]
    rows_local = norm1_gain.shape[0]
    model_width = rows_local * row_count
    ff_local = gate_weight.shape[1]
    head_local = half_width // HD
    images_local = local_rows // SEQ
    column = lax.axis_index("col")
    scaling = 1.0 / math.sqrt(HD)
    cosine_table, sine_table = rotary_tables(local_rows, SEQ, GRID, HD)

    def by_head(array):
        shaped = array.reshape(images_local, SEQ, head_local, HD).transpose(0, 2, 1, 3)
        return shaped.reshape(images_local * head_local, SEQ, HD)

    def from_head(array):
        shaped = array.reshape(images_local, head_local, SEQ, HD).transpose(0, 2, 1, 3)
        return shaped.reshape(local_rows, half_width)

    attn_pack, attn_at = pack(
        [
            qkv_weight.reshape(rows_local, 3 * half_width),
            proj_weight.T,
            jnp.stack([norm1_gain, norm1_bias, proj_bias], axis=1),
        ]
    )
    attn_full = lax.all_gather(attn_pack, "row", axis=0, tiled=True)
    qkv_full = attn_full[:, attn_at[0] : attn_at[0] + 3 * half_width].reshape(
        model_width, 3, half_width
    )
    proj_t = attn_full[:, attn_at[1] : attn_at[1] + half_width]
    attn_vectors = attn_full[:, attn_at[2] : attn_at[2] + 3].astype(single)

    whole_input = gather_columns(tokens).astype(single)
    normed_out, normed_one, inv_std_one = norm_forward(
        whole_input, attn_vectors[:, 0], attn_vectors[:, 1]
    )
    first_input = normed_out.astype(narrow)
    qkv_bias = jnp.stack(
        [query_bias.astype(single), jnp.zeros((half_width,), single), value_bias.astype(single)]
    )
    projected = (
        jnp.einsum("td,dpe->tpe", first_input, qkv_full, preferred_element_type=single) + qkv_bias
    )
    queries = apply_rotary(
        projected[:, 0].reshape(local_rows, head_local, HD), cosine_table, sine_table
    ).astype(narrow)
    keys_all = apply_rotary(
        projected[:, 1].reshape(local_rows, head_local, HD), cosine_table, sine_table
    ).astype(narrow)
    values_all = projected[:, 2].astype(narrow)

    def attend(operands):
        query_block, key_block, value_block = operands
        scores = (
            jnp.einsum("qd,kd->qk", query_block, key_block, preferred_element_type=single) * scaling
        )
        weights = jax.nn.softmax(scores, axis=-1)
        mixed = jnp.einsum(
            "qk,kd->qd", weights.astype(narrow), value_block, preferred_element_type=single
        )
        return mixed.astype(narrow)

    attended = from_head(
        lax.map(attend, (by_head(queries), by_head(keys_all), by_head(values_all)))
    )
    attn_partial = jnp.einsum("te,de->td", attended, proj_t, preferred_element_type=single)
    residual_half = (
        tokens.astype(single)
        + share_columns(attn_partial)
        + own_half(attn_vectors[:, 2], column, half_width)
    )
    residual_full = gather_columns(residual_half.astype(jnp.bfloat16)).astype(residual_half.dtype)

    ffn_pack, ffn_at = pack(
        [
            gate_weight,
            up_weight,
            down_weight.T,
            jnp.stack([norm2_gain, norm2_bias, down_bias], axis=1),
        ]
    )
    ffn_full = lax.all_gather(ffn_pack, "row", axis=0, tiled=True)
    gate_full = ffn_full[:, ffn_at[0] : ffn_at[0] + ff_local]
    up_full = ffn_full[:, ffn_at[1] : ffn_at[1] + ff_local]
    down_t = ffn_full[:, ffn_at[2] : ffn_at[2] + ff_local]
    ffn_vectors = ffn_full[:, ffn_at[3] : ffn_at[3] + 3].astype(single)

    second_out, normed_two, inv_std_two = norm_forward(
        residual_full, ffn_vectors[:, 0], ffn_vectors[:, 1]
    )
    second_input = second_out.astype(narrow)
    gate_value = jnp.dot(second_input, gate_full, preferred_element_type=single) + gate_bias.astype(
        single
    )
    up_value = jnp.dot(second_input, up_full, preferred_element_type=single) + up_bias.astype(
        single
    )
    sigmoid_gate = jax.nn.sigmoid(gate_value)
    hidden = gate_value * sigmoid_gate * up_value
    hidden_mean = hidden_totals((jnp.sum(hidden, axis=1),))[0][:, None] / FF
    hidden_centred = hidden - hidden_mean
    hidden_var = hidden_totals((jnp.sum(hidden_centred * hidden_centred, axis=1),))[0][:, None] / FF
    hidden_inv = lax.rsqrt(hidden_var + EPSILON)
    hidden_normed = hidden_centred * hidden_inv
    down_input = (hidden_normed * inner_gain.astype(single) + inner_bias.astype(single)).astype(
        narrow
    )
    ffn_partial = jnp.einsum("tf,df->td", down_input, down_t, preferred_element_type=single)
    layer_out = (
        residual_half
        + share_columns(ffn_partial)
        + own_half(ffn_vectors[:, 2], column, half_width)
    ).astype(narrow)
    out_full = gather_columns(cotangent)
    out_float = out_full.astype(single)
    down_weight_grad_t = jnp.einsum(
        "td,tf->df", out_full, down_input, preferred_element_type=single
    )
    down_bias_grad = jnp.sum(out_float, axis=0)
    normed_grad = jnp.einsum("td,df->tf", out_full, down_t, preferred_element_type=single)
    scaled_grad = normed_grad * inner_gain.astype(single)
    first_total, second_total = hidden_totals(
        (jnp.sum(scaled_grad, axis=1), jnp.sum(scaled_grad * hidden_normed, axis=1))
    )
    hidden_grad = hidden_inv * (
        scaled_grad - first_total[:, None] / FF - hidden_normed * (second_total[:, None] / FF)
    )
    inner_gain_grad = jnp.sum(normed_grad * hidden_normed, axis=0)
    inner_bias_grad = jnp.sum(normed_grad, axis=0)
    gate_grad = (
        hidden_grad * up_value * sigmoid_gate * (1.0 + gate_value * (1.0 - sigmoid_gate))
    ).astype(narrow)
    up_grad = (hidden_grad * gate_value * sigmoid_gate).astype(narrow)
    gate_bias_grad = jnp.sum(gate_grad.astype(single), axis=0)
    up_bias_grad = jnp.sum(up_grad.astype(single), axis=0)
    gate_weight_grad = jnp.einsum(
        "td,tf->df", second_input, gate_grad, preferred_element_type=single
    )
    up_weight_grad = jnp.einsum("td,tf->df", second_input, up_grad, preferred_element_type=single)
    second_back = join_columns(
        jnp.einsum("tf,df->td", gate_grad, gate_full, preferred_element_type=single)
        + jnp.einsum("tf,df->td", up_grad, up_full, preferred_element_type=single)
    )
    second_delta, gain_two_grad, shift_two_grad = norm_backward(
        second_back, normed_two, inv_std_two, ffn_vectors[:, 0]
    )
    residual_grad = out_float + second_delta
    attn_grad = residual_grad.astype(narrow)
    proj_bias_grad = jnp.sum(attn_grad.astype(single), axis=0)
    proj_weight_grad_t = jnp.einsum(
        "td,te->de", attn_grad, attended, preferred_element_type=single
    )
    mid_small = jnp.concatenate([gate_bias_grad, up_bias_grad, inner_gain_grad, inner_bias_grad])
    mid_pack, mid_at = pack(
        [
            gate_weight_grad.astype(narrow),
            up_weight_grad.astype(narrow),
            down_weight_grad_t.astype(narrow),
            proj_weight_grad_t.astype(narrow),
            jnp.stack(
                [gain_two_grad, shift_two_grad, down_bias_grad, proj_bias_grad], axis=1
            ).astype(narrow),
            spread(mid_small, rows_local, row_count).astype(narrow),
        ]
    )
    mid_pack, attn_grad_held = lax.optimization_barrier((mid_pack, attn_grad))
    mid_sums = lax.psum_scatter(mid_pack, "row", scatter_dimension=0, tiled=True).astype(single)
    attended_grad = jnp.einsum(
        "td,de->te", attn_grad_held, proj_t, preferred_element_type=single
    ).astype(narrow)

    def attend_back(operands):
        query_block, key_block, value_block, grad_block = operands
        scores = (
            jnp.einsum("qd,kd->qk", query_block, key_block, preferred_element_type=single) * scaling
        )
        weights = jax.nn.softmax(scores, axis=-1)
        value_grad = jnp.einsum(
            "qk,qd->kd", weights.astype(narrow), grad_block, preferred_element_type=single
        )
        weight_grad = jnp.einsum(
            "qd,kd->qk", grad_block, value_block, preferred_element_type=single
        )
        score_grad = (
            weights * (weight_grad - jnp.sum(weight_grad * weights, axis=-1, keepdims=True))
        ).astype(narrow)
        query_grad = (
            jnp.einsum("qk,kd->qd", score_grad, key_block, preferred_element_type=single) * scaling
        )
        key_grad = (
            jnp.einsum("qk,qd->kd", score_grad, query_block, preferred_element_type=single)
            * scaling
        )
        return (query_grad, key_grad, value_grad)

    query_grads, key_grads, value_grads = lax.map(
        attend_back,
        (by_head(queries), by_head(keys_all), by_head(values_all), by_head(attended_grad)),
    )
    query_pre = rotary_back(
        from_head(query_grads).reshape(local_rows, head_local, HD), cosine_table, sine_table
    )
    key_pre = rotary_back(
        from_head(key_grads).reshape(local_rows, head_local, HD), cosine_table, sine_table
    )
    qkv_grad = jnp.stack(
        [
            query_pre.reshape(local_rows, half_width),
            key_pre.reshape(local_rows, half_width),
            from_head(value_grads),
        ],
        axis=1,
    ).astype(narrow)
    qkv_grad_float = qkv_grad.astype(single)
    query_bias_grad = jnp.sum(qkv_grad_float[:, 0], axis=0)
    value_bias_grad = jnp.sum(qkv_grad_float[:, 2], axis=0)
    qkv_weight_grad = jnp.einsum(
        "td,tpe->dpe", first_input, qkv_grad, preferred_element_type=single
    )
    first_back = join_columns(
        jnp.einsum("tpe,dpe->td", qkv_grad, qkv_full, preferred_element_type=single)
    )
    first_delta, gain_one_grad, shift_one_grad = norm_backward(
        first_back, normed_one, inv_std_one, attn_vectors[:, 0]
    )
    input_grad = own_half(residual_grad + first_delta, column, half_width).astype(narrow)
    end_pack, end_at = pack(
        [
            qkv_weight_grad.reshape(model_width, 3 * half_width).astype(narrow),
            jnp.stack([gain_one_grad, shift_one_grad], axis=1).astype(narrow),
            spread(
                jnp.concatenate([query_bias_grad, value_bias_grad]), rows_local, row_count
            ).astype(narrow),
        ]
    )
    end_pack, mid_sums = lax.optimization_barrier((end_pack, mid_sums))
    end_sums = lax.psum_scatter(end_pack, "row", scatter_dimension=0, tiled=True).astype(single)

    def cut(sums, offset, width):
        return sums[:, offset : offset + width]

    mid_vectors = cut(mid_sums, mid_at[4], 4)
    mid_small_sum = cut(mid_sums, mid_at[5], -(-mid_small.shape[0] // rows_local)).reshape(-1)
    end_vectors = cut(end_sums, end_at[1], 2)
    end_small_sum = cut(end_sums, end_at[2], -(-2 * half_width // rows_local)).reshape(-1)
    return (
        layer_out,
        input_grad,
        end_vectors[:, 0],
        end_vectors[:, 1],
        cut(end_sums, end_at[0], 3 * half_width).reshape(rows_local, 3, half_width),
        end_small_sum[:half_width],
        end_small_sum[half_width : 2 * half_width],
        cut(mid_sums, mid_at[3], half_width).T,
        mid_vectors[:, 3],
        mid_vectors[:, 0],
        mid_vectors[:, 1],
        cut(mid_sums, mid_at[0], ff_local),
        mid_small_sum[:ff_local],
        cut(mid_sums, mid_at[1], ff_local),
        mid_small_sum[ff_local : 2 * ff_local],
        mid_small_sum[2 * ff_local : 3 * ff_local],
        mid_small_sum[3 * ff_local : 4 * ff_local],
        cut(mid_sums, mid_at[2], ff_local).T,
        mid_vectors[:, 2],
    )


def solution(mesh):
    placed = (
        P("row", "col"),
        P("row"),
        P("row"),
        P("row", None, "col"),
        P("col"),
        P("col"),
        P("col", "row"),
        P("row"),
        P("row"),
        P("row"),
        P("row", "col"),
        P("col"),
        P("row", "col"),
        P("col"),
        P("col"),
        P("col"),
        P("col", "row"),
        P("row"),
        P("row", "col"),
    )
    return jax.shard_map(
        functools.partial(body, mesh.shape["row"]),
        mesh=mesh,
        in_specs=placed,
        out_specs=(
            P("row", "col"),
            P("row", "col"),
            P("row"),
            P("row"),
            P("row", None, "col"),
            P("col"),
            P("col"),
            P("col", "row"),
            P("row"),
            P("row"),
            P("row"),
            P("row", "col"),
            P("col"),
            P("row", "col"),
            P("col"),
            P("col"),
            P("col"),
            P("col", "row"),
            P("row"),
        ),
        check_vma=False,
    )
```

profile of v0, /device:TPU:0, one launch (start us, length us, event | category | flops | bytes accessed | tf_op | source)
XLA Modules:
  0.0 608.7 jit_solution(8131681661385271592)
XLA Ops:
  18.9 72.9 %all-gather.3.cloned.1.call-done = bf16[1024,2176]{1,0:T(8,128)(2,1)} async-done(((bf16[64,2176]{1,0:T(8,128)(2,1)}), bf16[1024,2176]{1,0:T(8,128)(2,1)}) %all-gather.3.cloned.1.call-update) | async-done | bytes 4456464 | tf_op jit(solution)/shard_map/all_gather | solution.py:173
  93.9 3.7 slice.169
  97.6 4.6 copy.177
  102.3 6.1 convolution_add_fusion.2
  113.9 3.0 copy.179
  121.3 3.0 copy.184
  124.3 3.7 copy.185
  130.3 3.7 copy.186
  134.0 42.0 %while.24 = (s32[]{:T(128)}, bf16[8,1025,64]{1,2,0:T(8,128)(2,1)}, bf16[8,1025,64]{2,1,0:T(8,128)(2,1)S(1)}, bf16[8,1025,64]{2,1,0:T(8,128)(2,1)}, bf16[8,1025,64]{2,1,0:T(8,128)(2,1)}, /*index=5*/s32[]{:T(128)}) while((s32[]{:T(128)}, bf16[8,1025,64]{1,2,0:T(8,128)(2,1)}, bf16[8,1025,64]{2,1,0:T(8,128)(2,1)S(1)}, ...), condition=%wide.region_5.6_spmd, body=%wide.region_2.5_spmd.sunk | while | flops 276377920 | bytes 13570157 | solution.py:211
  141.8 2.6 fusion.193
  146.9 2.6 fusion.193
  152.1 2.6 fusion.193
  157.3 2.7 fusion.193
  162.5 2.6 fusion.193
  172.9 2.6 fusion.193
  176.0 3.8 fusion.104
  191.7 19.0 %all-gather.5.cloned.1.call-done = bf16[1024,4352]{1,0:T(8,128)(2,1)} async-done(((bf16[64,4352]{1,0:T(8,128)(2,1)}), bf16[1024,4352]{1,0:T(8,128)(2,1)}) %all-gather.5.cloned.1.call-update) | async-done | bytes 8912912 | tf_op jit(solution)/shard_map/all_gather | solution.py:229
  212.8 5.8 convolution_add_fusion.1
  218.6 11.8 %fusion.155 = (f32[1025]{0:T(1024)S(1)}, f32[1025,1365]{1,0:T(8,128)}, f32[1025,1365]{1,0:T(8,128)}) fusion(f32[1025,1365]{1,0:T(8,128)S(1)} %convolution_add_fusion.1, f32[1365]{0:T(1024)S(1)} %convert_element_type.244, bf16[1024,4352]{1,0:T(8,128)(2,1)} %all-gather.5.cloned.1.call-done, f32[1024]{0:T(1024)S(1)} %get-tuple-element.268, ...), kind=kOutput, calls=%fused_computation.277 | convolution fusion | flops 2884646912 | bytes 21798236 | tf_op jit(solution)/shard_map/dot_general | solution.py:242
  232.1 3.2 copy.195
  235.3 3.4 multiply_reduce_fusion.3
  241.2 8.3 %multiply_reduce_fusion.1 = (bf16[1365]{0:T(1024)(128)(2,1)S(1)}, f32[1025]{0:T(1024)S(1)}, f32[1025]{0:T(1024)S(1)}, bf16[1365]{0:T(1024)(128)(2,1)S(1)}, f32[1025,1365]{1,0:T(8,128)S(1)}) fusion(f32[1025,1365]{1,0:T(8,128)} %get-tuple-element.306, f32[1025]{0:T(1024)S(1)} %add_rsqrt_fusion, f32[1025]{0:T(1024)S(1)} %add_multiply_fusion.2, ...), kind=kOutput, calls=%fused_computation.60 | convolution fusion | flops 2882193152 | bytes 16418828 | tf_op jit(solution)/shard_map/td,df->tf/dot_general | solution.py:267
  250.1 6.0 convolution_convert_fusion
  256.2 7.0 %fusion.151 = (bf16[1365]{0:T(1024)(128)(2,1)S(1)}, bf16[1025,1365]{1,0:T(8,128)(2,1)S(1)}, bf16[1365]{0:T(1024)(128)(2,1)S(1)}, bf16[1025,1365]{1,0:T(8,128)(2,1)S(1)}) fusion(f32[1025,1365]{1,0:T(8,128)S(1)} %bitcast.224, f32[1025]{0:T(1024)S(1)} %add_multiply_fusion, f32[1025,1365]{1,0:T(8,128)S(1)} %bitcast.211, f32[1025]{0:T(1024)S(1)} %add_multiply_fusion.2, ...), kind=kLoop, calls=%fused_computation.274 | loop fusion | flops 30778012 | bytes 28009820 | tf_op jit(solution)/shard_map/reduce_sum | solution.py:282
  263.2 7.4 %fusion.83 = f32[1025,1024]{1,0:T(8,128)S(1)} fusion(bf16[1025,1365]{1,0:T(8,128)(2,1)S(1)} %get-tuple-element.314, bf16[1024,4352]{1,0:T(8,128)(2,1)} %all-gather.5.cloned.1.call-done), kind=kOutput, calls=%fused_computation.123 | convolution fusion | flops 2865408000 | bytes 9880234 | tf_op jit(solution)/shard_map/tf,df->td/dot_general | solution.py:288
  270.7 6.7 %fusion.69 = bf16[1025,1024]{1,0:T(8,128)(2,1)} fusion(f32[1025,1024]{1,0:T(8,128)S(1)} %fusion.83, bf16[1025,1365]{1,0:T(8,128)(2,1)S(1)} %get-tuple-element.299, bf16[1024,4352]{1,0:T(8,128)(2,1)} %all-gather.5.cloned.1.call-done), kind=kOutput, calls=%fused_computation.101 | convolution fusion | flops 2867507200 | bytes 11979434 | tf_op jit(solution)/shard_map/tf,df->td/dot_general | solution.py:289
  277.4 6.1 %convolution_convert_fusion.2 = bf16[1024,1365]{0,1:T(8,128)(2,1)} fusion(bf16[1025,1365]{1,0:T(8,128)(2,1)S(1)} %copy-done.24, f32[1024]{0:T(1024)S(1)} %get-tuple-element.268, f32[1024]{0:T(1024)S(1)} %get-tuple-element.267, f32[1025]{0:T(1024)S(1)} %add_rsqrt_fusion.1, f32[1025]{0:T(1024)S(1)} %broadcast_multiply_fusion.6, ...), kind=kOutput, calls=%fused_computation.104 | convolution fusion | flops 2876252160 | bytes 7709362 | tf_op jit(solution)/shard_map/td,tf->df/dot_general | solution.py:283
  284.7 3.8 pad_dynamic-update-slice_fusion.2
  288.5 4.9 convolution_convert_fusion.1
  298.2 5.2 fusion.65
  303.5 6.2 %fusion.153 = (bf16[1024]{0:T(1024)(128)(2,1)S(1)}, bf16[1025,1024]{1,0:T(8,128)(2,1)S(1)}, f32[1025,1024]{1,0:T(8,128)}, bf16[1024]{0:T(1024)(128)(2,1)S(1)}) fusion(f32[1025]{0:T(1024)S(1)} %broadcast_multiply_fusion.4, f32[1025]{0:T(1024)S(1)} %broadcast_multiply_fusion.6, bf16[1025,512]{1,0:T(8,128)(2,1)S(1)} %get-tuple-element.347, ...), kind=kLoop, calls=%fused_computation.276 | loop fusion | flops 24138752 | bytes 14718992 | tf_op jit(solution)/shard_map/reduce_sum | solution.py:296
  317.6 13.3 %copy.212 = bf16[1024,4992]{1,0:T(8,128)(2,1)} copy(bf16[1024,4992]{0,1:T(8,128)(2,1)} %pad_dynamic-update-slice_fusion.3) | data formatting | bytes 20447232
  332.6 100.8 %while.25 = (s32[]{:T(128)}, f32[8,1025,64]{1,2,0:T(8,128)S(1)}, f32[8,1025,64]{1,2,0:T(8,128)}, bf16[8,1025,64]{1,2,0:T(8,128)(2,1)}, bf16[8,1025,64]{2,1,0:T(8...) while((s32[]{:T(128)}, f32[8,1025,64]{1,2,0:T(8,128)S(1)}, ...), condition=%wide.region_26.27_spmd, body=%wide.region_22.26_spmd.sunk | while | flops 689338112 | bytes 38548656 | solution.py:343
  433.4 3.1 copy.200
  436.5 3.4 bitcast_multiply_fusion.1
  442.1 3.9 copy.194
  448.2 3.1 copy.197
  451.4 5.0 add_convert_fusion.3
  456.4 4.9 fusion.68
  463.9 7.8 %convolution_convert_fusion.4 = bf16[1024,3,512]{0,2,1:T(8,128)(2,1)} fusion(f32[1024]{0:T(1024)S(1)} %copy-done.49, f32[1024]{0:T(1024)S(1)} %copy-done.45, bf16[1025,1,512]{2,0,1:T(8,128)(2,1)} %copy.200, bf16[1025,1,512]{2,0,1:T(8,128)(2,1)} %copy-done.16, bf16[1025,1,512]{2,0,1:T(8,128)(2,1)S(1)} %get-tuple-element.341, f32[1025]{0:T(1024)S(1)} %copy-done.37, ...), kind=kOutput, calls=%fused_computation.136 | convolution fusion | flops 3244836864 | bytes 8410120 | tf_op jit(solution)/shard_map/td,tpe->dpe/dot_general | solution.py:364
  471.7 4.7 copy.202
  476.4 6.8 %fusion.149 = (f32[1025]{0:T(1024)S(1)}, f32[1025]{0:T(1024)S(1)}, bf16[1024]{0:T(1024)(128)(2,1)S(1)}, bf16[1024]{0:T(1024)(128)(2,1)S(1)}, f32[1025,1024]{1,0:T(8,128)}, /*index=5*/f32[1025,1024]{1,0:T(8,128)}) fusion(f32[1025]{0:T(1024)S(1)} %copy-done.37, f32[1025]{0:T(1024)S(1)} %copy-done.35, bf16[1025,512]{1,0:T(8,128)(2,1)S(1)} %copy-done.5, ...), kind=kLoop, calls=%fused_computation.273 | loop fusion | flops 16789502 | bytes 14718992 | tf_op jit(solution)/shard_map/reduce_sum | solution.py:30
  483.5 3.3 fusion.75
  486.8 20.7 %reduce-scatter.7.cloned.1.call-done = bf16[64,4992]{1,0:T(8,128)(2,1)} async-done(((bf16[1024,4992]{1,0:T(8,128)(2,1)}), bf16[64,4992]{1,0:T(8,128)(2,1)}) %reduce-scatter.7.cloned.1.call-update) | async-done | bytes 638992
  511.4 7.0 %fusion.79 = f32[1025,1024]{1,0:T(8,128)S(1)} fusion(bf16[1024,4352]{1,0:T(8,128)(2,1)} %all-gather.5.cloned.1.call-done, f32[1025,1365]{1,0:T(8,128)} %get-tuple-element.306, f32[1365]{0:T(1024)S(1)} %copy-done.47, f32[1365]{0:T(1024)S(1)} %copy-done.41, f32[1025]{0:T(1024)S(1)} %copy-done.39, f32[1025]{0:T(1024)S(1)} %copy-done.33), kind=kOutput, calls=%fused_computation.119 | convolution fusion | flops 2872403712 | bytes 12913328 | tf_op jit(solution)/shard_map/tf,df->td/dot_general | solution.py:255
  521.4 3.5 add_convert_fusion.4
  524.9 3.8 fusion.91
  537.3 58.9 %reduce-scatter.5.cloned.1.call-done = bf16[64,1792]{1,0:T(8,128)(2,1)} async-done(((bf16[1024,1792]{1,0:T(8,128)(2,1)}), bf16[64,1792]{1,0:T(8,128)(2,1)}) %reduce-scatter.5.cloned.1.call-update) | async-done | bytes 229392 | tf_op jit(solution)/shard_map/reduce_scatter | solution.py:384
  (348 shorter events, 214.5 us)
Async XLA Ops:
  7.2 9.1 %copy-start.6 = (bf16[1025,512]{1,0:T(8,128)(2,1)S(1)}, bf16[1025,512]{1,0:T(8,128)(2,1)}, u32[]{:S(2)}) copy-start(bf16[1025,512]{1,0:T(8,128)(2,1)} %param.23) | copy-start | bytes 3148804
  7.2 7.0 %copy-start.54 = (bf16[512]{0:T(512)(128)(2,1)S(1)}, bf16[512]{0:T(512)(128)(2,1)}, u32[]{:S(2)}) copy-start(bf16[512]{0:T(512)(128)(2,1)} %param.28) | copy-start | bytes 3076
  7.2 7.0 %copy-start.55 = (bf16[512]{0:T(512)(128)(2,1)S(1)}, bf16[512]{0:T(512)(128)(2,1)}, u32[]{:S(2)}) copy-start(bf16[512]{0:T(512)(128)(2,1)} %param.27) | copy-start | bytes 3076
  7.2 84.5 %all-gather.3.cloned.1.call-start = ((), (), s32[]{:S(2)}) async-start(), calls=%async_computation.2 | async-start | bytes 4734976 | tf_op jit(solution)/shard_map/all_gather | solution.py:173
  10.7 199.9 %all-gather.5.cloned.1.call-start = ((), (), s32[]{:S(2)}) async-start(), calls=%async_computation.3 | async-start | bytes 9469952 | tf_op jit(solution)/shard_map/all_gather | solution.py:229
  10.7 5.6 collective-permute-start
  14.1 493.4 %reduce-scatter.7.cloned.1.call-start = ((), (), s32[]{:S(2)}) async-start(), calls=%async_computation.5 | async-start | bytes 10862592
  17.7 84.5 %copy-start.2 = (bf16[1025,512]{1,0:T(8,128)(2,1)}, bf16[1025,512]{1,0:T(8,128)(2,1)S(1)}, u32[]{:S(2)}) copy-start(bf16[1025,512]{1,0:T(8,128)(2,1)S(1)} %get-tuple-element.348) | copy-start | bytes 3148804
  17.7 84.5 %copy-start.4 = (bf16[1025,512]{1,0:T(8,128)(2,1)}, bf16[1025,512]{1,0:T(8,128)(2,1)S(1)}, u32[]{:S(2)}) copy-start(bf16[1025,512]{1,0:T(8,128)(2,1)S(1)} %get-tuple-element.349) | copy-start | bytes 3148804
  18.1 84.1 %copy-start.34 = (f32[1025]{0:T(1024)}, f32[1025]{0:T(1024)S(1)}, u32[]{:S(2)}) copy-start(f32[1025]{0:T(1024)S(1)} %broadcast_multiply_fusion.7) | copy-start | bytes 12304
  18.9 83.4 %copy-start.36 = (f32[1025]{0:T(1024)}, f32[1025]{0:T(1024)S(1)}, u32[]{:S(2)}) copy-start(f32[1025]{0:T(1024)S(1)} %add_rsqrt_fusion.2) | copy-start | bytes 12304
  93.9 8.4 %copy-start.44 = (f32[1024]{0:T(1024)}, f32[1024]{0:T(1024)S(1)}, u32[]{:S(2)}) copy-start(f32[1024]{0:T(1024)S(1)} %get-tuple-element.265) | copy-start | bytes 12292
  93.9 8.4 %copy-start.48 = (f32[1024]{0:T(1024)}, f32[1024]{0:T(1024)S(1)}, u32[]{:S(2)}) copy-start(f32[1024]{0:T(1024)S(1)} %get-tuple-element.266) | copy-start | bytes 12292
  182.2 2.9 collective-permute-start.1
  187.5 2.7 collective-permute-start.2
  187.7 51.6 %collective-permute-start.6 = (bf16[1025,512]{1,0:T(8,128)(2,1)}, bf16[1025,512]{1,0:T(8,128)(2,1)}, u32[]{:S(2)}, u32[]{:S(2)}) collective-permute-start(bf16[1025,512]{1,0:T(8,128)(2,1)} %param.41), channel_id=1, source_target_pairs={{0,1},{1,0},{2,3},{3,2},{4,5},{5,4},{6,7},{7,6},{8,9},{9,8},{10,11... | collective-permute-start | bytes 3148808 | tf_op jit(solution)/shard_map/ppermute | solution.py:73
  218.6 11.9 %copy-start.13 = (f32[1025,1365]{1,0:T(8,128)}, f32[1025,1365]{1,0:T(8,128)S(1)}, u32[]{:S(2)}) copy-start(f32[1025,1365]{1,0:T(8,128)S(1)} %convolution_add_fusion.1) | copy-start | bytes 16789504
  218.6 11.9 %copy-start.52 = (bf16[1365]{0:T(1024)(128)(2,1)S(1)}, bf16[1365]{0:T(1024)(128)(2,1)}, u32[]{:S(2)}) copy-start(bf16[1365]{0:T(1024)(128)(2,1)} %param.38) | copy-start | bytes 8194
  218.6 11.9 %copy-start.53 = (bf16[1365]{0:T(1024)(128)(2,1)S(1)}, bf16[1365]{0:T(1024)(128)(2,1)}, u32[]{:S(2)}) copy-start(bf16[1365]{0:T(1024)(128)(2,1)} %param.37) | copy-start | bytes 8194
  218.6 11.9 %copy-start.29 = (f32[1025,64]{0,1:T(8,128)S(1)}, f32[1025,64]{0,1:T(8,128)}, u32[]{:S(2)}) copy-start(f32[1025,64]{0,1:T(8,128)} %get-tuple-element.358) | copy-start | bytes 787204
  230.5 4.8 collective-permute-start.3
  230.5 19.6 %copy-start.46 = (f32[1365]{0:T(1024)}, f32[1365]{0:T(1024)S(1)}, u32[]{:S(2)}) copy-start(f32[1365]{0:T(1024)S(1)} %convert_element_type.246) | copy-start | bytes 16384
  230.6 25.6 %copy-start.40 = (f32[1365]{0:T(1024)}, f32[1365]{0:T(1024)S(1)}, u32[]{:S(2)}) copy-start(f32[1365]{0:T(1024)S(1)} %convert_element_type.245) | copy-start | bytes 16384
  235.3 20.8 %copy-start.32 = (f32[1025]{0:T(1024)}, f32[1025]{0:T(1024)S(1)}, u32[]{:S(2)}) copy-start(f32[1025]{0:T(1024)S(1)} %add_multiply_fusion.2) | copy-start | bytes 12304
  238.7 2.4 collective-permute-start.4
  239.3 10.8 %slice-start = ((s8[5812224]{0:T(1024)(128)(4,1)}), s8[4194304]{0:T(1024)(128)(4,1)S(1)}, s32[]{:S(2)}) async-start(s8[5812224]{0:T(1024)(128)(4,1)} %bitcast.210), calls=%async_computation.6 | async-start | bytes 8388608
  241.1 9.0 %copy-start.17 = (bf16[1025,512]{1,0:T(8,128)(2,1)}, bf16[1025,512]{1,0:T(8,128)(2,1)S(1)}, u32[]{:S(2)}) copy-start(bf16[1025,512]{1,0:T(8,128)(2,1)S(1)} %get-tuple-element.345) | copy-start | bytes 3148804
  241.2 15.0 %copy-start.38 = (f32[1025]{0:T(1024)}, f32[1025]{0:T(1024)S(1)}, u32[]{:S(2)}) copy-start(f32[1025]{0:T(1024)S(1)} %add_rsqrt_fusion) | copy-start | bytes 12304
  241.2 9.0 %slice-start.1 = ((s8[5812224]{0:T(1024)(128)(4,1)}), s8[1617920]{0:T(1024)(128)(4,1)S(1)}, s32[]{:S(2)}) async-start(s8[5812224]{0:T(1024)(128)(4,1)} %bitcast.210), calls=%async_computation.7 | async-start | bytes 3235840
  249.5 6.7 %collective-permute-start.8 = (f32[1025]{0:T(1024)S(1)}, f32[1025]{0:T(1024)S(1)}, u32[]{:S(2)}, u32[]{:S(2)}) collective-permute-start(f32[1025]{0:T(1024)S(1)} %get-tuple-element.250), channel_id=1, source_target_pairs={{0,1},{1,0},{2,3},{3,2},{4,5},{5,4},{6,7},{7,6},{8,9},{9,8},{10,11... | collective-permute-start | bytes 12308 | tf_op jit(solution)/shard_map/ppermute | solution.py:73
  249.6 6.6 %slice-start.4 = ((s8[5812224]{0:T(1024)(128)(4,1)}), s8[4194304]{0:T(1024)(128)(4,1)S(1)}, s32[]{:S(2)}) async-start(s8[5812224]{0:T(1024)(128)(4,1)} %bitcast.223), calls=%async_computation.10 | async-start | bytes 8388608
  249.6 6.6 %slice-start.6 = ((s8[5812224]{0:T(1024)(128)(4,1)}), s8[4194304]{0:T(1024)(128)(4,1)S(1)}, s32[]{:S(2)}) async-start(s8[5812224]{0:T(1024)(128)(4,1)} %bitcast.225), calls=%async_computation.12 | async-start | bytes 8388608
  249.6 6.6 %slice-start.5 = ((s8[5812224]{0:T(1024)(128)(4,1)}), s8[1617920]{0:T(1024)(128)(4,1)S(1)}, s32[]{:S(2)}) async-start(s8[5812224]{0:T(1024)(128)(4,1)} %bitcast.223), calls=%async_computation.11 | async-start | bytes 3235840
  249.6 6.6 %slice-start.7 = ((s8[5812224]{0:T(1024)(128)(4,1)}), s8[1617920]{0:T(1024)(128)(4,1)S(1)}, s32[]{:S(2)}) async-start(s8[5812224]{0:T(1024)(128)(4,1)} %bitcast.225), calls=%async_computation.13 | async-start | bytes 3235840
  249.6 6.6 %collective-permute-start.7 = (f32[1025]{0:T(1024)S(1)}, f32[1025]{0:T(1024)S(1)}, u32[]{:S(2)}, u32[]{:S(2)}) collective-permute-start(f32[1025]{0:T(1024)S(1)} %get-tuple-element.255), channel_id=1, source_target_pairs={{0,1},{1,0},{2,3},{3,2},{4,5},{5,4},{6,7},{7,6},{8,9},{9,8},{10,11... | collective-permute-start | bytes 12308 | tf_op jit(solution)/shard_map/ppermute | solution.py:73
  263.2 7.4 %copy-start.23 = (bf16[1025,1365]{1,0:T(8,128)(2,1)}, bf16[1025,1365]{1,0:T(8,128)(2,1)S(1)}, u32[]{:S(2)}) copy-start(bf16[1025,1365]{1,0:T(8,128)(2,1)S(1)} %get-tuple-element.314) | copy-start | bytes 8394754
  263.2 7.4 %copy-start.21 = (bf16[1025,1365]{1,0:T(8,128)(2,1)}, bf16[1025,1365]{1,0:T(8,128)(2,1)S(1)}, u32[]{:S(2)}) copy-start(bf16[1025,1365]{1,0:T(8,128)(2,1)S(1)} %get-tuple-element.299) | copy-start | bytes 8394754
  270.6 6.8 %copy-start.24 = (bf16[1025,1365]{1,0:T(8,128)(2,1)S(1)}, bf16[1025,1365]{1,0:T(8,128)(2,1)}, u32[]{:S(2)}) copy-start(bf16[1025,1365]{1,0:T(8,128)(2,1)} %copy-done.23) | copy-start | bytes 8394754
  277.4 20.8 %collective-permute-start.9 = (bf16[1025,1024]{1,0:T(8,128)(2,1)}, bf16[1025,1024]{1,0:T(8,128)(2,1)}, u32[]{:S(2)}, u32[]{:S(2)}) collective-permute-start(bf16[1025,1024]{1,0:T(8,128)(2,1)} %fusion.69), channel_id=1, source_target_pairs={{0,1},{1,0},{2,3},{3,2},{4,5},{5,4},{6,7},{7,6},{8,9},{9,8},{10,11... | collective-permute-start | bytes 6297608 | tf_op jit(solution)/shard_map/ppermute | solution.py:73
  303.4 6.2 %copy-start.56 = (bf16[8,1025,64]{1,2,0:T(8,128)(2,1)S(1)}, bf16[8,1025,64]{1,2,0:T(8,128)(2,1)}, u32[]{:S(2)}) copy-start(bf16[8,1025,64]{1,2,0:T(8,128)(2,1)} %get-tuple-element.94) | copy-start | bytes 3148804
  331.0 265.3 %reduce-scatter.5.cloned.1.call-start = ((), (), s32[]{:S(2)}) async-start(), calls=%async_computation.4 | async-start | bytes 3899392 | tf_op jit(solution)/shard_map/reduce_scatter | solution.py:384
  332.6 103.9 %copy-start.27 = (f32[1025,64]{0,1:T(8,128)S(1)}, f32[1025,64]{0,1:T(8,128)}, u32[]{:S(2)}) copy-start(f32[1025,64]{0,1:T(8,128)} %get-tuple-element.359) | copy-start | bytes 787204
  433.4 6.5 %copy-start.9 = (f32[8,1025,64]{1,2,0:T(8,128)}, f32[8,1025,64]{1,2,0:T(8,128)S(1)}, u32[]{:S(2)}) copy-start(f32[8,1025,64]{1,2,0:T(8,128)S(1)} %get-tuple-element.96) | copy-start | bytes 6297604
  461.3 15.1 %collective-permute-start.10 = (bf16[1025,1024]{1,0:T(8,128)(2,1)}, bf16[1025,1024]{1,0:T(8,128)(2,1)}, u32[]{:S(2)}, u32[]{:S(2)}) collective-permute-start(bf16[1025,1024]{1,0:T(8,128)(2,1)} %fusion.68), channel_id=1, source_target_pairs={{0,1},{1,0},{2,3},{3,2},{4,5},{5,4},{6,7},{7,6},{8,9},{9,8},{10,11... | collective-permute-start | bytes 6297608 | tf_op jit(solution)/shard_map/ppermute | solution.py:73
  511.4 7.3 %copy-start.30 = (f32[1024,1]{1,0:T(8,128)S(1)}, f32[1024,1]{1,0:T(8,128)}, u32[]{:S(2)}) copy-start(f32[1024,1]{1,0:T(8,128)} %get-tuple-element.352) | copy-start | bytes 12292
  511.4 9.9 %copy-start.43 = (f32[512]{0:T(512)S(1)}, f32[512]{0:T(512)}, u32[]{:S(2)}) copy-start(f32[512]{0:T(512)} %copy-done.42) | copy-start | bytes 6148
  518.6 2.7 collective-permute-start.5
  518.7 6.2 %slice-start.2 = ((s8[4227072]{0:T(1024)(128)(4,1)}), s8[4194304]{0:T(1024)(128)(4,1)S(1)}, s32[]{:S(2)}) async-start(s8[4227072]{0:T(1024)(128)(4,1)} %bitcast.216), calls=%async_computation.8 | async-start | bytes 8388608
  (32 other events, 99.7 us)
Sparse Core Ops, SparseCore 0:
  11.4 80.3 all-gather.2
  95.0 115.5 all-gather.4
  331.1 176.3 reduce-scatter.6
  511.5 84.7 reduce-scatter.4
where the time goes:
time: 620 us; the launch traced here: 609 us
  matrix products  213 us (34%)
  waiting for transfers between devices  178 us (29%)
  local copies, waits for them, and re-layouts  104 us (17%)
  other arithmetic  94.2 us (15%)
  between operations  15.3 us (2%)
    all_gather x1, waiting for transfers between devices, body(): attn_full = lax.all_gather(attn_pack, 'row', axis=0, tiled=True)  72.9 us
    reduce_scatter x1, waiting for transfers between devices, body(): lax.psum_scatter(end_pack, 'row', scatter_dimension=0, tiled=True)  58.9 us
    unnamed x141, local copies, waits for them, and re-layouts  34.7 us
    dot_general x8, matrix products, attend(): jnp.einsum('qk,kd->qd', weights.astype(narrow), value_block, preferred_el...  20.9 us
    unnamed x5, waiting for transfers between devices  20.8 us
    dot_general x8, matrix products, attend_back(): jnp.einsum('qk,qd->kd', weights.astype(narrow), grad_block, preferred_ele...  20.3 us
    dot_general x8, matrix products, attend_back(): jnp.einsum('qk,qd->kd', score_grad, query_block, preferred_element_type=s...  20 us
    all_gather x1, waiting for transfers between devices, body(): ffn_full = lax.all_gather(ffn_pack, 'row', axis=0, tiled=True)  19 us
  transfers between devices with their start and end apart: 15, of which 7 were waited for; matrix products, arithmetic and copies ran while one was open for 55% of the time, Pallas kernels for 0%

commit v1 on v0

--- a/solution.py
+++ b/solution.py
@@ -284,36 +284,34 @@
         "td,tf->df", second_input, gate_grad, preferred_element_type=single
     )
     up_weight_grad = jnp.einsum("td,tf->df", second_input, up_grad, preferred_element_type=single)
-    second_back = join_columns(
-        jnp.einsum("tf,df->td", gate_grad, gate_full, preferred_element_type=single)
-        + jnp.einsum("tf,df->td", up_grad, up_full, preferred_element_type=single)
-    )
-    second_delta, gain_two_grad, shift_two_grad = norm_backward(
-        second_back, normed_two, inv_std_two, ffn_vectors[:, 0]
-    )
-    residual_grad = out_float + second_delta
-    attn_grad = residual_grad.astype(narrow)
-    proj_bias_grad = jnp.sum(attn_grad.astype(single), axis=0)
-    proj_weight_grad_t = jnp.einsum(
-        "td,te->de", attn_grad, attended, preferred_element_type=single
-    )
     mid_small = jnp.concatenate([gate_bias_grad, up_bias_grad, inner_gain_grad, inner_bias_grad])
     mid_pack, mid_at = pack(
         [
             gate_weight_grad.astype(narrow),
             up_weight_grad.astype(narrow),
             down_weight_grad_t.astype(narrow),
-            proj_weight_grad_t.astype(narrow),
-            jnp.stack(
-                [gain_two_grad, shift_two_grad, down_bias_grad, proj_bias_grad], axis=1
+            jnp.concatenate(
+                [down_bias_grad[:, None], spread(mid_small, rows_local, row_count)], axis=1
             ).astype(narrow),
-            spread(mid_small, rows_local, row_count).astype(narrow),
         ]
     )
-    mid_pack, attn_grad_held = lax.optimization_barrier((mid_pack, attn_grad))
+    mid_pack, gate_grad, up_grad = lax.optimization_barrier((mid_pack, gate_grad, up_grad))
     mid_sums = lax.psum_scatter(mid_pack, "row", scatter_dimension=0, tiled=True).astype(single)
+    second_back = join_columns(
+        jnp.einsum("tf,df->td", gate_grad, gate_full, preferred_element_type=single)
+        + jnp.einsum("tf,df->td", up_grad, up_full, preferred_element_type=single)
+    )
+    second_delta, gain_two_grad, shift_two_grad = norm_backward(
+        second_back, normed_two, inv_std_two, ffn_vectors[:, 0]
+    )
+    residual_grad = out_float + second_delta
+    attn_grad = residual_grad.astype(narrow)
+    proj_bias_grad = jnp.sum(attn_grad.astype(single), axis=0)
+    proj_weight_grad_t = jnp.einsum(
+        "td,te->de", attn_grad, attended, preferred_element_type=single
+    )
     attended_grad = jnp.einsum(
-        "td,de->te", attn_grad_held, proj_t, preferred_element_type=single
+        "td,de->te", attn_grad, proj_t, preferred_element_type=single
     ).astype(narrow)
 
     def attend_back(operands):
@@ -374,9 +372,18 @@
     end_pack, end_at = pack(
         [
             qkv_weight_grad.reshape(model_width, 3 * half_width).astype(narrow),
-            jnp.stack([gain_one_grad, shift_one_grad], axis=1).astype(narrow),
-            spread(
-                jnp.concatenate([query_bias_grad, value_bias_grad]), rows_local, row_count
+            proj_weight_grad_t.astype(narrow),
+            jnp.concatenate(
+                [
+                    jnp.stack(
+                        [gain_one_grad, shift_one_grad, proj_bias_grad, gain_two_grad, shift_two_grad],
+                        axis=1,
+                    ),
+                    spread(
+                        jnp.concatenate([query_bias_grad, value_bias_grad]), rows_local, row_count
+                    ),
+                ],
+                axis=1,
             ).astype(narrow),
         ]
     )
@@ -386,22 +393,22 @@
     def cut(sums, offset, width):
         return sums[:, offset : offset + width]
 
-    mid_vectors = cut(mid_sums, mid_at[4], 4)
-    mid_small_sum = cut(mid_sums, mid_at[5], -(-mid_small.shape[0] // rows_local)).reshape(-1)
-    end_vectors = cut(end_sums, end_at[1], 2)
-    end_small_sum = cut(end_sums, end_at[2], -(-2 * half_width // rows_local)).reshape(-1)
+    mid_tail = cut(mid_sums, mid_at[3], 1 + -(-mid_small.shape[0] // rows_local))
+    mid_small_sum = mid_tail[:, 1:].reshape(-1)
+    end_tail = cut(end_sums, end_at[2], 5 + -(-2 * half_width // rows_local))
+    end_small_sum = end_tail[:, 5:].reshape(-1)
     return (
         layer_out,
         input_grad,
-        end_vectors[:, 0],
-        end_vectors[:, 1],
+        end_tail[:, 0],
+        end_tail[:, 1],
         cut(end_sums, end_at[0], 3 * half_width).reshape(rows_local, 3, half_width),
         end_small_sum[:half_width],
         end_small_sum[half_width : 2 * half_width],
-        cut(mid_sums, mid_at[3], half_width).T,
-        mid_vectors[:, 3],
-        mid_vectors[:, 0],
-        mid_vectors[:, 1],
+        cut(end_sums, end_at[1], half_width).T,
+        end_tail[:, 2],
+        end_tail[:, 3],
+        end_tail[:, 4],
         cut(mid_sums, mid_at[0], ff_local),
         mid_small_sum[:ff_local],
         cut(mid_sums, mid_at[1], ff_local),
@@ -409,7 +416,7 @@
         mid_small_sum[2 * ff_local : 3 * ff_local],
         mid_small_sum[3 * ff_local : 4 * ff_local],
         cut(mid_sums, mid_at[2], ff_local).T,
-        mid_vectors[:, 2],
+        mid_tail[:, 0],
     )
 
 

time: 620 us -> 621 us (level)
  local copies, waits for them, and re-layouts: 104 us -> 95 us
  waiting for transfers between devices: 178 us -> 186 us
  other arithmetic: 94.2 us -> 101 us
    reduce_scatter x1, waiting for transfers between devices: 58.9 us -> 78.2 us  [body(): lax.psum_scatter(end_pack, 'row', scatter_dimension=0, tiled=True)]
    unnamed x141 -> x123, local copies, waits for them, and re-layouts: 34.7 us -> 22.9 us
    unnamed x5, waiting for transfers between devices: 20.8 us -> 9.31 us
    concatenate x3 -> x4, other arithmetic: 6.85 us -> 14.7 us  [pack(): return (jnp.concatenate(padded, axis=1), offsets)]
    reduce_sum x2 -> x3, other arithmetic: 13.7 us -> 15.5 us  [the longest x1 7.56 us: body(): gate_bias_grad = jnp.sum(gate_grad.astype(single), axis=0)]
  transfers between devices with their start and end apart: 15 -> 15, of which waited for: 7 -> 9; matrix products, arithmetic and copies ran while one was open for 55% -> 56% of each run, Pallas kernels for 0% -> 0%
where the time goes in v1:
time: 621 us; the launch traced here: 609 us
  matrix products  209 us (34%)
  waiting for transfers between devices  186 us (30%)
  other arithmetic  101 us (16%)
  local copies, waits for them, and re-layouts  95 us (15%)
  between operations  15 us (2%)
    reduce_scatter x1, waiting for transfers between devices, body(): lax.psum_scatter(end_pack, 'row', scatter_dimension=0, tiled=True)  78.2 us
    all_gather x1, waiting for transfers between devices, body(): attn_full = lax.all_gather(attn_pack, 'row', axis=0, tiled=True)  71.5 us
    unnamed x123, local copies, waits for them, and re-layouts  22.9 us
    dot_general x8, matrix products, attend(): jnp.einsum('qk,kd->qd', weights.astype(narrow), value_block, preferred_el...  20.9 us
    dot_general x8, matrix products, attend_back(): jnp.einsum('qk,qd->kd', weights.astype(narrow), grad_block, preferred_ele...  20.2 us
    dot_general x8, matrix products, attend_back(): jnp.einsum('qk,qd->kd', score_grad, query_block, preferred_element_type=s...  20 us
    all_gather x1, waiting for transfers between devices, body(): ffn_full = lax.all_gather(ffn_pack, 'row', axis=0, tiled=True)  18.8 us
    dot_general x8, matrix products, attend_back(): jnp.einsum('qd,kd->qk', grad_block, value_block, preferred_element_type=s...  17.3 us
  transfers between devices with their start and end apart: 15, of which 9 were waited for; matrix products, arithmetic and copies ran while one was open for 56% of the time, Pallas kernels for 0%

profile of v1, /device:TPU:0, one launch (start us, length us, event | category | flops | bytes accessed | tf_op | source)
XLA Modules:
  0.0 608.8 jit_solution(5914213318398008296)
XLA Ops:
  20.2 71.5 %all-gather.3.cloned.1.call-done = bf16[1024,2176]{1,0:T(8,128)(2,1)} async-done(((bf16[64,2176]{1,0:T(8,128)(2,1)}), bf16[1024,2176]{1,0:T(8,128)(2,1)}) %all-gather.3.cloned.1.call-update) | async-done | bytes 4456464 | tf_op jit(solution)/shard_map/all_gather | solution.py:173
  93.9 3.8 slice.171
  97.6 4.7 copy.108
  102.4 6.1 convolution_add_fusion.2
  114.0 3.0 copy.110
  121.4 3.0 copy.115
  124.4 3.7 copy.116
  130.5 3.7 copy.117
  134.2 41.9 %while.24 = (s32[]{:T(128)}, bf16[8,1025,64]{1,2,0:T(8,128)(2,1)}, bf16[8,1025,64]{2,1,0:T(8,128)(2,1)S(1)}, bf16[8,1025,64]{2,1,0:T(8,128)(2,1)}, bf16[8,1025,64]{2,1,0:T(8,128)(2,1)}, /*index=5*/s32[]{:T(128)}) while((s32[]{:T(128)}, bf16[8,1025,64]{1,2,0:T(8,128)(2,1)}, bf16[8,1025,64]{2,1,0:T(8,128)(2,1)S(1)}, ...), condition=%wide.region_5.6_spmd, body=%wide.region_2.5_spmd.sunk | while | flops 276377920 | bytes 13570157 | solution.py:211
  136.8 2.6 fusion.189
  142.0 2.6 fusion.189
  157.5 2.7 fusion.189
  167.9 2.6 fusion.189
  176.2 3.8 fusion.108
  191.9 18.8 %all-gather.5.cloned.1.call-done = bf16[1024,4352]{1,0:T(8,128)(2,1)} async-done(((bf16[64,4352]{1,0:T(8,128)(2,1)}), bf16[1024,4352]{1,0:T(8,128)(2,1)}) %all-gather.5.cloned.1.call-update) | async-done | bytes 8912912 | tf_op jit(solution)/shard_map/all_gather | solution.py:229
  212.8 5.8 convolution_add_fusion.1
  218.6 6.4 %fusion.153 = (f32[1025]{0:T(1024)S(1)}, f32[1025,1365]{1,0:T(8,128)S(1)}, f32[1025,1365]{1,0:T(8,128)S(1)}) fusion(f32[1025,1365]{1,0:T(8,128)S(1)} %convolution_add_fusion.1, f32[1365]{0:T(1024)S(1)} %convert_element_type.227, bf16[1024,4352]{1,0:T(8,128)(2,1)} %all-gather.5.cloned.1.call-done, f32[1024]{0:T(1024)S(1)} %get-tuple-element.209, ...), kind=kOutput, calls=%fused_computation.277 | convolution fusion | flops 2884646912 | bytes 21798236 | tf_op jit(solution)/shard_map/dot_general | solution.py:242
  225.1 3.3 broadcast_select_fusion.1
  230.4 8.2 %multiply_reduce_fusion.1 = (bf16[1365]{0:T(1024)(128)(2,1)S(1)}, f32[1025]{0:T(1024)S(1)}, f32[1025]{0:T(1024)S(1)}, bf16[1365]{0:T(1024)(128)(2,1)S(1)}, f32[1025,1365]{1,0:T(8,128)}) fusion(f32[1025,1365]{1,0:T(8,128)S(1)} %get-tuple-element.244, f32[1025]{0:T(1024)S(1)} %add_rsqrt_fusion, f32[1025]{0:T(1024)S(1)} %add_multiply_fusion.2, ...), kind=kOutput, calls=%fused_computation.69 | convolution fusion | flops 2882193152 | bytes 16203104 | tf_op jit(solution)/shard_map/td,df->tf/dot_general | solution.py:267
  238.8 5.8 convolution_convert_fusion
  245.8 7.6 %convert_reduce_fusion.1 = (bf16[1365]{0:T(1024)(128)(2,1)S(1)}, bf16[1025,1365]{1,0:T(8,128)(2,1)S(1)}, bf16[1365]{0:T(1024)(128)(2,1)S(1)}, bf16[1025,1365]{1,0:T(8,128)(2,1)S(1)}) fusion(f32[1025,1365]{1,0:T(8,128)S(1)} %convolution_add_fusion.1, f32[1025,1365]{1,0:T(8,128)S(1)} %get-tuple-element.302, f32[1025]{0:T(1024)S(1)} %add_multiply_fusion, ...), kind=kLoop, calls=%fused_computation.71 | loop fusion | flops 33576260 | bytes 28009820 | tf_op jit(solution)/shard_map/reduce_sum | solution.py:281
  253.4 6.3 %convolution_convert_fusion.1 = bf16[1024,1365]{0,1:T(8,128)(2,1)} fusion(bf16[1025,1365]{1,0:T(8,128)(2,1)S(1)} %get-tuple-element.97, f32[1024]{0:T(1024)S(1)} %get-tuple-element.209, f32[1024]{0:T(1024)S(1)} %get-tuple-element.208, f32[1025]{0:T(1024)S(1)} %add_rsqrt_fusion.1, f32[1025]{0:T(1024)S(1)} %broadcast_multiply_fusion.6, ...), kind=kOutput, calls=%fused_computation.115 | convolution fusion | flops 2876252160 | bytes 7709362 | tf_op jit(solution)/shard_map/td,tf->df/dot_general | solution.py:286
  259.8 6.1 convolution_convert_fusion.2
  268.0 7.5 %fusion.54 = bf16[1024,4352]{0,1:T(8,128)(2,1)} fusion(bf16[1024,1365]{0,1:T(8,128)(2,1)} %convolution_convert_fusion, bf16[1024,1365]{0,1:T(8,128)(2,1)} %convolution_convert_fusion.1, bf16[1024,1365]{0,1:T(8,128)(2,1)} %convolution_convert_fusion.2, bf16[1024,128]{0,1:T(8,128)(2,1)S(1)} %fusion.122), kind=kLoop, calls=%fused_computation.65 | loop fusion | flops 80216064 | bytes 17561600 | tf_op jit(solution)/shard_map/concatenate | solution.py:114
  275.5 5.5 fusion.88
  281.0 6.6 %fusion.76 = bf16[1025,1024]{1,0:T(8,128)(2,1)} fusion(f32[1025,1024]{1,0:T(8,128)S(1)} %fusion.88, bf16[1025,1365]{1,0:T(8,128)(2,1)S(1)} %copy-done.24, bf16[1024,4352]{1,0:T(8,128)(2,1)} %all-gather.5.cloned.1.call-done), kind=kOutput, calls=%fused_computation.113 | convolution fusion | flops 2867507200 | bytes 11979434 | tf_op jit(solution)/shard_map/tf,df->td/dot_general | solution.py:302
  289.5 3.0 copy.126
  292.5 11.7 %copy.145 = bf16[1024,4352]{1,0:T(8,128)(2,1)} copy(bf16[1024,4352]{0,1:T(8,128)(2,1)} %fusion.54) | data formatting | bytes 17825792
  304.3 5.4 fusion.72
  309.8 4.3 convert_reduce_fusion.4
  316.2 2.6 convolution_convert_fusion.3
  320.3 100.7 %while.25 = (s32[]{:T(128)}, f32[8,1025,64]{1,2,0:T(8,128)S(1)}, f32[8,1025,64]{1,2,0:T(8,128)}, bf16[8,1025,64]{1,2,0:T(8,128)(2,1)}, bf16[8,1025,64]{2,1,0:T(8...) while((s32[]{:T(128)}, f32[8,1025,64]{1,2,0:T(8,128)S(1)}, ...), condition=%wide.region_23.24_spmd, body=%wide.region_19.23_spmd.sunk | while | flops 689338112 | bytes 38548656 | solution.py:341
  421.0 3.1 copy.131
  424.1 3.5 bitcast_multiply_fusion.1
  429.8 3.2 copy.125
  435.3 3.3 copy.128
  438.6 5.0 add_convert_fusion.3
  443.6 4.8 fusion.75
  450.1 5.2 convolution_convert_fusion.5
  457.6 7.9 %convolution_convert_fusion.4 = bf16[1024,3,512]{0,2,1:T(8,128)(2,1)} fusion(f32[1024]{0:T(1024)S(1)} %copy-done.49, f32[1024]{0:T(1024)S(1)} %copy-done.45, bf16[1025,1,512]{2,0,1:T(8,128)(2,1)} %copy.131, bf16[1025,1,512]{2,0,1:T(8,128)(2,1)} %copy-done.19, bf16[1025,1,512]{2,0,1:T(8,128)(2,1)S(1)} %get-tuple-element.278, f32[1025]{0:T(1024)S(1)} %copy-done.37, ...), kind=kOutput, calls=%fused_computation.143 | convolution fusion | flops 3244836864 | bytes 8410120 | tf_op jit(solution)/shard_map/td,tpe->dpe/dot_general | solution.py:362
  465.5 4.7 copy.135
  470.2 7.4 %fusion.79 = (bf16[1024]{0:T(1024)(128)(2,1)S(1)}, bf16[1024]{0:T(1024)(128)(2,1)S(1)}, f32[1025]{0:T(1024)S(1)}, f32[1025]{0:T(1024)S(1)}, f32[1025,1024]{1,0:T(8,128)}, /*index=5*/f32[1025,1024]{1,0:T(8,128)}) fusion(bf16[1025,1024]{1,0:T(8,128)(2,1)} %collective-permute-done.10, bf16[1025,1024]{1,0:T(8,128)(2,1)} %fusion.75, f32[1025]{0:T(1024)S(1)} %copy-done.37, ...), kind=kLoop, calls=%fused_computation.119 | loop fusion | flops 16789502 | bytes 14718992 | tf_op jit(solution)/shard_map/reduce_sum | solution.py:33
  478.0 3.6 fusion.65
  481.6 9.2 %reduce-scatter.7.cloned.1.call-done = bf16[64,4352]{1,0:T(8,128)(2,1)} async-done(((bf16[1024,4352]{1,0:T(8,128)(2,1)}), bf16[64,4352]{1,0:T(8,128)(2,1)}) %reduce-scatter.7.cloned.1.call-update) | async-done | bytes 557072
  493.3 6.8 %fusion.84 = f32[1025,1024]{1,0:T(8,128)S(1)} fusion(bf16[1024,4352]{1,0:T(8,128)(2,1)} %all-gather.5.cloned.1.call-done, f32[1025,1365]{1,0:T(8,128)} %copy-done, f32[1365]{0:T(1024)S(1)} %copy-done.47, f32[1365]{0:T(1024)S(1)} %copy-done.41, f32[1025]{0:T(1024)S(1)} %copy-done.39, f32[1025]{0:T(1024)S(1)} %copy-done.33), kind=kOutput, calls=%fused_computation.126 | convolution fusion | flops 2872403712 | bytes 12913328 | tf_op jit(solution)/shard_map/tf,df->td/dot_general | solution.py:255
  503.0 3.5 add_convert_fusion.4
  506.6 3.1 fusion.96
  517.5 78.2 %reduce-scatter.5.cloned.1.call-done = bf16[64,2176]{1,0:T(8,128)(2,1)} async-done(((bf16[1024,2176]{1,0:T(8,128)(2,1)}), bf16[64,2176]{1,0:T(8,128)(2,1)}) %reduce-scatter.5.cloned.1.call-update) | async-done | bytes 278544 | tf_op jit(solution)/shard_map/reduce_scatter | solution.py:391
  (333 shorter events, 211.7 us)
Async XLA Ops:
  7.2 10.4 %copy-start.7 = (bf16[1025,512]{1,0:T(8,128)(2,1)S(1)}, bf16[1025,512]{1,0:T(8,128)(2,1)}, u32[]{:S(2)}) copy-start(bf16[1025,512]{1,0:T(8,128)(2,1)} %param.23) | copy-start | bytes 3148804
  7.2 84.5 %all-gather.3.cloned.1.call-start = ((), (), s32[]{:S(2)}) async-start(), calls=%async_computation.2 | async-start | bytes 4734976 | tf_op jit(solution)/shard_map/all_gather | solution.py:173
  10.7 199.9 %all-gather.5.cloned.1.call-start = ((), (), s32[]{:S(2)}) async-start(), calls=%async_computation.3 | async-start | bytes 9469952 | tf_op jit(solution)/shard_map/all_gather | solution.py:229
  10.7 6.9 %collective-permute-start = (bf16[1025,512]{1,0:T(8,128)(2,1)}, bf16[1025,512]{1,0:T(8,128)(2,1)}, u32[]{:S(2)}, u32[]{:S(2)}) collective-permute-start(bf16[1025,512]{1,0:T(8,128)(2,1)} %param.23), channel_id=1, source_target_pairs={{0,1},{1,0},{2,3},{3,2},{4,5},{5,4},{6,7},{7,6},{8,9},{9,8},{10,11... | collective-permute-start | bytes 3148808 | tf_op jit(solution)/shard_map/ppermute | solution.py:73
  14.1 476.8 %reduce-scatter.7.cloned.1.call-start = ((), (), s32[]{:S(2)}) async-start(), calls=%async_computation.5 | async-start | bytes 9469952
  19.0 83.3 %copy-start.3 = (bf16[1025,512]{1,0:T(8,128)(2,1)}, bf16[1025,512]{1,0:T(8,128)(2,1)S(1)}, u32[]{:S(2)}) copy-start(bf16[1025,512]{1,0:T(8,128)(2,1)S(1)} %get-tuple-element.284) | copy-start | bytes 3148804
  19.0 83.3 %copy-start.5 = (bf16[1025,512]{1,0:T(8,128)(2,1)}, bf16[1025,512]{1,0:T(8,128)(2,1)S(1)}, u32[]{:S(2)}) copy-start(bf16[1025,512]{1,0:T(8,128)(2,1)S(1)} %get-tuple-element.285) | copy-start | bytes 3148804
  19.4 82.9 %copy-start.34 = (f32[1025]{0:T(1024)}, f32[1025]{0:T(1024)S(1)}, u32[]{:S(2)}) copy-start(f32[1025]{0:T(1024)S(1)} %broadcast_multiply_fusion.7) | copy-start | bytes 12304
  20.2 82.2 %copy-start.36 = (f32[1025]{0:T(1024)}, f32[1025]{0:T(1024)S(1)}, u32[]{:S(2)}) copy-start(f32[1025]{0:T(1024)S(1)} %add_rsqrt_fusion.2) | copy-start | bytes 12304
  93.9 8.5 %copy-start.44 = (f32[1024]{0:T(1024)}, f32[1024]{0:T(1024)S(1)}, u32[]{:S(2)}) copy-start(f32[1024]{0:T(1024)S(1)} %get-tuple-element.206) | copy-start | bytes 12292
  93.9 8.5 %copy-start.48 = (f32[1024]{0:T(1024)}, f32[1024]{0:T(1024)S(1)}, u32[]{:S(2)}) copy-start(f32[1024]{0:T(1024)S(1)} %get-tuple-element.207) | copy-start | bytes 12292
  182.3 2.9 collective-permute-start.1
  187.7 2.7 collective-permute-start.2
  187.9 37.2 %collective-permute-start.6 = (bf16[1025,512]{1,0:T(8,128)(2,1)}, bf16[1025,512]{1,0:T(8,128)(2,1)}, u32[]{:S(2)}, u32[]{:S(2)}) collective-permute-start(bf16[1025,512]{1,0:T(8,128)(2,1)} %param.41), channel_id=1, source_target_pairs={{0,1},{1,0},{2,3},{3,2},{4,5},{5,4},{6,7},{7,6},{8,9},{9,8},{10,11... | collective-permute-start | bytes 3148808 | tf_op jit(solution)/shard_map/ppermute | solution.py:73
  188.3 50.5 %copy-start.46 = (f32[1365]{0:T(1024)}, f32[1365]{0:T(1024)S(1)}, u32[]{:S(2)}) copy-start(f32[1365]{0:T(1024)S(1)} %convert_element_type.229) | copy-start | bytes 16384
  188.4 57.4 %copy-start.40 = (f32[1365]{0:T(1024)}, f32[1365]{0:T(1024)S(1)}, u32[]{:S(2)}) copy-start(f32[1365]{0:T(1024)S(1)} %convert_element_type.228) | copy-start | bytes 16384
  225.0 20.8 %copy-start = (f32[1025,1365]{1,0:T(8,128)}, f32[1025,1365]{1,0:T(8,128)S(1)}, u32[]{:S(2)}) copy-start(f32[1025,1365]{1,0:T(8,128)S(1)} %get-tuple-element.244) | copy-start | bytes 16789504
  225.0 3.4 collective-permute-start.3
  228.4 10.4 %copy-start.9 = (bf16[1025,512]{1,0:T(8,128)(2,1)}, bf16[1025,512]{1,0:T(8,128)(2,1)S(1)}, u32[]{:S(2)}) copy-start(bf16[1025,512]{1,0:T(8,128)(2,1)S(1)} %get-tuple-element.281) | copy-start | bytes 3148804
  228.4 17.4 %copy-start.32 = (f32[1025]{0:T(1024)}, f32[1025]{0:T(1024)S(1)}, u32[]{:S(2)}) copy-start(f32[1025]{0:T(1024)S(1)} %add_multiply_fusion.2) | copy-start | bytes 12304
  229.2 1.2 collective-permute-start.4
  230.4 15.4 %copy-start.38 = (f32[1025]{0:T(1024)}, f32[1025]{0:T(1024)S(1)}, u32[]{:S(2)}) copy-start(f32[1025]{0:T(1024)S(1)} %add_rsqrt_fusion) | copy-start | bytes 12304
  238.7 6.3 %collective-permute-start.8 = (f32[1025]{0:T(1024)S(1)}, f32[1025]{0:T(1024)S(1)}, u32[]{:S(2)}, u32[]{:S(2)}) collective-permute-start(f32[1025]{0:T(1024)S(1)} %get-tuple-element.188), channel_id=1, source_target_pairs={{0,1},{1,0},{2,3},{3,2},{4,5},{5,4},{6,7},{7,6},{8,9},{9,8},{10,11... | collective-permute-start | bytes 12308 | tf_op jit(solution)/shard_map/ppermute | solution.py:73
  244.6 1.2 collective-permute-start.7
  253.4 6.4 %copy-start.23 = (bf16[1025,1365]{1,0:T(8,128)(2,1)}, bf16[1025,1365]{1,0:T(8,128)(2,1)S(1)}, u32[]{:S(2)}) copy-start(bf16[1025,1365]{1,0:T(8,128)(2,1)S(1)} %get-tuple-element.97) | copy-start | bytes 8394754
  253.4 6.4 %copy-start.25 = (bf16[1025,1365]{1,0:T(8,128)(2,1)}, bf16[1025,1365]{1,0:T(8,128)(2,1)S(1)}, u32[]{:S(2)}) copy-start(bf16[1025,1365]{1,0:T(8,128)(2,1)S(1)} %get-tuple-element.96) | copy-start | bytes 8394754
  268.0 7.5 %copy-start.26 = (bf16[1025,1365]{1,0:T(8,128)(2,1)S(1)}, bf16[1025,1365]{1,0:T(8,128)(2,1)}, u32[]{:S(2)}) copy-start(bf16[1025,1365]{1,0:T(8,128)(2,1)} %copy-done.25) | copy-start | bytes 8394754
  281.0 7.0 %copy-start.30 = (f32[1025,64]{0,1:T(8,128)S(1)}, f32[1025,64]{0,1:T(8,128)}, u32[]{:S(2)}) copy-start(f32[1025,64]{0,1:T(8,128)} %get-tuple-element.294) | copy-start | bytes 787204
  287.6 16.7 %collective-permute-start.9 = (bf16[1025,1024]{1,0:T(8,128)(2,1)}, bf16[1025,1024]{1,0:T(8,128)(2,1)}, u32[]{:S(2)}, u32[]{:S(2)}) collective-permute-start(bf16[1025,1024]{1,0:T(8,128)(2,1)} %fusion.76), channel_id=1, source_target_pairs={{0,1},{1,0},{2,3},{3,2},{4,5},{5,4},{6,7},{7,6},{8,9},{9,8},{10,11... | collective-permute-start | bytes 6297608 | tf_op jit(solution)/shard_map/ppermute | solution.py:73
  304.3 291.5 %reduce-scatter.5.cloned.1.call-start = ((), (), s32[]{:S(2)}) async-start(), calls=%async_computation.4 | async-start | bytes 4734976 | tf_op jit(solution)/shard_map/reduce_scatter | solution.py:391
  320.3 103.8 %copy-start.28 = (f32[1025,64]{0,1:T(8,128)S(1)}, f32[1025,64]{0,1:T(8,128)}, u32[]{:S(2)}) copy-start(f32[1025,64]{0,1:T(8,128)} %get-tuple-element.295) | copy-start | bytes 787204
  421.0 6.6 %copy-start.13 = (f32[8,1025,64]{1,2,0:T(8,128)}, f32[8,1025,64]{1,2,0:T(8,128)S(1)}, u32[]{:S(2)}) copy-start(f32[8,1025,64]{1,2,0:T(8,128)S(1)} %get-tuple-element.98) | copy-start | bytes 6297604
  448.4 21.8 %collective-permute-start.10 = (bf16[1025,1024]{1,0:T(8,128)(2,1)}, bf16[1025,1024]{1,0:T(8,128)(2,1)}, u32[]{:S(2)}, u32[]{:S(2)}) collective-permute-start(bf16[1025,1024]{1,0:T(8,128)(2,1)} %fusion.75), channel_id=1, source_target_pairs={{0,1},{1,0},{2,3},{3,2},{4,5},{5,4},{6,7},{7,6},{8,9},{9,8},{10,11... | collective-permute-start | bytes 6297608 | tf_op jit(solution)/shard_map/ppermute | solution.py:73
  450.0 7.6 %copy-start.4 = (bf16[1025,512]{1,0:T(8,128)(2,1)S(1)}, bf16[1025,512]{1,0:T(8,128)(2,1)}, u32[]{:S(2)}) copy-start(bf16[1025,512]{1,0:T(8,128)(2,1)} %copy-done.3) | copy-start | bytes 3148804
  450.0 7.6 %copy-start.6 = (bf16[1025,512]{1,0:T(8,128)(2,1)S(1)}, bf16[1025,512]{1,0:T(8,128)(2,1)}, u32[]{:S(2)}) copy-start(bf16[1025,512]{1,0:T(8,128)(2,1)} %copy-done.5) | copy-start | bytes 3148804
  450.0 7.6 %copy-start.35 = (f32[1025]{0:T(1024)S(1)}, f32[1025]{0:T(1024)}, u32[]{:S(2)}) copy-start(f32[1025]{0:T(1024)} %copy-done.34) | copy-start | bytes 12304
  450.0 7.6 %copy-start.37 = (f32[1025]{0:T(1024)S(1)}, f32[1025]{0:T(1024)}, u32[]{:S(2)}) copy-start(f32[1025]{0:T(1024)} %copy-done.36) | copy-start | bytes 12304
  450.0 7.6 %copy-start.45 = (f32[1024]{0:T(1024)S(1)}, f32[1024]{0:T(1024)}, u32[]{:S(2)}) copy-start(f32[1024]{0:T(1024)} %copy-done.44) | copy-start | bytes 12292
  450.0 7.6 %copy-start.49 = (f32[1024]{0:T(1024)S(1)}, f32[1024]{0:T(1024)}, u32[]{:S(2)}) copy-start(f32[1024]{0:T(1024)} %copy-done.48) | copy-start | bytes 12292
  470.2 7.8 %copy-start.21 = (bf16[1024,512]{1,0:T(8,128)(2,1)S(1)}, bf16[1024,512]{1,0:T(8,128)(2,1)}, u32[]{:S(2)}) copy-start(bf16[1024,512]{1,0:T(8,128)(2,1)} %copy.136) | copy-start | bytes 3145732
  492.7 13.8 %slice-start.2 = ((s8[4227072]{0:T(1024)(128)(4,1)}), s8[32768]{0:T(1024)(128)(4,1)S(1)}, s32[]{:S(2)}) async-start(s8[4227072]{0:T(1024)(128)(4,1)} %bitcast.209), calls=%async_computation.8 | async-start | bytes 65536
  493.3 7.1 %copy-start.31 = (f32[1024,1]{1,0:T(8,128)S(1)}, f32[1024,1]{1,0:T(8,128)}, u32[]{:S(2)}) copy-start(f32[1024,1]{1,0:T(8,128)} %get-tuple-element.288) | copy-start | bytes 12292
  493.3 9.7 %copy-start.8 = (bf16[1025,512]{1,0:T(8,128)(2,1)S(1)}, bf16[1025,512]{1,0:T(8,128)(2,1)}, u32[]{:S(2)}) copy-start(bf16[1025,512]{1,0:T(8,128)(2,1)} %param.23) | copy-start | bytes 3148804
  493.3 9.7 %copy-start.18 = (bf16[1025,512]{1,0:T(8,128)(2,1)S(1)}, bf16[1025,512]{1,0:T(8,128)(2,1)}, u32[]{:S(2)}) copy-start(bf16[1025,512]{1,0:T(8,128)(2,1)} %copy-done.17) | copy-start | bytes 3148804
  493.3 9.7 %copy-start.43 = (f32[512]{0:T(512)S(1)}, f32[512]{0:T(512)}, u32[]{:S(2)}) copy-start(f32[512]{0:T(512)} %copy-done.42) | copy-start | bytes 6148
  493.3 13.3 %slice-start.3 = ((s8[4227072]{0:T(1024)(128)(4,1)}), s8[4194304]{0:T(1024)(128)(4,1)S(1)}, s32[]{:S(2)}) async-start(s8[4227072]{0:T(1024)(128)(4,1)} %bitcast.209), calls=%async_computation.9 | async-start | bytes 8388608
  500.3 2.7 collective-permute-start.5
  500.4 6.2 %slice-start = ((s8[4227072]{0:T(1024)(128)(4,1)}), s8[4194304]{0:T(1024)(128)(4,1)S(1)}, s32[]{:S(2)}) async-start(s8[4227072]{0:T(1024)(128)(4,1)} %bitcast.207), calls=%async_computation.6 | async-start | bytes 8388608
  (25 other events, 93.0 us)
Sparse Core Ops, SparseCore 0:
  11.3 80.3 all-gather.2
  95.0 115.5 all-gather.4
  304.4 186.4 reduce-scatter.6
  493.1 102.6 reduce-scatter.4

commit v2 on v0

--- a/solution.py
+++ b/solution.py
@@ -4,6 +4,7 @@
 import jax
 import jax.numpy as jnp
 from jax import lax
+from jax.experimental.layout import Layout, with_layout_constraint
 from jax.sharding import PartitionSpec as P
 
 
@@ -96,6 +97,10 @@
 
 def hidden_totals(row_sums):
     return tuple(part + swap_columns(part) for part in row_sums)
+
+
+def row_major(values):
+    return with_layout_constraint(values, Layout((0, 1)))
 
 
 def lane_round(width):
@@ -300,10 +305,10 @@
     mid_small = jnp.concatenate([gate_bias_grad, up_bias_grad, inner_gain_grad, inner_bias_grad])
     mid_pack, mid_at = pack(
         [
-            gate_weight_grad.astype(narrow),
-            up_weight_grad.astype(narrow),
-            down_weight_grad_t.astype(narrow),
-            proj_weight_grad_t.astype(narrow),
+            row_major(gate_weight_grad.astype(narrow)),
+            row_major(up_weight_grad.astype(narrow)),
+            row_major(down_weight_grad_t.astype(narrow)),
+            row_major(proj_weight_grad_t.astype(narrow)),
             jnp.stack(
                 [gain_two_grad, shift_two_grad, down_bias_grad, proj_bias_grad], axis=1
             ).astype(narrow),

time: 620 us -> 608 us (0.981)
  local copies, waits for them, and re-layouts: 104 us -> 80 us
    unnamed x141 -> x138, local copies, waits for them, and re-layouts: 34.7 us -> 10.2 us
    unnamed x5 -> x4, waiting for transfers between devices: 20.8 us -> 0.07 us
    reduce_scatter x0 -> x1, waiting for transfers between devices: none -> 20.6 us  [body(): lax.psum_scatter(mid_pack, 'row', scatter_dimension=0, tiled=True)]
    reduce_scatter x1, waiting for transfers between devices: 58.9 us -> 65.8 us  [body(): lax.psum_scatter(end_pack, 'row', scatter_dimension=0, tiled=True)]
  transfers between devices with their start and end apart: 15 -> 15, of which waited for: 7 -> 7; matrix products, arithmetic and copies ran while one was open for 55% -> 54% of each run, Pallas kernels for 0% -> 0%
where the time goes in v2:
time: 608 us; the launch traced here: 597 us
  matrix products  216 us (36%)
  waiting for transfers between devices  184 us (30%)
  other arithmetic  96.8 us (16%)
  local copies, waits for them, and re-layouts  80 us (13%)
  between operations  15.4 us (3%)
    all_gather x1, waiting for transfers between devices, body(): attn_full = lax.all_gather(attn_pack, 'row', axis=0, tiled=True)  72.9 us
    reduce_scatter x1, waiting for transfers between devices, body(): lax.psum_scatter(end_pack, 'row', scatter_dimension=0, tiled=True)  65.8 us
    dot_general x8, matrix products, attend(): jnp.einsum('qk,kd->qd', weights.astype(narrow), value_block, preferred_el...  20.9 us
    reduce_scatter x1, waiting for transfers between devices, body(): lax.psum_scatter(mid_pack, 'row', scatter_dimension=0, tiled=True)  20.6 us
    dot_general x8, matrix products, attend_back(): jnp.einsum('qk,qd->kd', weights.astype(narrow), grad_block, preferred_ele...  20.3 us
    dot_general x8, matrix products, attend_back(): jnp.einsum('qk,qd->kd', score_grad, query_block, preferred_element_type=s...  20.1 us
    all_gather x1, waiting for transfers between devices, body(): ffn_full = lax.all_gather(ffn_pack, 'row', axis=0, tiled=True)  18.8 us
    dot_general x8, matrix products, attend_back(): jnp.einsum('qd,kd->qk', grad_block, value_block, preferred_element_type=s...  17.3 us
  transfers between devices with their start and end apart: 15, of which 7 were waited for; matrix products, arithmetic and copies ran while one was open for 54% of the time, Pallas kernels for 0%

profile of v2, /device:TPU:0, one launch (start us, length us, event | category | flops | bytes accessed | tf_op | source)
XLA Modules:
  0.0 596.5 jit_solution(3297287169671091407)
XLA Ops:
  18.9 72.9 %all-gather.3.cloned.1.call-done = bf16[1024,2176]{1,0:T(8,128)(2,1)} async-done(((bf16[64,2176]{1,0:T(8,128)(2,1)}), bf16[1024,2176]{1,0:T(8,128)(2,1)}) %all-gather.3.cloned.1.call-update) | async-done | bytes 4456464 | tf_op jit(solution)/shard_map/all_gather | solution.py:178
  93.9 3.8 slice.169
  97.7 4.7 copy.164
  102.4 6.1 %convolution_add_fusion.2 = f32[1025,3,512]{2,0,1:T(8,128)S(1)} fusion(bf16[1024,3,512]{0,2,1:T(8,128)(2,1)} %bitcast.221, f32[3,512]{1,0:T(4,128)S(1)} %pad_maximum_fusion.8, f32[1024]{0:T(1024)S(1)} %get-tuple-element.251, f32[1024]{0:T(1024)S(1)} %get-tuple-element.250, f32[1025]{0:T(1024)S(1)} %add_rsqrt_fusion.2, ...), kind=kOutput, calls=%fused_computation.69 | convolution fusion | flops 3235392000 | bytes 11565064 | tf_op jit(solution)/shard_map/td,dpe->tpe/dot_general | solution.py:194
  114.0 3.0 copy.166
  121.5 3.0 copy.171
  124.5 3.7 copy.172
  130.5 3.7 copy.173
  134.2 42.0 %while.24 = (s32[]{:T(128)}, bf16[8,1025,64]{1,2,0:T(8,128)(2,1)}, bf16[8,1025,64]{2,1,0:T(8,128)(2,1)S(1)}, bf16[8,1025,64]{2,1,0:T(8,128)(2,1)}, bf16[8,1025,64]{2,1,0:T(8,128)(2,1)}, /*index=5*/s32[]{:T(128)}) while((s32[]{:T(128)}, bf16[8,1025,64]{1,2,0:T(8,128)(2,1)}, bf16[8,1025,64]{2,1,0:T(8,128)(2,1)S(1)}, ...), condition=%wide.region_5.6_spmd, body=%wide.region_2.5_spmd.sunk | while | flops 276377920 | bytes 13570157 | solution.py:216
  136.8 2.6 fusion.185
  147.2 2.6 fusion.185
  152.3 2.6 fusion.185
  157.5 2.7 fusion.185
  162.8 2.6 fusion.185
  167.9 2.6 fusion.185
  173.1 2.6 fusion.185
  176.2 3.8 fusion.104
  191.9 18.8 %all-gather.5.cloned.1.call-done = bf16[1024,4352]{1,0:T(8,128)(2,1)} async-done(((bf16[64,4352]{1,0:T(8,128)(2,1)}), bf16[1024,4352]{1,0:T(8,128)(2,1)}) %all-gather.5.cloned.1.call-update) | async-done | bytes 8912912 | tf_op jit(solution)/shard_map/all_gather | solution.py:234
  212.8 5.8 convolution_add_fusion.1
  218.7 11.8 %fusion.147 = (f32[1025]{0:T(1024)S(1)}, f32[1025,1365]{1,0:T(8,128)}, f32[1025,1365]{1,0:T(8,128)}) fusion(f32[1025,1365]{1,0:T(8,128)S(1)} %convolution_add_fusion.1, f32[1365]{0:T(1024)S(1)} %convert_element_type.244, bf16[1024,4352]{1,0:T(8,128)(2,1)} %all-gather.5.cloned.1.call-done, f32[1024]{0:T(1024)S(1)} %get-tuple-element.253, ...), kind=kOutput, calls=%fused_computation.270 | convolution fusion | flops 2884646912 | bytes 21798236 | tf_op jit(solution)/shard_map/dot_general | solution.py:247
  232.1 3.1 copy.182
  235.3 3.4 multiply_reduce_fusion.3
  241.1 8.3 %multiply_reduce_fusion.1 = (bf16[1365]{0:T(1024)(128)(2,1)S(1)}, f32[1025]{0:T(1024)S(1)}, f32[1025]{0:T(1024)S(1)}, bf16[1365]{0:T(1024)(128)(2,1)S(1)}, f32[1025,1365]{1,0:T(8,128)S(1)}) fusion(f32[1025,1365]{1,0:T(8,128)} %get-tuple-element.291, f32[1025]{0:T(1024)S(1)} %add_rsqrt_fusion, f32[1025]{0:T(1024)S(1)} %add_multiply_fusion.2, ...), kind=kOutput, calls=%fused_computation.60 | convolution fusion | flops 2882193152 | bytes 16418828 | tf_op jit(solution)/shard_map/td,df->tf/dot_general | solution.py:272
  250.1 6.7 %convolution_convert_fusion = bf16[1024,1365]{1,0:T(8,128)(2,1)} fusion(bf16[1025,512]{1,0:T(8,128)(2,1)S(1)} %get-tuple-element.323, bf16[1025,512]{1,0:T(8,128)(2,1)S(1)} %get-tuple-element.322, f32[1025,1365]{1,0:T(8,128)S(1)} %bitcast.202, f32[1365]{0:T(1024)S(1)} %convert_element_type.246, f32[1365]{0:T(1024)S(1)} %convert_element_type.245, ...), kind=kOutput, calls=%fused_computation.102 | convolution fusion | flops 2877999872 | bytes 10510340 | tf_op jit(solution)/shard_map/td,tf->df/dot_general | solution.py:268
  256.9 7.7 %fusion.143 = (bf16[1365]{0:T(1024)(128)(2,1)S(1)}, bf16[1025,1365]{1,0:T(8,128)(2,1)S(1)}, bf16[1365]{0:T(1024)(128)(2,1)S(1)}, bf16[1025,1365]{1,0:T(8,128)(2,1)}) fusion(f32[1025,1365]{1,0:T(8,128)S(1)} %bitcast.217, f32[1025]{0:T(1024)S(1)} %add_multiply_fusion, f32[1025,1365]{1,0:T(8,128)S(1)} %bitcast.202, f32[1025]{0:T(1024)S(1)} %add_multiply_fusion.2, ...), kind=kLoop, calls=%fused_computation.267 | loop fusion | flops 30778012 | bytes 28009820 | tf_op jit(solution)/shard_map/reduce_sum | solution.py:287
  264.7 7.2 %fusion.83 = f32[1025,1024]{1,0:T(8,128)S(1)} fusion(bf16[1025,1365]{1,0:T(8,128)(2,1)} %get-tuple-element.299, bf16[1024,4352]{1,0:T(8,128)(2,1)} %all-gather.5.cloned.1.call-done), kind=kOutput, calls=%fused_computation.123 | convolution fusion | flops 2865408000 | bytes 9988096 | tf_op jit(solution)/shard_map/tf,df->td/dot_general | solution.py:293
  271.9 6.7 %fusion.69 = bf16[1025,1024]{1,0:T(8,128)(2,1)} fusion(f32[1025,1024]{1,0:T(8,128)S(1)} %fusion.83, bf16[1025,1365]{1,0:T(8,128)(2,1)S(1)} %get-tuple-element.284, bf16[1024,4352]{1,0:T(8,128)(2,1)} %all-gather.5.cloned.1.call-done), kind=kOutput, calls=%fused_computation.101 | convolution fusion | flops 2867507200 | bytes 11979434 | tf_op jit(solution)/shard_map/tf,df->td/dot_general | solution.py:294
  278.7 6.2 %convolution_convert_fusion.2 = bf16[1024,1365]{1,0:T(8,128)(2,1)} fusion(bf16[1025,1365]{1,0:T(8,128)(2,1)S(1)} %copy-done.24, f32[1024]{0:T(1024)S(1)} %get-tuple-element.253, f32[1024]{0:T(1024)S(1)} %get-tuple-element.252, f32[1025]{0:T(1024)S(1)} %add_rsqrt_fusion.1, f32[1025]{0:T(1024)S(1)} %broadcast_multiply_fusion.6, ...), kind=kOutput, calls=%fused_computation.104 | convolution fusion | flops 2876252160 | bytes 7709362 | tf_op jit(solution)/shard_map/td,tf->df/dot_general | solution.py:288
  287.9 4.9 convolution_convert_fusion.1
  295.1 7.9 %fusion.65 = (bf16[1024]{0:T(1024)(128)(2,1)S(1)}, f32[1025]{0:T(1024)S(1)}, f32[1025]{0:T(1024)S(1)}, bf16[1024]{0:T(1024)(128)(2,1)S(1)}) fusion(bf16[1025,1024]{1,0:T(8,128)(2,1)} %collective-permute-done.9, bf16[1025,1024]{1,0:T(8,128)(2,1)} %fusion.69, f32[1025]{0:T(1024)S(1)} %add_rsqrt_fusion.1, f32[1025]{0:T(1024)S(1)} %broadcast_multiply_fusion.6, ...), kind=kLoop, calls=%fused_computation.92 | loop fusion | flops 16789502 | bytes 6322192 | tf_op jit(solution)/shard_map/reduce_sum | solution.py:34
  303.0 6.9 %fusion.145 = (bf16[1024]{0:T(1024)(128)(2,1)S(1)}, bf16[1025,1024]{1,0:T(8,128)(2,1)}, f32[1025,1024]{1,0:T(8,128)}, bf16[1024]{0:T(1024)(128)(2,1)S(1)}) fusion(f32[1025]{0:T(1024)S(1)} %broadcast_multiply_fusion.4, f32[1025]{0:T(1024)S(1)} %broadcast_multiply_fusion.6, bf16[1025,512]{1,0:T(8,128)(2,1)S(1)} %get-tuple-element.325, ...), kind=kLoop, calls=%fused_computation.269 | loop fusion | flops 24138752 | bytes 14718992 | tf_op jit(solution)/shard_map/reduce_sum | solution.py:301
  310.2 4.7 fusion.94
  322.1 100.9 %while.25 = (s32[]{:T(128)}, f32[8,1025,64]{1,2,0:T(8,128)S(1)}, f32[8,1025,64]{1,2,0:T(8,128)}, bf16[8,1025,64]{1,2,0:T(8,128)(2,1)}, bf16[8,1025,64]{2,1,0:T(8...) while((s32[]{:T(128)}, f32[8,1025,64]{1,2,0:T(8,128)S(1)}, ...), condition=%wide.region_26.27_spmd, body=%wide.region_22.26_spmd.sunk | while | flops 689338112 | bytes 38548656 | solution.py:348
  423.0 3.1 copy.187
  426.1 3.4 bitcast_multiply_fusion.1
  431.7 3.8 copy.181
  437.7 3.2 copy.184
  440.9 5.0 add_convert_fusion.3
  445.9 4.9 fusion.68
  453.5 7.9 %convolution_convert_fusion.4 = bf16[1024,3,512]{0,2,1:T(8,128)(2,1)} fusion(f32[1024]{0:T(1024)S(1)} %copy-done.49, f32[1024]{0:T(1024)S(1)} %copy-done.45, bf16[1025,1,512]{2,0,1:T(8,128)(2,1)} %copy.187, bf16[1025,1,512]{2,0,1:T(8,128)(2,1)} %copy-done.17, bf16[1025,1,512]{2,0,1:T(8,128)(2,1)S(1)} %get-tuple-element.319, f32[1025]{0:T(1024)S(1)} %copy-done.37, ...), kind=kOutput, calls=%fused_computation.136 | convolution fusion | flops 3244836864 | bytes 8410120 | tf_op jit(solution)/shard_map/td,tpe->dpe/dot_general | solution.py:369
  461.3 4.7 copy.189
  466.1 6.7 %fusion.141 = (f32[1025]{0:T(1024)S(1)}, f32[1025]{0:T(1024)S(1)}, bf16[1024]{0:T(1024)(128)(2,1)S(1)}, bf16[1024]{0:T(1024)(128)(2,1)S(1)}, f32[1025,1024]{1,0:T(8,128)}, /*index=5*/f32[1025,1024]{1,0:T(8,128)}) fusion(f32[1025]{0:T(1024)S(1)} %copy-done.37, f32[1025]{0:T(1024)S(1)} %copy-done.35, bf16[1025,512]{1,0:T(8,128)(2,1)S(1)} %copy-done.5, ...), kind=kLoop, calls=%fused_computation.266 | loop fusion | flops 16789502 | bytes 14718992 | tf_op jit(solution)/shard_map/reduce_sum | solution.py:31
  473.1 3.5 fusion.75
  476.6 20.6 %reduce-scatter.3.cloned.1.call-done = bf16[64,4992]{1,0:T(8,128)(2,1)} async-done(((bf16[1024,4992]{1,0:T(8,128)(2,1)}), bf16[64,4992]{1,0:T(8,128)(2,1)}) %reduce-scatter.3.cloned.1.call-update) | async-done | bytes 638992 | tf_op jit(solution)/shard_map/reduce_scatter | solution.py:319
  498.4 7.1 %fusion.79 = f32[1025,1024]{1,0:T(8,128)S(1)} fusion(bf16[1024,4352]{1,0:T(8,128)(2,1)} %all-gather.5.cloned.1.call-done, f32[1025,1365]{1,0:T(8,128)} %get-tuple-element.291, f32[1365]{0:T(1024)S(1)} %copy-done.47, f32[1365]{0:T(1024)S(1)} %copy-done.41, f32[1025]{0:T(1024)S(1)} %copy-done.39, f32[1025]{0:T(1024)S(1)} %copy-done.33), kind=kOutput, calls=%fused_computation.119 | convolution fusion | flops 2872403712 | bytes 12913328 | tf_op jit(solution)/shard_map/tf,df->td/dot_general | solution.py:260
  508.4 3.5 add_convert_fusion.4
  512.0 3.1 fusion.91
  518.4 65.8 %reduce-scatter.5.cloned.1.call-done = bf16[64,1792]{1,0:T(8,128)(2,1)} async-done(((bf16[1024,1792]{1,0:T(8,128)(2,1)}), bf16[64,1792]{1,0:T(8,128)(2,1)}) %reduce-scatter.5.cloned.1.call-update) | async-done | bytes 229392 | tf_op jit(solution)/shard_map/reduce_scatter | solution.py:389
  (345 shorter events, 201.1 us)
Async XLA Ops:
  7.2 9.1 %copy-start.7 = (bf16[1025,512]{1,0:T(8,128)(2,1)S(1)}, bf16[1025,512]{1,0:T(8,128)(2,1)}, u32[]{:S(2)}) copy-start(bf16[1025,512]{1,0:T(8,128)(2,1)} %param.23) | copy-start | bytes 3148804
  7.2 84.5 %all-gather.3.cloned.1.call-start = ((), (), s32[]{:S(2)}) async-start(), calls=%async_computation.2 | async-start | bytes 4734976 | tf_op jit(solution)/shard_map/all_gather | solution.py:178
  10.7 200.0 %all-gather.5.cloned.1.call-start = ((), (), s32[]{:S(2)}) async-start(), calls=%async_computation.3 | async-start | bytes 9469952 | tf_op jit(solution)/shard_map/all_gather | solution.py:234
  10.7 5.6 collective-permute-start
  14.1 483.1 %reduce-scatter.3.cloned.1.call-start = ((), (), s32[]{:S(2)}) async-start(), calls=%async_computation.4 | async-start | bytes 10862592 | tf_op jit(solution)/shard_map/reduce_scatter | solution.py:319
  17.7 84.7 %copy-start.2 = (bf16[1025,512]{1,0:T(8,128)(2,1)}, bf16[1025,512]{1,0:T(8,128)(2,1)S(1)}, u32[]{:S(2)}) copy-start(bf16[1025,512]{1,0:T(8,128)(2,1)S(1)} %get-tuple-element.326) | copy-start | bytes 3148804
  17.7 84.7 %copy-start.4 = (bf16[1025,512]{1,0:T(8,128)(2,1)}, bf16[1025,512]{1,0:T(8,128)(2,1)S(1)}, u32[]{:S(2)}) copy-start(bf16[1025,512]{1,0:T(8,128)(2,1)S(1)} %get-tuple-element.327) | copy-start | bytes 3148804
  18.1 84.3 %copy-start.34 = (f32[1025]{0:T(1024)}, f32[1025]{0:T(1024)S(1)}, u32[]{:S(2)}) copy-start(f32[1025]{0:T(1024)S(1)} %broadcast_multiply_fusion.7) | copy-start | bytes 12304
  18.9 83.5 %copy-start.36 = (f32[1025]{0:T(1024)}, f32[1025]{0:T(1024)S(1)}, u32[]{:S(2)}) copy-start(f32[1025]{0:T(1024)S(1)} %add_rsqrt_fusion.2) | copy-start | bytes 12304
  93.9 8.5 %copy-start.44 = (f32[1024]{0:T(1024)}, f32[1024]{0:T(1024)S(1)}, u32[]{:S(2)}) copy-start(f32[1024]{0:T(1024)S(1)} %get-tuple-element.250) | copy-start | bytes 12292
  93.9 8.5 %copy-start.48 = (f32[1024]{0:T(1024)}, f32[1024]{0:T(1024)S(1)}, u32[]{:S(2)}) copy-start(f32[1024]{0:T(1024)S(1)} %get-tuple-element.251) | copy-start | bytes 12292
  182.4 2.9 collective-permute-start.1
  187.7 2.7 collective-permute-start.2
  187.9 51.3 %collective-permute-start.6 = (bf16[1025,512]{1,0:T(8,128)(2,1)}, bf16[1025,512]{1,0:T(8,128)(2,1)}, u32[]{:S(2)}, u32[]{:S(2)}) collective-permute-start(bf16[1025,512]{1,0:T(8,128)(2,1)} %param.41), channel_id=1, source_target_pairs={{0,1},{1,0},{2,3},{3,2},{4,5},{5,4},{6,7},{7,6},{8,9},{9,8},{10,11... | collective-permute-start | bytes 3148808 | tf_op jit(solution)/shard_map/ppermute | solution.py:74
  218.6 11.9 %copy-start.14 = (f32[1025,1365]{1,0:T(8,128)}, f32[1025,1365]{1,0:T(8,128)S(1)}, u32[]{:S(2)}) copy-start(f32[1025,1365]{1,0:T(8,128)S(1)} %convolution_add_fusion.1) | copy-start | bytes 16789504
  218.6 11.9 %copy-start.52 = (bf16[1365]{0:T(1024)(128)(2,1)S(1)}, bf16[1365]{0:T(1024)(128)(2,1)}, u32[]{:S(2)}) copy-start(bf16[1365]{0:T(1024)(128)(2,1)} %param.38) | copy-start | bytes 8194
  218.6 11.9 %copy-start.53 = (bf16[1365]{0:T(1024)(128)(2,1)S(1)}, bf16[1365]{0:T(1024)(128)(2,1)}, u32[]{:S(2)}) copy-start(bf16[1365]{0:T(1024)(128)(2,1)} %param.37) | copy-start | bytes 8194
  218.6 11.9 %copy-start.29 = (f32[1025,64]{0,1:T(8,128)S(1)}, f32[1025,64]{0,1:T(8,128)}, u32[]{:S(2)}) copy-start(f32[1025,64]{0,1:T(8,128)} %get-tuple-element.339) | copy-start | bytes 787204
  230.5 4.8 collective-permute-start.3
  230.5 19.5 %copy-start.46 = (f32[1365]{0:T(1024)}, f32[1365]{0:T(1024)S(1)}, u32[]{:S(2)}) copy-start(f32[1365]{0:T(1024)S(1)} %convert_element_type.246) | copy-start | bytes 16384
  230.6 26.3 %copy-start.40 = (f32[1365]{0:T(1024)}, f32[1365]{0:T(1024)S(1)}, u32[]{:S(2)}) copy-start(f32[1365]{0:T(1024)S(1)} %convert_element_type.245) | copy-start | bytes 16384
  235.3 21.6 %copy-start.32 = (f32[1025]{0:T(1024)}, f32[1025]{0:T(1024)S(1)}, u32[]{:S(2)}) copy-start(f32[1025]{0:T(1024)S(1)} %add_multiply_fusion.2) | copy-start | bytes 12304
  238.7 2.4 collective-permute-start.4
  239.2 10.8 %slice-start = ((s8[5812224]{0:T(1024)(128)(4,1)}), s8[4194304]{0:T(1024)(128)(4,1)S(1)}, s32[]{:S(2)}) async-start(s8[5812224]{0:T(1024)(128)(4,1)} %bitcast.201), calls=%async_computation.6 | async-start | bytes 8388608
  241.1 9.0 %copy-start.18 = (bf16[1025,512]{1,0:T(8,128)(2,1)}, bf16[1025,512]{1,0:T(8,128)(2,1)S(1)}, u32[]{:S(2)}) copy-start(bf16[1025,512]{1,0:T(8,128)(2,1)S(1)} %get-tuple-element.323) | copy-start | bytes 3148804
  241.1 15.7 %copy-start.38 = (f32[1025]{0:T(1024)}, f32[1025]{0:T(1024)S(1)}, u32[]{:S(2)}) copy-start(f32[1025]{0:T(1024)S(1)} %add_rsqrt_fusion) | copy-start | bytes 12304
  241.1 8.9 %slice-start.1 = ((s8[5812224]{0:T(1024)(128)(4,1)}), s8[1617920]{0:T(1024)(128)(4,1)S(1)}, s32[]{:S(2)}) async-start(s8[5812224]{0:T(1024)(128)(4,1)} %bitcast.201), calls=%async_computation.7 | async-start | bytes 3235840
  249.4 7.4 %collective-permute-start.8 = (f32[1025]{0:T(1024)S(1)}, f32[1025]{0:T(1024)S(1)}, u32[]{:S(2)}, u32[]{:S(2)}) collective-permute-start(f32[1025]{0:T(1024)S(1)} %get-tuple-element.231), channel_id=1, source_target_pairs={{0,1},{1,0},{2,3},{3,2},{4,5},{5,4},{6,7},{7,6},{8,9},{9,8},{10,11... | collective-permute-start | bytes 12308 | tf_op jit(solution)/shard_map/ppermute | solution.py:74
  249.5 7.4 %slice-start.6 = ((s8[5812224]{0:T(1024)(128)(4,1)}), s8[4194304]{0:T(1024)(128)(4,1)S(1)}, s32[]{:S(2)}) async-start(s8[5812224]{0:T(1024)(128)(4,1)} %bitcast.216), calls=%async_computation.12 | async-start | bytes 8388608
  249.5 7.4 %slice-start.8 = ((s8[5812224]{0:T(1024)(128)(4,1)}), s8[4194304]{0:T(1024)(128)(4,1)S(1)}, s32[]{:S(2)}) async-start(s8[5812224]{0:T(1024)(128)(4,1)} %bitcast.218), calls=%async_computation.14 | async-start | bytes 8388608
  249.5 7.4 %slice-start.7 = ((s8[5812224]{0:T(1024)(128)(4,1)}), s8[1617920]{0:T(1024)(128)(4,1)S(1)}, s32[]{:S(2)}) async-start(s8[5812224]{0:T(1024)(128)(4,1)} %bitcast.216), calls=%async_computation.13 | async-start | bytes 3235840
  249.5 7.4 %slice-start.9 = ((s8[5812224]{0:T(1024)(128)(4,1)}), s8[1617920]{0:T(1024)(128)(4,1)S(1)}, s32[]{:S(2)}) async-start(s8[5812224]{0:T(1024)(128)(4,1)} %bitcast.218), calls=%async_computation.15 | async-start | bytes 3235840
  249.5 7.3 %collective-permute-start.7 = (f32[1025]{0:T(1024)S(1)}, f32[1025]{0:T(1024)S(1)}, u32[]{:S(2)}, u32[]{:S(2)}) collective-permute-start(f32[1025]{0:T(1024)S(1)} %get-tuple-element.236), channel_id=1, source_target_pairs={{0,1},{1,0},{2,3},{3,2},{4,5},{5,4},{6,7},{7,6},{8,9},{9,8},{10,11... | collective-permute-start | bytes 12308 | tf_op jit(solution)/shard_map/ppermute | solution.py:74
  278.6 16.4 %collective-permute-start.9 = (bf16[1025,1024]{1,0:T(8,128)(2,1)}, bf16[1025,1024]{1,0:T(8,128)(2,1)}, u32[]{:S(2)}, u32[]{:S(2)}) collective-permute-start(bf16[1025,1024]{1,0:T(8,128)(2,1)} %fusion.69), channel_id=1, source_target_pairs={{0,1},{1,0},{2,3},{3,2},{4,5},{5,4},{6,7},{7,6},{8,9},{9,8},{10,11... | collective-permute-start | bytes 6297608 | tf_op jit(solution)/shard_map/ppermute | solution.py:74
  295.0 14.8 %copy-start.6 = (bf16[1024,4992]{1,0:T(8,128)(2,1)}, bf16[1024,4992]{1,0:T(8,128)(2,1)S(1)}, u32[]{:S(2)}) copy-start(bf16[1024,4992]{1,0:T(8,128)(2,1)S(1)} %pad_dynamic-update-slice_fusion) | copy-start | bytes 30670852
  295.0 7.9 %copy-start.19 = (bf16[1025,512]{1,0:T(8,128)(2,1)S(1)}, bf16[1025,512]{1,0:T(8,128)(2,1)}, u32[]{:S(2)}) copy-start(bf16[1025,512]{1,0:T(8,128)(2,1)} %copy-done.18) | copy-start | bytes 3148804
  320.4 263.7 %reduce-scatter.5.cloned.1.call-start = ((), (), s32[]{:S(2)}) async-start(), calls=%async_computation.5 | async-start | bytes 3899392 | tf_op jit(solution)/shard_map/reduce_scatter | solution.py:389
  322.1 104.0 %copy-start.27 = (f32[1025,64]{0,1:T(8,128)S(1)}, f32[1025,64]{0,1:T(8,128)}, u32[]{:S(2)}) copy-start(f32[1025,64]{0,1:T(8,128)} %get-tuple-element.340) | copy-start | bytes 787204
  450.8 15.2 %collective-permute-start.10 = (bf16[1025,1024]{1,0:T(8,128)(2,1)}, bf16[1025,1024]{1,0:T(8,128)(2,1)}, u32[]{:S(2)}, u32[]{:S(2)}) collective-permute-start(bf16[1025,1024]{1,0:T(8,128)(2,1)} %fusion.68), channel_id=1, source_target_pairs={{0,1},{1,0},{2,3},{3,2},{4,5},{5,4},{6,7},{7,6},{8,9},{9,8},{10,11... | collective-permute-start | bytes 6297608 | tf_op jit(solution)/shard_map/ppermute | solution.py:74
  476.5 21.8 %copy-start.33 = (f32[1025]{0:T(1024)S(1)}, f32[1025]{0:T(1024)}, u32[]{:S(2)}) copy-start(f32[1025]{0:T(1024)} %copy-done.32) | copy-start | bytes 12304
  476.5 21.8 %copy-start.39 = (f32[1025]{0:T(1024)S(1)}, f32[1025]{0:T(1024)}, u32[]{:S(2)}) copy-start(f32[1025]{0:T(1024)} %copy-done.38) | copy-start | bytes 12304
  476.5 21.8 %copy-start.41 = (f32[1365]{0:T(1024)S(1)}, f32[1365]{0:T(1024)}, u32[]{:S(2)}) copy-start(f32[1365]{0:T(1024)} %copy-done.40) | copy-start | bytes 16384
  476.5 21.8 %copy-start.47 = (f32[1365]{0:T(1024)S(1)}, f32[1365]{0:T(1024)}, u32[]{:S(2)}) copy-start(f32[1365]{0:T(1024)} %copy-done.46) | copy-start | bytes 16384
  498.3 13.6 %slice-start.4 = ((s8[4227072]{0:T(1024)(128)(4,1)}), s8[32768]{0:T(1024)(128)(4,1)S(1)}, s32[]{:S(2)}) async-start(s8[4227072]{0:T(1024)(128)(4,1)} %bitcast.209), calls=%async_computation.10 | async-start | bytes 65536
  498.4 7.4 %copy-start.31 = (f32[1024,1]{1,0:T(8,128)S(1)}, f32[1024,1]{1,0:T(8,128)}, u32[]{:S(2)}) copy-start(f32[1024,1]{1,0:T(8,128)} %get-tuple-element.333) | copy-start | bytes 12292
  498.4 10.0 %copy-start.43 = (f32[512]{0:T(512)S(1)}, f32[512]{0:T(512)}, u32[]{:S(2)}) copy-start(f32[512]{0:T(512)} %copy-done.42) | copy-start | bytes 6148
  498.4 13.5 %slice-start.5 = ((s8[4227072]{0:T(1024)(128)(4,1)}), s8[4194304]{0:T(1024)(128)(4,1)S(1)}, s32[]{:S(2)}) async-start(s8[4227072]{0:T(1024)(128)(4,1)} %bitcast.209), calls=%async_computation.11 | async-start | bytes 8388608
  505.7 2.7 collective-permute-start.5
  (33 other events, 129.5 us)
Sparse Core Ops, SparseCore 0:
  11.4 80.3 all-gather.2
  95.0 115.5 all-gather.4
  320.5 176.5 reduce-scatter.2
  499.3 84.7 reduce-scatter.4

commit v3 on v2

--- a/solution.py
+++ b/solution.py
@@ -257,12 +257,6 @@
     down_input = (hidden_normed * inner_gain.astype(single) + inner_bias.astype(single)).astype(
         narrow
     )
-    ffn_partial = jnp.einsum("tf,df->td", down_input, down_t, preferred_element_type=single)
-    layer_out = (
-        residual_half
-        + share_columns(ffn_partial)
-        + own_half(ffn_vectors[:, 2], column, half_width)
-    ).astype(narrow)
     out_full = gather_columns(cotangent)
     out_float = out_full.astype(single)
     down_weight_grad_t = jnp.einsum(
@@ -315,7 +309,17 @@
             spread(mid_small, rows_local, row_count).astype(narrow),
         ]
     )
-    mid_pack, attn_grad_held = lax.optimization_barrier((mid_pack, attn_grad))
+    mid_pack, attn_grad_held, down_input_held = lax.optimization_barrier(
+        (mid_pack, attn_grad, down_input)
+    )
+    ffn_partial = jnp.einsum(
+        "tf,df->td", down_input_held, down_t, preferred_element_type=single
+    )
+    layer_out = (
+        residual_half
+        + share_columns(ffn_partial)
+        + own_half(ffn_vectors[:, 2], column, half_width)
+    ).astype(narrow)
     mid_sums = lax.psum_scatter(mid_pack, "row", scatter_dimension=0, tiled=True).astype(single)
     attended_grad = jnp.einsum(
         "td,de->te", attn_grad_held, proj_t, preferred_element_type=single

time: 608 us -> 605 us (level)
  no operation moved by 1% of the time
where the time goes in v3:
time: 605 us; the launch traced here: 594 us
  matrix products  213 us (35%)
  waiting for transfers between devices  186 us (31%)
  other arithmetic  98.8 us (16%)
  local copies, waits for them, and re-layouts  77.5 us (13%)
  between operations  15.4 us (3%)
    all_gather x1, waiting for transfers between devices, body(): attn_full = lax.all_gather(attn_pack, 'row', axis=0, tiled=True)  72.9 us
    reduce_scatter x1, waiting for transfers between devices, body(): lax.psum_scatter(end_pack, 'row', scatter_dimension=0, tiled=True)  66.5 us
    dot_general x8, matrix products, attend(): jnp.einsum('qk,kd->qd', weights.astype(narrow), value_block, preferred_el...  20.9 us
    reduce_scatter x1, waiting for transfers between devices, body(): lax.psum_scatter(mid_pack, 'row', scatter_dimension=0, tiled=True)  20.9 us
    dot_general x8, matrix products, attend_back(): jnp.einsum('qk,qd->kd', weights.astype(narrow), grad_block, preferred_ele...  20.3 us
    dot_general x8, matrix products, attend_back(): jnp.einsum('qk,qd->kd', score_grad, query_block, preferred_element_type=s...  20 us
    all_gather x1, waiting for transfers between devices, body(): ffn_full = lax.all_gather(ffn_pack, 'row', axis=0, tiled=True)  19 us
    dot_general x8, matrix products, attend_back(): jnp.einsum('qd,kd->qk', grad_block, value_block, preferred_element_type=s...  17.6 us
  transfers between devices with their start and end apart: 15, of which 7 were waited for; matrix products, arithmetic and copies ran while one was open for 54% of the time, Pallas kernels for 0%

profile of v3, /device:TPU:0, one launch (start us, length us, event | category | flops | bytes accessed | tf_op | source)
XLA Modules:
  0.0 593.9 jit_solution(16162372364157051919)
XLA Ops:
  18.9 72.9 %all-gather.3.cloned.1.call-done = bf16[1024,2176]{1,0:T(8,128)(2,1)} async-done(((bf16[64,2176]{1,0:T(8,128)(2,1)}), bf16[1024,2176]{1,0:T(8,128)(2,1)}) %all-gather.3.cloned.1.call-update) | async-done | bytes 4456464 | tf_op jit(solution)/shard_map/all_gather | solution.py:178
  93.9 3.8 slice.169
  97.7 4.7 copy.164
  102.4 6.1 %convolution_add_fusion.2 = f32[1025,3,512]{2,0,1:T(8,128)S(1)} fusion(bf16[1024,3,512]{0,2,1:T(8,128)(2,1)} %bitcast.223, f32[3,512]{1,0:T(4,128)S(1)} %pad_maximum_fusion.8, f32[1024]{0:T(1024)S(1)} %get-tuple-element.253, f32[1024]{0:T(1024)S(1)} %get-tuple-element.252, f32[1025]{0:T(1024)S(1)} %add_rsqrt_fusion.2, ...), kind=kOutput, calls=%fused_computation.69 | convolution fusion | flops 3235392000 | bytes 11565064 | tf_op jit(solution)/shard_map/td,dpe->tpe/dot_general | solution.py:194
  114.0 3.0 copy.168
  121.5 3.0 copy.171
  124.5 3.7 copy.172
  130.5 3.7 copy.173
  134.2 41.9 %while.24 = (s32[]{:T(128)}, bf16[8,1025,64]{1,2,0:T(8,128)(2,1)}, bf16[8,1025,64]{2,1,0:T(8,128)(2,1)S(1)}, bf16[8,1025,64]{2,1,0:T(8,128)(2,1)}, bf16[8,1025,64]{2,1,0:T(8,128)(2,1)}, /*index=5*/s32[]{:T(128)}) while((s32[]{:T(128)}, bf16[8,1025,64]{1,2,0:T(8,128)(2,1)}, bf16[8,1025,64]{2,1,0:T(8,128)(2,1)S(1)}, ...), condition=%wide.region_5.6_spmd, body=%wide.region_2.5_spmd.sunk | while | flops 276377920 | bytes 13570149 | solution.py:216
  136.8 2.6 fusion.187
  141.9 2.6 fusion.187
  147.1 2.6 fusion.187
  152.3 2.6 fusion.187
  157.4 2.7 fusion.187
  162.7 2.6 fusion.187
  167.9 2.6 fusion.187
  173.0 2.6 fusion.187
  176.1 3.8 fusion.104
  191.8 19.0 %all-gather.5.cloned.1.call-done = bf16[1024,4352]{1,0:T(8,128)(2,1)} async-done(((bf16[64,4352]{1,0:T(8,128)(2,1)}), bf16[1024,4352]{1,0:T(8,128)(2,1)}) %all-gather.5.cloned.1.call-update) | async-done | bytes 8912912 | tf_op jit(solution)/shard_map/all_gather | solution.py:234
  212.8 5.8 convolution_add_fusion.1
  218.7 12.0 %fusion.147 = (f32[1025]{0:T(1024)S(1)}, f32[1025,1365]{1,0:T(8,128)}, f32[1025,1365]{1,0:T(8,128)}) fusion(f32[1025,1365]{1,0:T(8,128)S(1)} %convolution_add_fusion.1, f32[1365]{0:T(1024)S(1)} %convert_element_type.244, bf16[1024,4352]{1,0:T(8,128)(2,1)} %all-gather.5.cloned.1.call-done, f32[1024]{0:T(1024)S(1)} %get-tuple-element.255, ...), kind=kOutput, calls=%fused_computation.270 | convolution fusion | flops 2884646912 | bytes 21798236 | tf_op jit(solution)/shard_map/dot_general | solution.py:247
  232.4 3.1 copy.182
  235.5 3.4 multiply_reduce_fusion.3
  241.2 8.6 %multiply_reduce_fusion.1 = (bf16[1365]{0:T(1024)(128)(2,1)S(1)}, f32[1025]{0:T(1024)S(1)}, f32[1025]{0:T(1024)S(1)}, bf16[1365]{0:T(1024)(128)(2,1)S(1)}, bf16[...) fusion(f32[1025,1365]{1,0:T(8,128)} %get-tuple-element.293, f32[1025]{0:T(1024)S(1)} %add_rsqrt_fusion, ...), kind=kOutput, calls=%fused_computation.60 | convolution fusion | flops 2886390272 | bytes 19222538 | tf_op jit(solution)/shard_map/td,df->tf/dot_general | solution.py:266
  250.4 5.7 convolution_convert_fusion
  257.8 6.5 %fusion.143 = (bf16[1365]{0:T(1024)(128)(2,1)S(1)}, bf16[1025,1365]{1,0:T(8,128)(2,1)S(1)}, bf16[1365]{0:T(1024)(128)(2,1)S(1)}, bf16[1025,1365]{1,0:T(8,128)(2,1)S(1)}) fusion(f32[1025,1365]{1,0:T(8,128)S(1)} %bitcast.219, f32[1025]{0:T(1024)S(1)} %add_multiply_fusion, f32[1025,1365]{1,0:T(8,128)S(1)} %bitcast.204, f32[1025]{0:T(1024)S(1)} %add_multiply_fusion.2, ...), kind=kLoop, calls=%fused_computation.267 | loop fusion | flops 30778012 | bytes 28009820 | tf_op jit(solution)/shard_map/reduce_sum | solution.py:281
  264.4 6.3 %fusion.83 = f32[1025,1024]{1,0:T(8,128)S(1)} fusion(bf16[1025,1365]{1,0:T(8,128)(2,1)S(1)} %get-tuple-element.301, bf16[1024,4352]{1,0:T(8,128)(2,1)} %all-gather.5.cloned.1.call-done), kind=kOutput, calls=%fused_computation.123 | convolution fusion | flops 2865408000 | bytes 9880234 | tf_op jit(solution)/shard_map/tf,df->td/dot_general | solution.py:287
  270.7 7.0 %fusion.69 = bf16[1025,1024]{1,0:T(8,128)(2,1)} fusion(f32[1025,1024]{1,0:T(8,128)S(1)} %fusion.83, bf16[1025,1365]{1,0:T(8,128)(2,1)S(1)} %get-tuple-element.286, bf16[1024,4352]{1,0:T(8,128)(2,1)} %all-gather.5.cloned.1.call-done), kind=kOutput, calls=%fused_computation.101 | convolution fusion | flops 2867507200 | bytes 11979434 | tf_op jit(solution)/shard_map/tf,df->td/dot_general | solution.py:288
  277.7 6.1 %convolution_convert_fusion.2 = bf16[1024,1365]{1,0:T(8,128)(2,1)} fusion(bf16[1025,1365]{1,0:T(8,128)(2,1)S(1)} %get-tuple-element.301, f32[1024]{0:T(1024)S(1)} %get-tuple-element.255, f32[1024]{0:T(1024)S(1)} %get-tuple-element.254, f32[1025]{0:T(1024)S(1)} %add_rsqrt_fusion.1, f32[1025]{0:T(1024)S(1)} %broadcast_multiply_fusion.6, ...), kind=kOutput, calls=%fused_computation.104 | convolution fusion | flops 2876252160 | bytes 7709362 | tf_op jit(solution)/shard_map/td,tf->df/dot_general | solution.py:282
  286.8 4.9 convolution_convert_fusion.1
  294.0 7.2 %fusion.65 = (bf16[1024]{0:T(1024)(128)(2,1)S(1)}, f32[1025]{0:T(1024)S(1)}, f32[1025]{0:T(1024)S(1)}, bf16[1024]{0:T(1024)(128)(2,1)S(1)}) fusion(bf16[1025,1024]{1,0:T(8,128)(2,1)} %collective-permute-done.8, bf16[1025,1024]{1,0:T(8,128)(2,1)} %fusion.69, f32[1025]{0:T(1024)S(1)} %add_rsqrt_fusion.1, f32[1025]{0:T(1024)S(1)} %broadcast_multiply_fusion.6, ...), kind=kLoop, calls=%fused_computation.92 | loop fusion | flops 16789502 | bytes 6322192 | tf_op jit(solution)/shard_map/reduce_sum | solution.py:34
  301.2 6.9 %fusion.145 = (bf16[1024]{0:T(1024)(128)(2,1)S(1)}, bf16[1025,1024]{1,0:T(8,128)(2,1)}, f32[1025,1024]{1,0:T(8,128)}, bf16[1024]{0:T(1024)(128)(2,1)S(1)}) fusion(f32[1025]{0:T(1024)S(1)} %broadcast_multiply_fusion.4, f32[1025]{0:T(1024)S(1)} %broadcast_multiply_fusion.6, bf16[1025,512]{1,0:T(8,128)(2,1)S(1)} %get-tuple-element.328, ...), kind=kLoop, calls=%fused_computation.269 | loop fusion | flops 24138752 | bytes 14718992 | tf_op jit(solution)/shard_map/reduce_sum | solution.py:295
  308.5 4.7 fusion.94
  320.3 101.0 %while.25 = (s32[]{:T(128)}, f32[8,1025,64]{1,2,0:T(8,128)S(1)}, f32[8,1025,64]{1,2,0:T(8,128)}, bf16[8,1025,64]{1,2,0:T(8,128)(2,1)}, bf16[8,1025,64]{2,1,0:T(8...) while((s32[]{:T(128)}, f32[8,1025,64]{1,2,0:T(8,128)S(1)}, ...), condition=%wide.region_26.27_spmd, body=%wide.region_22.26_spmd.sunk | while | flops 689338112 | bytes 38548648 | solution.py:352
  348.3 2.5 fusion.198
  421.4 4.3 bitcast_multiply_fusion.1
  431.8 3.2 copy.181
  438.9 5.0 add_convert_fusion.3
  444.0 4.9 fusion.68
  449.4 6.4 %convolution_convert_fusion.4 = bf16[1024,3,512]{0,2,1:T(8,128)(2,1)} fusion(f32[1024]{0:T(1024)S(1)} %copy-done.41, f32[1024]{0:T(1024)S(1)} %copy-done.39, bf16[1025,1,512]{2,0,1:T(8,128)(2,1)S(1)} %copy-done.20, bf16[1025,1,512]{2,0,1:T(8,128)(2,1)S(1)} %get-tuple-element.323, bf16[1025,1,512]{2,0,1:T(8,128)(2,1)S(1)} %get-tuple-element.322, ...), kind=kOutput, calls=%fused_computation.136 | convolution fusion | flops 3244836864 | bytes 8410120 | tf_op jit(solution)/shard_map/td,tpe->dpe/dot_general | solution.py:373
  455.8 4.7 copy.189
  463.1 6.7 %fusion.141 = (f32[1025]{0:T(1024)S(1)}, f32[1025]{0:T(1024)S(1)}, bf16[1024]{0:T(1024)(128)(2,1)S(1)}, bf16[1024]{0:T(1024)(128)(2,1)S(1)}, f32[1025,1024]{1,0:T(8,128)}, /*index=5*/f32[1025,1024]{1,0:T(8,128)}) fusion(f32[1025]{0:T(1024)S(1)} %copy-done.35, f32[1025]{0:T(1024)S(1)} %copy-done.33, bf16[1025,512]{1,0:T(8,128)(2,1)S(1)} %copy-done.5, ...), kind=kLoop, calls=%fused_computation.266 | loop fusion | flops 16789502 | bytes 14718992 | tf_op jit(solution)/shard_map/reduce_sum | solution.py:31
  470.1 3.6 fusion.75
  473.7 20.9 %reduce-scatter.3.cloned.1.call-done = bf16[64,4992]{1,0:T(8,128)(2,1)} async-done(((bf16[1024,4992]{1,0:T(8,128)(2,1)}), bf16[64,4992]{1,0:T(8,128)(2,1)}) %reduce-scatter.3.cloned.1.call-update) | async-done | bytes 638992 | tf_op jit(solution)/shard_map/reduce_scatter | solution.py:323
  495.8 6.3 %fusion.77 = f32[1025,1024]{1,0:T(8,128)S(1)} fusion(bf16[1025,1365]{1,0:T(8,128)(2,1)} %copy-done.48, bf16[1024,4352]{1,0:T(8,128)(2,1)} %all-gather.5.cloned.1.call-done), kind=kOutput, calls=%fused_computation.117 | convolution fusion | flops 2865408000 | bytes 9988096 | tf_op jit(solution)/shard_map/tf,df->td/dot_general | solution.py:315
  505.1 3.5 add_convert_fusion.4
  508.6 3.1 fusion.91
  515.0 66.5 %reduce-scatter.5.cloned.1.call-done = bf16[64,1792]{1,0:T(8,128)(2,1)} async-done(((bf16[1024,1792]{1,0:T(8,128)(2,1)}), bf16[64,1792]{1,0:T(8,128)(2,1)}) %reduce-scatter.5.cloned.1.call-update) | async-done | bytes 229392 | tf_op jit(solution)/shard_map/reduce_scatter | solution.py:393
  (331 shorter events, 203.2 us)
Async XLA Ops:
  7.2 9.2 %copy-start.7 = (bf16[1025,512]{1,0:T(8,128)(2,1)S(1)}, bf16[1025,512]{1,0:T(8,128)(2,1)}, u32[]{:S(2)}) copy-start(bf16[1025,512]{1,0:T(8,128)(2,1)} %param.23) | copy-start | bytes 3148804
  7.2 7.0 %copy-start.46 = (bf16[512]{0:T(512)(128)(2,1)S(1)}, bf16[512]{0:T(512)(128)(2,1)}, u32[]{:S(2)}) copy-start(bf16[512]{0:T(512)(128)(2,1)} %param.27) | copy-start | bytes 3076
  7.2 7.0 %copy-start.47 = (bf16[512]{0:T(512)(128)(2,1)S(1)}, bf16[512]{0:T(512)(128)(2,1)}, u32[]{:S(2)}) copy-start(bf16[512]{0:T(512)(128)(2,1)} %param.28) | copy-start | bytes 3076
  7.2 84.5 %all-gather.3.cloned.1.call-start = ((), (), s32[]{:S(2)}) async-start(), calls=%async_computation.2 | async-start | bytes 4734976 | tf_op jit(solution)/shard_map/all_gather | solution.py:178
  10.7 200.0 %all-gather.5.cloned.1.call-start = ((), (), s32[]{:S(2)}) async-start(), calls=%async_computation.3 | async-start | bytes 9469952 | tf_op jit(solution)/shard_map/all_gather | solution.py:234
  10.7 5.6 collective-permute-start
  14.1 480.5 %reduce-scatter.3.cloned.1.call-start = ((), (), s32[]{:S(2)}) async-start(), calls=%async_computation.4 | async-start | bytes 10862592 | tf_op jit(solution)/shard_map/reduce_scatter | solution.py:323
  17.7 84.6 %copy-start.2 = (bf16[1025,512]{1,0:T(8,128)(2,1)}, bf16[1025,512]{1,0:T(8,128)(2,1)S(1)}, u32[]{:S(2)}) copy-start(bf16[1025,512]{1,0:T(8,128)(2,1)S(1)} %get-tuple-element.329) | copy-start | bytes 3148804
  17.7 84.6 %copy-start.4 = (bf16[1025,512]{1,0:T(8,128)(2,1)}, bf16[1025,512]{1,0:T(8,128)(2,1)S(1)}, u32[]{:S(2)}) copy-start(bf16[1025,512]{1,0:T(8,128)(2,1)S(1)} %get-tuple-element.330) | copy-start | bytes 3148804
  18.1 84.2 %copy-start.32 = (f32[1025]{0:T(1024)}, f32[1025]{0:T(1024)S(1)}, u32[]{:S(2)}) copy-start(f32[1025]{0:T(1024)S(1)} %broadcast_multiply_fusion.7) | copy-start | bytes 12304
  18.9 83.5 %copy-start.34 = (f32[1025]{0:T(1024)}, f32[1025]{0:T(1024)S(1)}, u32[]{:S(2)}) copy-start(f32[1025]{0:T(1024)S(1)} %add_rsqrt_fusion.2) | copy-start | bytes 12304
  93.9 8.5 %copy-start.38 = (f32[1024]{0:T(1024)}, f32[1024]{0:T(1024)S(1)}, u32[]{:S(2)}) copy-start(f32[1024]{0:T(1024)S(1)} %get-tuple-element.252) | copy-start | bytes 12292
  93.9 8.5 %copy-start.40 = (f32[1024]{0:T(1024)}, f32[1024]{0:T(1024)S(1)}, u32[]{:S(2)}) copy-start(f32[1024]{0:T(1024)S(1)} %get-tuple-element.253) | copy-start | bytes 12292
  182.3 5.9 copy-start.42
  182.3 5.9 copy-start.43
  182.3 2.9 collective-permute-start.1
  187.6 2.7 collective-permute-start.2
  187.8 51.6 %collective-permute-start.5 = (bf16[1025,512]{1,0:T(8,128)(2,1)}, bf16[1025,512]{1,0:T(8,128)(2,1)}, u32[]{:S(2)}, u32[]{:S(2)}) collective-permute-start(bf16[1025,512]{1,0:T(8,128)(2,1)} %param.41), channel_id=1, source_target_pairs={{0,1},{1,0},{2,3},{3,2},{4,5},{5,4},{6,7},{7,6},{8,9},{9,8},{10,11... | collective-permute-start | bytes 3148808 | tf_op jit(solution)/shard_map/ppermute | solution.py:74
  218.7 12.0 %copy-start.14 = (f32[1025,1365]{1,0:T(8,128)}, f32[1025,1365]{1,0:T(8,128)S(1)}, u32[]{:S(2)}) copy-start(f32[1025,1365]{1,0:T(8,128)S(1)} %convolution_add_fusion.1) | copy-start | bytes 16789504
  218.7 12.1 %copy-start.44 = (bf16[1365]{0:T(1024)(128)(2,1)S(1)}, bf16[1365]{0:T(1024)(128)(2,1)}, u32[]{:S(2)}) copy-start(bf16[1365]{0:T(1024)(128)(2,1)} %param.37) | copy-start | bytes 8194
  218.7 12.1 %copy-start.45 = (bf16[1365]{0:T(1024)(128)(2,1)S(1)}, bf16[1365]{0:T(1024)(128)(2,1)}, u32[]{:S(2)}) copy-start(bf16[1365]{0:T(1024)(128)(2,1)} %param.38) | copy-start | bytes 8194
  218.7 12.1 %copy-start.28 = (f32[1025,64]{0,1:T(8,128)S(1)}, f32[1025,64]{0,1:T(8,128)}, u32[]{:S(2)}) copy-start(f32[1025,64]{0,1:T(8,128)} %get-tuple-element.342) | copy-start | bytes 787204
  230.7 4.8 collective-permute-start.3
  238.9 2.2 collective-permute-start.4
  241.1 9.2 %copy-start.18 = (bf16[1025,512]{1,0:T(8,128)(2,1)}, bf16[1025,512]{1,0:T(8,128)(2,1)S(1)}, u32[]{:S(2)}) copy-start(bf16[1025,512]{1,0:T(8,128)(2,1)S(1)} %get-tuple-element.326) | copy-start | bytes 3148804
  249.8 6.4 %copy-start.48 = (bf16[1025,1365]{1,0:T(8,128)(2,1)}, bf16[1025,1365]{1,0:T(8,128)(2,1)S(1)}, u32[]{:S(2)}) copy-start(bf16[1025,1365]{1,0:T(8,128)(2,1)S(1)} %get-tuple-element.96) | copy-start | bytes 8394754
  249.8 6.4 %collective-permute-start.6 = (f32[1025]{0:T(1024)S(1)}, f32[1025]{0:T(1024)S(1)}, u32[]{:S(2)}, u32[]{:S(2)}) collective-permute-start(f32[1025]{0:T(1024)S(1)} %get-tuple-element.238), channel_id=1, source_target_pairs={{0,1},{1,0},{2,3},{3,2},{4,5},{5,4},{6,7},{7,6},{8,9},{9,8},{10,11... | collective-permute-start | bytes 12308 | tf_op jit(solution)/shard_map/ppermute | solution.py:74
  249.9 6.3 %collective-permute-start.7 = (f32[1025]{0:T(1024)S(1)}, f32[1025]{0:T(1024)S(1)}, u32[]{:S(2)}, u32[]{:S(2)}) collective-permute-start(f32[1025]{0:T(1024)S(1)} %get-tuple-element.233), channel_id=1, source_target_pairs={{0,1},{1,0},{2,3},{3,2},{4,5},{5,4},{6,7},{7,6},{8,9},{9,8},{10,11... | collective-permute-start | bytes 12308 | tf_op jit(solution)/shard_map/ppermute | solution.py:74
  250.4 5.8 slice-start.6
  250.4 5.8 slice-start.8
  250.4 6.5 %slice-start.1 = ((s8[5812224]{0:T(1024)(128)(4,1)}), s8[1617920]{0:T(1024)(128)(4,1)S(1)}, s32[]{:S(2)}) async-start(s8[5812224]{0:T(1024)(128)(4,1)} %bitcast.203), calls=%async_computation.7 | async-start | bytes 3235840
  250.4 7.0 %slice-start.7 = ((s8[5812224]{0:T(1024)(128)(4,1)}), s8[1617920]{0:T(1024)(128)(4,1)S(1)}, s32[]{:S(2)}) async-start(s8[5812224]{0:T(1024)(128)(4,1)} %bitcast.218), calls=%async_computation.13 | async-start | bytes 3235840
  250.4 7.4 %slice-start.9 = ((s8[5812224]{0:T(1024)(128)(4,1)}), s8[1617920]{0:T(1024)(128)(4,1)S(1)}, s32[]{:S(2)}) async-start(s8[5812224]{0:T(1024)(128)(4,1)} %bitcast.220), calls=%async_computation.15 | async-start | bytes 3235840
  264.4 6.4 %copy-start.22 = (bf16[1025,1365]{1,0:T(8,128)(2,1)}, bf16[1025,1365]{1,0:T(8,128)(2,1)S(1)}, u32[]{:S(2)}) copy-start(bf16[1025,1365]{1,0:T(8,128)(2,1)S(1)} %get-tuple-element.286) | copy-start | bytes 8394754
  277.7 16.3 %collective-permute-start.8 = (bf16[1025,1024]{1,0:T(8,128)(2,1)}, bf16[1025,1024]{1,0:T(8,128)(2,1)}, u32[]{:S(2)}, u32[]{:S(2)}) collective-permute-start(bf16[1025,1024]{1,0:T(8,128)(2,1)} %fusion.69), channel_id=1, source_target_pairs={{0,1},{1,0},{2,3},{3,2},{4,5},{5,4},{6,7},{7,6},{8,9},{9,8},{10,11... | collective-permute-start | bytes 6297608 | tf_op jit(solution)/shard_map/ppermute | solution.py:74
  294.0 14.2 %copy-start.6 = (bf16[1024,4992]{1,0:T(8,128)(2,1)}, bf16[1024,4992]{1,0:T(8,128)(2,1)S(1)}, u32[]{:S(2)}) copy-start(bf16[1024,4992]{1,0:T(8,128)(2,1)S(1)} %pad_dynamic-update-slice_fusion) | copy-start | bytes 30670852
  294.0 7.3 %copy-start.19 = (bf16[1025,512]{1,0:T(8,128)(2,1)S(1)}, bf16[1025,512]{1,0:T(8,128)(2,1)}, u32[]{:S(2)}) copy-start(bf16[1025,512]{1,0:T(8,128)(2,1)} %copy-done.18) | copy-start | bytes 3148804
  308.5 6.3 %copy-start.29 = (bf16[1025,1024]{1,0:T(8,128)(2,1)S(1)}, bf16[1025,1024]{1,0:T(8,128)(2,1)}, u32[]{:S(2)}) copy-start(bf16[1025,1024]{1,0:T(8,128)(2,1)} %get-tuple-element.97) | copy-start | bytes 6297604
  318.7 262.8 %reduce-scatter.5.cloned.1.call-start = ((), (), s32[]{:S(2)}) async-start(), calls=%async_computation.5 | async-start | bytes 3899392 | tf_op jit(solution)/shard_map/reduce_scatter | solution.py:393
  320.3 101.1 %copy-start.26 = (f32[1025,64]{0,1:T(8,128)S(1)}, f32[1025,64]{0,1:T(8,128)}, u32[]{:S(2)}) copy-start(f32[1025,64]{0,1:T(8,128)} %get-tuple-element.343) | copy-start | bytes 787204
  448.9 14.2 %collective-permute-start.10 = (bf16[1025,1024]{1,0:T(8,128)(2,1)}, bf16[1025,1024]{1,0:T(8,128)(2,1)}, u32[]{:S(2)}, u32[]{:S(2)}) collective-permute-start(bf16[1025,1024]{1,0:T(8,128)(2,1)} %fusion.68), channel_id=1, source_target_pairs={{0,1},{1,0},{2,3},{3,2},{4,5},{5,4},{6,7},{7,6},{8,9},{9,8},{10,11... | collective-permute-start | bytes 6297608 | tf_op jit(solution)/shard_map/ppermute | solution.py:74
  495.7 12.8 %slice-start.4 = ((s8[4227072]{0:T(1024)(128)(4,1)}), s8[32768]{0:T(1024)(128)(4,1)S(1)}, s32[]{:S(2)}) async-start(s8[4227072]{0:T(1024)(128)(4,1)} %bitcast.211), calls=%async_computation.10 | async-start | bytes 65536
  495.8 6.6 %copy-start.31 = (f32[1024,1]{1,0:T(8,128)S(1)}, f32[1024,1]{1,0:T(8,128)}, u32[]{:S(2)}) copy-start(f32[1024,1]{1,0:T(8,128)} %get-tuple-element.336) | copy-start | bytes 12292
  495.8 9.3 %copy-start.37 = (f32[512]{0:T(512)S(1)}, f32[512]{0:T(512)}, u32[]{:S(2)}) copy-start(f32[512]{0:T(512)} %copy-done.36) | copy-start | bytes 6148
  495.8 12.8 %slice-start.5 = ((s8[4227072]{0:T(1024)(128)(4,1)}), s8[4194304]{0:T(1024)(128)(4,1)S(1)}, s32[]{:S(2)}) async-start(s8[4227072]{0:T(1024)(128)(4,1)} %bitcast.211), calls=%async_computation.11 | async-start | bytes 8388608
  502.3 2.7 collective-permute-start.9
  502.4 6.2 %slice-start.2 = ((s8[4227072]{0:T(1024)(128)(4,1)}), s8[4194304]{0:T(1024)(128)(4,1)S(1)}, s32[]{:S(2)}) async-start(s8[4227072]{0:T(1024)(128)(4,1)} %bitcast.209), calls=%async_computation.8 | async-start | bytes 8388608
  502.6 6.0 %slice-start.3 = ((s8[4227072]{0:T(1024)(128)(4,1)}), s8[32768]{0:T(1024)(128)(4,1)S(1)}, s32[]{:S(2)}) async-start(s8[4227072]{0:T(1024)(128)(4,1)} %bitcast.209), calls=%async_computation.9 | async-start | bytes 65536
  (26 other events, 98.9 us)
Sparse Core Ops, SparseCore 0:
  11.4 80.3 all-gather.2
  95.0 115.6 all-gather.4
  318.8 175.7 reduce-scatter.2
  496.7 84.7 reduce-scatter.4

commit v4 on v3

--- a/solution.py
+++ b/solution.py
@@ -172,7 +172,9 @@
         [
             qkv_weight.reshape(rows_local, 3 * half_width),
             proj_weight.T,
-            jnp.stack([norm1_gain, norm1_bias, proj_bias], axis=1),
+            jnp.stack(
+                [norm1_gain, norm1_bias, proj_bias, norm2_gain, norm2_bias, down_bias], axis=1
+            ),
         ]
     )
     attn_full = lax.all_gather(attn_pack, "row", axis=0, tiled=True)
@@ -180,7 +182,8 @@
         model_width, 3, half_width
     )
     proj_t = attn_full[:, attn_at[1] : attn_at[1] + half_width]
-    attn_vectors = attn_full[:, attn_at[2] : attn_at[2] + 3].astype(single)
+    attn_vectors = attn_full[:, attn_at[2] : attn_at[2] + 6].astype(single)
+    ffn_vectors = attn_vectors[:, 3:]
 
     whole_input = gather_columns(tokens).astype(single)
     normed_out, normed_one, inv_std_one = norm_forward(
@@ -228,14 +231,12 @@
             gate_weight,
             up_weight,
             down_weight.T,
-            jnp.stack([norm2_gain, norm2_bias, down_bias], axis=1),
         ]
     )
     ffn_full = lax.all_gather(ffn_pack, "row", axis=0, tiled=True)
     gate_full = ffn_full[:, ffn_at[0] : ffn_at[0] + ff_local]
     up_full = ffn_full[:, ffn_at[1] : ffn_at[1] + ff_local]
     down_t = ffn_full[:, ffn_at[2] : ffn_at[2] + ff_local]
-    ffn_vectors = ffn_full[:, ffn_at[3] : ffn_at[3] + 3].astype(single)
 
     second_out, normed_two, inv_std_two = norm_forward(
         residual_full, ffn_vectors[:, 0], ffn_vectors[:, 1]

time: 605 us -> 602 us (level)
    unnamed x124 -> x127, local copies, waits for them, and re-layouts: 11.4 us -> 12.3 us
where the time goes in v4:
time: 602 us; the launch traced here: 590 us
  matrix products  213 us (35%)
  waiting for transfers between devices  183 us (30%)
  other arithmetic  96.5 us (16%)
  local copies, waits for them, and re-layouts  78.8 us (13%)
  between operations  15.4 us (3%)
    all_gather x1, waiting for transfers between devices, body(): attn_full = lax.all_gather(attn_pack, 'row', axis=0, tiled=True)  73.6 us
    reduce_scatter x1, waiting for transfers between devices, body(): lax.psum_scatter(end_pack, 'row', scatter_dimension=0, tiled=True)  66.9 us
    reduce_scatter x1, waiting for transfers between devices, body(): lax.psum_scatter(mid_pack, 'row', scatter_dimension=0, tiled=True)  21.2 us
    dot_general x8, matrix products, attend(): jnp.einsum('qk,kd->qd', weights.astype(narrow), value_block, preferred_el...  20.8 us
    dot_general x8, matrix products, attend_back(): jnp.einsum('qk,qd->kd', weights.astype(narrow), grad_block, preferred_ele...  20.3 us
    dot_general x8, matrix products, attend_back(): jnp.einsum('qk,qd->kd', score_grad, query_block, preferred_element_type=s...  20 us
    dot_general x8, matrix products, attend_back(): jnp.einsum('qd,kd->qk', grad_block, value_block, preferred_element_type=s...  17.6 us
    dot_general x8, matrix products, attend_back(): jnp.einsum('qd,kd->qk', query_block, key_block, preferred_element_type=si...  15.6 us
  transfers between devices with their start and end apart: 15, of which 7 were waited for; matrix products, arithmetic and copies ran while one was open for 54% of the time, Pallas kernels for 0%

profile of v4, /device:TPU:0, one launch (start us, length us, event | category | flops | bytes accessed | tf_op | source)
XLA Modules:
  0.0 590.2 jit_solution(15684426046268974)
XLA Ops:
  18.1 73.6 %all-gather.3.cloned.1.call-done = bf16[1024,2176]{1,0:T(8,128)(2,1)} async-done(((bf16[64,2176]{1,0:T(8,128)(2,1)}), bf16[1024,2176]{1,0:T(8,128)(2,1)}) %all-gather.3.cloned.1.call-update) | async-done | bytes 4456464 | tf_op jit(solution)/shard_map/all_gather | solution.py:180
  96.6 4.7 copy.166
  101.3 6.1 %convolution_add_fusion.2 = f32[1025,3,512]{2,0,1:T(8,128)S(1)} fusion(bf16[1024,3,512]{0,2,1:T(8,128)(2,1)} %bitcast.223, f32[3,512]{1,0:T(4,128)S(1)} %pad_maximum_fusion.8, f32[1024]{0:T(1024)S(1)} %get-tuple-element.338, f32[1024]{0:T(1024)S(1)} %get-tuple-element.341, f32[1025]{0:T(1024)S(1)} %add_rsqrt_fusion.2, ...), kind=kOutput, calls=%fused_computation.69 | convolution fusion | flops 3235392000 | bytes 11565064 | tf_op jit(solution)/shard_map/td,dpe->tpe/dot_general | solution.py:197
  107.4 2.8 fusion.147
  113.5 3.1 copy.170
  118.7 2.7 slice.224
  123.3 2.9 copy.173
  126.2 3.7 copy.174
  132.3 3.7 copy.175
  135.9 41.9 %while.24 = (s32[]{:T(128)}, bf16[8,1025,64]{1,2,0:T(8,128)(2,1)}, bf16[8,1025,64]{2,1,0:T(8,128)(2,1)S(1)}, bf16[8,1025,64]{2,1,0:T(8,128)(2,1)}, bf16[8,1025,64]{2,1,0:T(8,128)(2,1)}, /*index=5*/s32[]{:T(128)}) while((s32[]{:T(128)}, bf16[8,1025,64]{1,2,0:T(8,128)(2,1)}, bf16[8,1025,64]{2,1,0:T(8,128)(2,1)S(1)}, ...), condition=%wide.region_5.6_spmd, body=%wide.region_2.5_spmd.sunk | while | flops 276377920 | bytes 13570149 | solution.py:219
  138.5 2.6 fusion.185
  143.7 2.6 fusion.185
  148.9 2.6 fusion.185
  154.1 2.6 fusion.185
  159.3 2.6 fusion.185
  164.5 2.6 fusion.185
  169.7 2.6 fusion.185
  174.8 2.6 fusion.185
  177.9 3.8 fusion.102
  193.6 15.0 %all-gather.5.cloned.1.call-done = bf16[1024,4224]{1,0:T(8,128)(2,1)} async-done(((bf16[64,4224]{1,0:T(8,128)(2,1)}), bf16[1024,4224]{1,0:T(8,128)(2,1)}) %all-gather.5.cloned.1.call-update) | async-done | bytes 8650768 | tf_op jit(solution)/shard_map/all_gather | solution.py:236
  208.5 5.8 convolution_add_fusion.1
  214.4 11.9 %fusion.144 = (f32[1025]{0:T(1024)S(1)}, f32[1025,1365]{1,0:T(8,128)}, f32[1025,1365]{1,0:T(8,128)}) fusion(f32[1025,1365]{1,0:T(8,128)S(1)} %convolution_add_fusion.1, f32[1365]{0:T(1024)S(1)} %convert_element_type.239, bf16[1024,4224]{1,0:T(8,128)(2,1)} %all-gather.5.cloned.1.call-done, f32[1024]{0:T(1024)S(1)} %get-tuple-element.340, ...), kind=kOutput, calls=%fused_computation.262 | convolution fusion | flops 2884646912 | bytes 21798236 | tf_op jit(solution)/shard_map/dot_general | solution.py:248
  228.0 3.1 copy.183
  231.2 3.4 multiply_reduce_fusion.3
  236.8 8.6 %multiply_reduce_fusion.1 = (bf16[1365]{0:T(1024)(128)(2,1)S(1)}, f32[1025]{0:T(1024)S(1)}, f32[1025]{0:T(1024)S(1)}, bf16[1365]{0:T(1024)(128)(2,1)S(1)}, bf16[...) fusion(f32[1025,1365]{1,0:T(8,128)} %get-tuple-element.293, f32[1025]{0:T(1024)S(1)} %add_rsqrt_fusion, ...), kind=kOutput, calls=%fused_computation.60 | convolution fusion | flops 2886390272 | bytes 19222538 | tf_op jit(solution)/shard_map/td,df->tf/dot_general | solution.py:267
  246.0 5.7 convolution_convert_fusion
  253.5 6.5 %fusion.140 = (bf16[1365]{0:T(1024)(128)(2,1)S(1)}, bf16[1025,1365]{1,0:T(8,128)(2,1)S(1)}, bf16[1365]{0:T(1024)(128)(2,1)S(1)}, bf16[1025,1365]{1,0:T(8,128)(2,1)S(1)}) fusion(f32[1025,1365]{1,0:T(8,128)S(1)} %bitcast.219, f32[1025]{0:T(1024)S(1)} %add_multiply_fusion, f32[1025,1365]{1,0:T(8,128)S(1)} %bitcast.204, f32[1025]{0:T(1024)S(1)} %add_multiply_fusion.2, ...), kind=kLoop, calls=%fused_computation.259 | loop fusion | flops 30778012 | bytes 28009820 | tf_op jit(solution)/shard_map/reduce_sum | solution.py:282
  260.0 6.3 %fusion.83 = f32[1025,1024]{1,0:T(8,128)S(1)} fusion(bf16[1025,1365]{1,0:T(8,128)(2,1)S(1)} %get-tuple-element.301, bf16[1024,4224]{1,0:T(8,128)(2,1)} %all-gather.5.cloned.1.call-done), kind=kOutput, calls=%fused_computation.123 | convolution fusion | flops 2865408000 | bytes 9880234 | tf_op jit(solution)/shard_map/tf,df->td/dot_general | solution.py:288
  266.4 7.0 %fusion.69 = bf16[1025,1024]{1,0:T(8,128)(2,1)} fusion(f32[1025,1024]{1,0:T(8,128)S(1)} %fusion.83, bf16[1025,1365]{1,0:T(8,128)(2,1)S(1)} %get-tuple-element.286, bf16[1024,4224]{1,0:T(8,128)(2,1)} %all-gather.5.cloned.1.call-done), kind=kOutput, calls=%fused_computation.101 | convolution fusion | flops 2867507200 | bytes 11979434 | tf_op jit(solution)/shard_map/tf,df->td/dot_general | solution.py:289
  273.3 6.1 %convolution_convert_fusion.2 = bf16[1024,1365]{1,0:T(8,128)(2,1)} fusion(bf16[1025,1365]{1,0:T(8,128)(2,1)S(1)} %get-tuple-element.301, f32[1024]{0:T(1024)S(1)} %get-tuple-element.340, f32[1024]{0:T(1024)S(1)} %get-tuple-element.339, f32[1025]{0:T(1024)S(1)} %add_rsqrt_fusion.1, f32[1025]{0:T(1024)S(1)} %broadcast_multiply_fusion.6, ...), kind=kOutput, calls=%fused_computation.104 | convolution fusion | flops 2876252160 | bytes 7709362 | tf_op jit(solution)/shard_map/td,tf->df/dot_general | solution.py:283
  282.3 4.9 convolution_convert_fusion.1
  289.6 7.2 %fusion.65 = (bf16[1024]{0:T(1024)(128)(2,1)S(1)}, f32[1025]{0:T(1024)S(1)}, f32[1025]{0:T(1024)S(1)}, bf16[1024]{0:T(1024)(128)(2,1)S(1)}) fusion(bf16[1025,1024]{1,0:T(8,128)(2,1)} %collective-permute-done.8, bf16[1025,1024]{1,0:T(8,128)(2,1)} %fusion.69, f32[1025]{0:T(1024)S(1)} %add_rsqrt_fusion.1, f32[1025]{0:T(1024)S(1)} %broadcast_multiply_fusion.6, ...), kind=kLoop, calls=%fused_computation.92 | loop fusion | flops 16789502 | bytes 6322192 | tf_op jit(solution)/shard_map/reduce_sum | solution.py:34
  296.8 6.9 %fusion.142 = (bf16[1024]{0:T(1024)(128)(2,1)S(1)}, bf16[1025,1024]{1,0:T(8,128)(2,1)}, f32[1025,1024]{1,0:T(8,128)}, bf16[1024]{0:T(1024)(128)(2,1)S(1)}) fusion(f32[1025]{0:T(1024)S(1)} %broadcast_multiply_fusion.4, f32[1025]{0:T(1024)S(1)} %broadcast_multiply_fusion.6, bf16[1025,512]{1,0:T(8,128)(2,1)S(1)} %get-tuple-element.328, ...), kind=kLoop, calls=%fused_computation.261 | loop fusion | flops 24138752 | bytes 14718992 | tf_op jit(solution)/shard_map/reduce_sum | solution.py:296
  304.0 4.7 fusion.94
  315.9 101.0 %while.25 = (s32[]{:T(128)}, f32[8,1025,64]{1,2,0:T(8,128)S(1)}, f32[8,1025,64]{1,2,0:T(8,128)}, bf16[8,1025,64]{1,2,0:T(8,128)(2,1)}, bf16[8,1025,64]{2,1,0:T(8...) while((s32[]{:T(128)}, f32[8,1025,64]{1,2,0:T(8,128)S(1)}, ...), condition=%wide.region_26.27_spmd, body=%wide.region_22.26_spmd.sunk | while | flops 689338112 | bytes 38548648 | solution.py:353
  416.9 4.3 bitcast_multiply_fusion.1
  427.3 3.2 copy.182
  434.4 5.0 add_convert_fusion.3
  439.5 5.0 fusion.68
  445.0 6.4 %convolution_convert_fusion.4 = bf16[1024,3,512]{0,2,1:T(8,128)(2,1)} fusion(f32[1024]{0:T(1024)S(1)} %copy-done.47, f32[1024]{0:T(1024)S(1)} %copy-done.41, bf16[1025,1,512]{2,0,1:T(8,128)(2,1)S(1)} %copy-done.21, bf16[1025,1,512]{2,0,1:T(8,128)(2,1)S(1)} %get-tuple-element.323, bf16[1025,1,512]{2,0,1:T(8,128)(2,1)S(1)} %get-tuple-element.322, ...), kind=kOutput, calls=%fused_computation.136 | convolution fusion | flops 3244836864 | bytes 8410120 | tf_op jit(solution)/shard_map/td,tpe->dpe/dot_general | solution.py:374
  451.4 4.7 copy.190
  458.6 6.7 %fusion.138 = (f32[1025]{0:T(1024)S(1)}, f32[1025]{0:T(1024)S(1)}, bf16[1024]{0:T(1024)(128)(2,1)S(1)}, bf16[1024]{0:T(1024)(128)(2,1)S(1)}, f32[1025,1024]{1,0:T(8,128)}, /*index=5*/f32[1025,1024]{1,0:T(8,128)}) fusion(f32[1025]{0:T(1024)S(1)} %copy-done.37, f32[1025]{0:T(1024)S(1)} %copy-done.35, bf16[1025,512]{1,0:T(8,128)(2,1)S(1)} %copy-done.5, ...), kind=kLoop, calls=%fused_computation.258 | loop fusion | flops 16789502 | bytes 14718992 | tf_op jit(solution)/shard_map/reduce_sum | solution.py:31
  465.6 3.6 fusion.75
  469.3 21.2 %reduce-scatter.3.cloned.1.call-done = bf16[64,4992]{1,0:T(8,128)(2,1)} async-done(((bf16[1024,4992]{1,0:T(8,128)(2,1)}), bf16[64,4992]{1,0:T(8,128)(2,1)}) %reduce-scatter.3.cloned.1.call-update) | async-done | bytes 638992 | tf_op jit(solution)/shard_map/reduce_scatter | solution.py:324
  491.7 6.3 %fusion.77 = f32[1025,1024]{1,0:T(8,128)S(1)} fusion(bf16[1025,1365]{1,0:T(8,128)(2,1)} %copy-done.50, bf16[1024,4224]{1,0:T(8,128)(2,1)} %all-gather.5.cloned.1.call-done), kind=kOutput, calls=%fused_computation.117 | convolution fusion | flops 2865408000 | bytes 9988096 | tf_op jit(solution)/shard_map/tf,df->td/dot_general | solution.py:316
  500.9 3.5 add_convert_fusion.4
  504.5 3.1 fusion.91
  510.8 66.9 %reduce-scatter.5.cloned.1.call-done = bf16[64,1792]{1,0:T(8,128)(2,1)} async-done(((bf16[1024,1792]{1,0:T(8,128)(2,1)}), bf16[64,1792]{1,0:T(8,128)(2,1)}) %reduce-scatter.5.cloned.1.call-update) | async-done | bytes 229392 | tf_op jit(solution)/shard_map/reduce_scatter | solution.py:394
  (331 shorter events, 203.1 us)
Async XLA Ops:
  7.2 8.4 %copy-start.7 = (bf16[1025,512]{1,0:T(8,128)(2,1)S(1)}, bf16[1025,512]{1,0:T(8,128)(2,1)}, u32[]{:S(2)}) copy-start(bf16[1025,512]{1,0:T(8,128)(2,1)} %param.23) | copy-start | bytes 3148804
  7.2 6.2 %copy-start.48 = (bf16[512]{0:T(512)(128)(2,1)S(1)}, bf16[512]{0:T(512)(128)(2,1)}, u32[]{:S(2)}) copy-start(bf16[512]{0:T(512)(128)(2,1)} %param.27) | copy-start | bytes 3076
  7.2 6.2 %copy-start.49 = (bf16[512]{0:T(512)(128)(2,1)S(1)}, bf16[512]{0:T(512)(128)(2,1)}, u32[]{:S(2)}) copy-start(bf16[512]{0:T(512)(128)(2,1)} %param.28) | copy-start | bytes 3076
  7.2 84.5 %all-gather.3.cloned.1.call-start = ((), (), s32[]{:S(2)}) async-start(), calls=%async_computation.2 | async-start | bytes 4734976 | tf_op jit(solution)/shard_map/all_gather | solution.py:180
  10.8 197.8 %all-gather.5.cloned.1.call-start = ((), (), s32[]{:S(2)}) async-start(), calls=%async_computation.3 | async-start | bytes 9191424 | tf_op jit(solution)/shard_map/all_gather | solution.py:236
  10.8 4.8 collective-permute-start
  13.3 477.1 %reduce-scatter.3.cloned.1.call-start = ((), (), s32[]{:S(2)}) async-start(), calls=%async_computation.4 | async-start | bytes 10862592 | tf_op jit(solution)/shard_map/reduce_scatter | solution.py:324
  17.0 84.3 %copy-start.2 = (bf16[1025,512]{1,0:T(8,128)(2,1)}, bf16[1025,512]{1,0:T(8,128)(2,1)S(1)}, u32[]{:S(2)}) copy-start(bf16[1025,512]{1,0:T(8,128)(2,1)S(1)} %get-tuple-element.329) | copy-start | bytes 3148804
  17.0 84.3 %copy-start.4 = (bf16[1025,512]{1,0:T(8,128)(2,1)}, bf16[1025,512]{1,0:T(8,128)(2,1)S(1)}, u32[]{:S(2)}) copy-start(bf16[1025,512]{1,0:T(8,128)(2,1)S(1)} %get-tuple-element.330) | copy-start | bytes 3148804
  17.4 83.9 %copy-start.34 = (f32[1025]{0:T(1024)}, f32[1025]{0:T(1024)S(1)}, u32[]{:S(2)}) copy-start(f32[1025]{0:T(1024)S(1)} %broadcast_multiply_fusion.7) | copy-start | bytes 12304
  18.1 83.2 %copy-start.36 = (f32[1025]{0:T(1024)}, f32[1025]{0:T(1024)S(1)}, u32[]{:S(2)}) copy-start(f32[1025]{0:T(1024)S(1)} %add_rsqrt_fusion.2) | copy-start | bytes 12304
  94.6 6.7 %copy-start.40 = (f32[1024]{0:T(1024)}, f32[1024]{0:T(1024)S(1)}, u32[]{:S(2)}) copy-start(f32[1024]{0:T(1024)S(1)} %get-tuple-element.341) | copy-start | bytes 12292
  94.6 6.7 %copy-start.46 = (f32[1024]{0:T(1024)}, f32[1024]{0:T(1024)S(1)}, u32[]{:S(2)}) copy-start(f32[1024]{0:T(1024)S(1)} %get-tuple-element.338) | copy-start | bytes 12292
  184.1 5.9 %copy-start.42 = (bf16[1365]{0:T(1024)(128)(2,1)S(1)}, bf16[1365]{0:T(1024)(128)(2,1)}, u32[]{:S(2)}) copy-start(bf16[1365]{0:T(1024)(128)(2,1)} %param.34) | copy-start | bytes 8194
  184.1 5.9 %copy-start.43 = (bf16[1365]{0:T(1024)(128)(2,1)S(1)}, bf16[1365]{0:T(1024)(128)(2,1)}, u32[]{:S(2)}) copy-start(bf16[1365]{0:T(1024)(128)(2,1)} %param.36) | copy-start | bytes 8194
  184.1 2.9 collective-permute-start.1
  189.4 2.7 collective-permute-start.2
  189.6 45.5 %collective-permute-start.5 = (bf16[1025,512]{1,0:T(8,128)(2,1)}, bf16[1025,512]{1,0:T(8,128)(2,1)}, u32[]{:S(2)}, u32[]{:S(2)}) collective-permute-start(bf16[1025,512]{1,0:T(8,128)(2,1)} %param.41), channel_id=1, source_target_pairs={{0,1},{1,0},{2,3},{3,2},{4,5},{5,4},{6,7},{7,6},{8,9},{9,8},{10,11... | collective-permute-start | bytes 3148808 | tf_op jit(solution)/shard_map/ppermute | solution.py:74
  214.3 12.0 %copy-start.14 = (f32[1025,1365]{1,0:T(8,128)}, f32[1025,1365]{1,0:T(8,128)S(1)}, u32[]{:S(2)}) copy-start(f32[1025,1365]{1,0:T(8,128)S(1)} %convolution_add_fusion.1) | copy-start | bytes 16789504
  214.3 12.0 %copy-start.44 = (bf16[1365]{0:T(1024)(128)(2,1)S(1)}, bf16[1365]{0:T(1024)(128)(2,1)}, u32[]{:S(2)}) copy-start(bf16[1365]{0:T(1024)(128)(2,1)} %param.37) | copy-start | bytes 8194
  214.4 12.0 %copy-start.45 = (bf16[1365]{0:T(1024)(128)(2,1)S(1)}, bf16[1365]{0:T(1024)(128)(2,1)}, u32[]{:S(2)}) copy-start(bf16[1365]{0:T(1024)(128)(2,1)} %param.38) | copy-start | bytes 8194
  214.4 12.0 %copy-start.29 = (f32[1025,64]{0,1:T(8,128)S(1)}, f32[1025,64]{0,1:T(8,128)}, u32[]{:S(2)}) copy-start(f32[1025,64]{0,1:T(8,128)} %get-tuple-element.346) | copy-start | bytes 787204
  226.3 4.8 collective-permute-start.3
  234.6 2.2 collective-permute-start.4
  236.8 9.2 %copy-start.19 = (bf16[1025,512]{1,0:T(8,128)(2,1)}, bf16[1025,512]{1,0:T(8,128)(2,1)S(1)}, u32[]{:S(2)}) copy-start(bf16[1025,512]{1,0:T(8,128)(2,1)S(1)} %get-tuple-element.326) | copy-start | bytes 3148804
  245.4 6.4 %copy-start.50 = (bf16[1025,1365]{1,0:T(8,128)(2,1)}, bf16[1025,1365]{1,0:T(8,128)(2,1)S(1)}, u32[]{:S(2)}) copy-start(bf16[1025,1365]{1,0:T(8,128)(2,1)S(1)} %get-tuple-element.96) | copy-start | bytes 8394754
  245.4 6.4 %collective-permute-start.6 = (f32[1025]{0:T(1024)S(1)}, f32[1025]{0:T(1024)S(1)}, u32[]{:S(2)}, u32[]{:S(2)}) collective-permute-start(f32[1025]{0:T(1024)S(1)} %get-tuple-element.238), channel_id=1, source_target_pairs={{0,1},{1,0},{2,3},{3,2},{4,5},{5,4},{6,7},{7,6},{8,9},{9,8},{10,11... | collective-permute-start | bytes 12308 | tf_op jit(solution)/shard_map/ppermute | solution.py:74
  245.5 6.3 %collective-permute-start.7 = (f32[1025]{0:T(1024)S(1)}, f32[1025]{0:T(1024)S(1)}, u32[]{:S(2)}, u32[]{:S(2)}) collective-permute-start(f32[1025]{0:T(1024)S(1)} %get-tuple-element.233), channel_id=1, source_target_pairs={{0,1},{1,0},{2,3},{3,2},{4,5},{5,4},{6,7},{7,6},{8,9},{9,8},{10,11... | collective-permute-start | bytes 12308 | tf_op jit(solution)/shard_map/ppermute | solution.py:74
  246.0 5.8 slice-start.6
  246.0 5.8 slice-start.8
  246.0 6.5 %slice-start.1 = ((s8[5812224]{0:T(1024)(128)(4,1)}), s8[1617920]{0:T(1024)(128)(4,1)S(1)}, s32[]{:S(2)}) async-start(s8[5812224]{0:T(1024)(128)(4,1)} %bitcast.203), calls=%async_computation.7 | async-start | bytes 3235840
  246.0 7.0 %slice-start.7 = ((s8[5812224]{0:T(1024)(128)(4,1)}), s8[1617920]{0:T(1024)(128)(4,1)S(1)}, s32[]{:S(2)}) async-start(s8[5812224]{0:T(1024)(128)(4,1)} %bitcast.218), calls=%async_computation.13 | async-start | bytes 3235840
  246.0 7.4 %slice-start.9 = ((s8[5812224]{0:T(1024)(128)(4,1)}), s8[1617920]{0:T(1024)(128)(4,1)S(1)}, s32[]{:S(2)}) async-start(s8[5812224]{0:T(1024)(128)(4,1)} %bitcast.220), calls=%async_computation.15 | async-start | bytes 3235840
  260.0 6.4 %copy-start.23 = (bf16[1025,1365]{1,0:T(8,128)(2,1)}, bf16[1025,1365]{1,0:T(8,128)(2,1)S(1)}, u32[]{:S(2)}) copy-start(bf16[1025,1365]{1,0:T(8,128)(2,1)S(1)} %get-tuple-element.286) | copy-start | bytes 8394754
  273.3 16.2 %collective-permute-start.8 = (bf16[1025,1024]{1,0:T(8,128)(2,1)}, bf16[1025,1024]{1,0:T(8,128)(2,1)}, u32[]{:S(2)}, u32[]{:S(2)}) collective-permute-start(bf16[1025,1024]{1,0:T(8,128)(2,1)} %fusion.69), channel_id=1, source_target_pairs={{0,1},{1,0},{2,3},{3,2},{4,5},{5,4},{6,7},{7,6},{8,9},{9,8},{10,11... | collective-permute-start | bytes 6297608 | tf_op jit(solution)/shard_map/ppermute | solution.py:74
  289.5 14.2 %copy-start.6 = (bf16[1024,4992]{1,0:T(8,128)(2,1)}, bf16[1024,4992]{1,0:T(8,128)(2,1)S(1)}, u32[]{:S(2)}) copy-start(bf16[1024,4992]{1,0:T(8,128)(2,1)S(1)} %pad_dynamic-update-slice_fusion) | copy-start | bytes 30670852
  289.5 7.3 %copy-start.20 = (bf16[1025,512]{1,0:T(8,128)(2,1)S(1)}, bf16[1025,512]{1,0:T(8,128)(2,1)}, u32[]{:S(2)}) copy-start(bf16[1025,512]{1,0:T(8,128)(2,1)} %copy-done.19) | copy-start | bytes 3148804
  304.0 6.3 %copy-start.31 = (bf16[1025,1024]{1,0:T(8,128)(2,1)S(1)}, bf16[1025,1024]{1,0:T(8,128)(2,1)}, u32[]{:S(2)}) copy-start(bf16[1025,1024]{1,0:T(8,128)(2,1)} %get-tuple-element.97) | copy-start | bytes 6297604
  314.2 263.6 %reduce-scatter.5.cloned.1.call-start = ((), (), s32[]{:S(2)}) async-start(), calls=%async_computation.5 | async-start | bytes 3899392 | tf_op jit(solution)/shard_map/reduce_scatter | solution.py:394
  315.8 101.0 %copy-start.27 = (f32[1025,64]{0,1:T(8,128)S(1)}, f32[1025,64]{0,1:T(8,128)}, u32[]{:S(2)}) copy-start(f32[1025,64]{0,1:T(8,128)} %get-tuple-element.347) | copy-start | bytes 787204
  444.5 14.1 %collective-permute-start.10 = (bf16[1025,1024]{1,0:T(8,128)(2,1)}, bf16[1025,1024]{1,0:T(8,128)(2,1)}, u32[]{:S(2)}, u32[]{:S(2)}) collective-permute-start(bf16[1025,1024]{1,0:T(8,128)(2,1)} %fusion.68), channel_id=1, source_target_pairs={{0,1},{1,0},{2,3},{3,2},{4,5},{5,4},{6,7},{7,6},{8,9},{9,8},{10,11... | collective-permute-start | bytes 6297608 | tf_op jit(solution)/shard_map/ppermute | solution.py:74
  491.6 12.8 %slice-start.4 = ((s8[4227072]{0:T(1024)(128)(4,1)}), s8[32768]{0:T(1024)(128)(4,1)S(1)}, s32[]{:S(2)}) async-start(s8[4227072]{0:T(1024)(128)(4,1)} %bitcast.211), calls=%async_computation.10 | async-start | bytes 65536
  491.6 6.6 %copy-start.33 = (f32[1024,1]{1,0:T(8,128)S(1)}, f32[1024,1]{1,0:T(8,128)}, u32[]{:S(2)}) copy-start(f32[1024,1]{1,0:T(8,128)} %get-tuple-element.336) | copy-start | bytes 12292
  491.7 9.3 %copy-start.39 = (f32[512]{0:T(512)S(1)}, f32[512]{0:T(512)}, u32[]{:S(2)}) copy-start(f32[512]{0:T(512)} %copy-done.38) | copy-start | bytes 6148
  491.7 12.8 %slice-start.5 = ((s8[4227072]{0:T(1024)(128)(4,1)}), s8[4194304]{0:T(1024)(128)(4,1)S(1)}, s32[]{:S(2)}) async-start(s8[4227072]{0:T(1024)(128)(4,1)} %bitcast.211), calls=%async_computation.11 | async-start | bytes 8388608
  498.2 2.7 collective-permute-start.9
  498.3 6.2 %slice-start.2 = ((s8[4227072]{0:T(1024)(128)(4,1)}), s8[4194304]{0:T(1024)(128)(4,1)S(1)}, s32[]{:S(2)}) async-start(s8[4227072]{0:T(1024)(128)(4,1)} %bitcast.209), calls=%async_computation.8 | async-start | bytes 8388608
  498.4 6.0 %slice-start.3 = ((s8[4227072]{0:T(1024)(128)(4,1)}), s8[32768]{0:T(1024)(128)(4,1)S(1)}, s32[]{:S(2)}) async-start(s8[4227072]{0:T(1024)(128)(4,1)} %bitcast.209), calls=%async_computation.9 | async-start | bytes 65536
  (28 other events, 113.8 us)
Sparse Core Ops, SparseCore 0:
  11.4 80.3 all-gather.2
  95.1 113.3 all-gather.4
  314.3 176.0 reduce-scatter.2
  492.6 85.1 reduce-scatter.4

commit v5 on v4

--- a/solution.py
+++ b/solution.py
@@ -304,10 +304,15 @@
             row_major(up_weight_grad.astype(narrow)),
             row_major(down_weight_grad_t.astype(narrow)),
             row_major(proj_weight_grad_t.astype(narrow)),
-            jnp.stack(
-                [gain_two_grad, shift_two_grad, down_bias_grad, proj_bias_grad], axis=1
+            jnp.concatenate(
+                [
+                    jnp.stack(
+                        [gain_two_grad, shift_two_grad, down_bias_grad, proj_bias_grad], axis=1
+                    ),
+                    spread(mid_small, rows_local, row_count),
+                ],
+                axis=1,
             ).astype(narrow),
-            spread(mid_small, rows_local, row_count).astype(narrow),
         ]
     )
     mid_pack, attn_grad_held, down_input_held = lax.optimization_barrier(
@@ -384,9 +389,14 @@
     end_pack, end_at = pack(
         [
             qkv_weight_grad.reshape(model_width, 3 * half_width).astype(narrow),
-            jnp.stack([gain_one_grad, shift_one_grad], axis=1).astype(narrow),
-            spread(
-                jnp.concatenate([query_bias_grad, value_bias_grad]), rows_local, row_count
+            jnp.concatenate(
+                [
+                    jnp.stack([gain_one_grad, shift_one_grad], axis=1),
+                    spread(
+                        jnp.concatenate([query_bias_grad, value_bias_grad]), rows_local, row_count
+                    ),
+                ],
+                axis=1,
             ).astype(narrow),
         ]
     )
@@ -397,9 +407,11 @@
         return sums[:, offset : offset + width]
 
     mid_vectors = cut(mid_sums, mid_at[4], 4)
-    mid_small_sum = cut(mid_sums, mid_at[5], -(-mid_small.shape[0] // rows_local)).reshape(-1)
+    mid_small_sum = cut(
+        mid_sums, mid_at[4] + 4, -(-mid_small.shape[0] // rows_local)
+    ).reshape(-1)
     end_vectors = cut(end_sums, end_at[1], 2)
-    end_small_sum = cut(end_sums, end_at[2], -(-2 * half_width // rows_local)).reshape(-1)
+    end_small_sum = cut(end_sums, end_at[1] + 2, -(-2 * half_width // rows_local)).reshape(-1)
     return (
         layer_out,
         input_grad,

time: 602 us -> 638 us (1.060)
  waiting for transfers between devices: 183 us -> 217 us
    reduce_scatter x1, waiting for transfers between devices: 21.2 us -> 51.9 us  [body(): lax.psum_scatter(mid_pack, 'row', scatter_dimension=0, tiled=True)]
    unnamed x127 -> x124, local copies, waits for them, and re-layouts: 12.3 us -> 15.3 us
  transfers between devices with their start and end apart: 15 -> 15, of which waited for: 7 -> 7; matrix products, arithmetic and copies ran while one was open for 54% -> 51% of each run, Pallas kernels for 0% -> 0%
where the time goes in v5:
time: 638 us; the launch traced here: 627 us
  waiting for transfers between devices  217 us (34%)
  matrix products  212 us (33%)
  other arithmetic  94.1 us (15%)
  local copies, waits for them, and re-layouts  83.3 us (13%)
  between operations  15.3 us (2%)
    all_gather x1, waiting for transfers between devices, body(): attn_full = lax.all_gather(attn_pack, 'row', axis=0, tiled=True)  73.6 us
    reduce_scatter x1, waiting for transfers between devices, body(): lax.psum_scatter(end_pack, 'row', scatter_dimension=0, tiled=True)  70.5 us
    reduce_scatter x1, waiting for transfers between devices, body(): lax.psum_scatter(mid_pack, 'row', scatter_dimension=0, tiled=True)  51.9 us
    dot_general x8, matrix products, attend(): jnp.einsum('qk,kd->qd', weights.astype(narrow), value_block, preferred_el...  20.8 us
    dot_general x8, matrix products, attend_back(): jnp.einsum('qk,qd->kd', weights.astype(narrow), grad_block, preferred_ele...  20.3 us
    dot_general x8, matrix products, attend_back(): jnp.einsum('qk,qd->kd', score_grad, query_block, preferred_element_type=s...  20.1 us
    dot_general x8, matrix products, attend_back(): jnp.einsum('qd,kd->qk', grad_block, value_block, preferred_element_type=s...  17.6 us
    dot_general x8, matrix products, attend_back(): jnp.einsum('qd,kd->qk', query_block, key_block, preferred_element_type=si...  15.6 us
  transfers between devices with their start and end apart: 15, of which 7 were waited for; matrix products, arithmetic and copies ran while one was open for 51% of the time, Pallas kernels for 0%

profile of v5, /device:TPU:0, one launch (start us, length us, event | category | flops | bytes accessed | tf_op | source)
XLA Modules:
  0.0 626.6 jit_solution(16141997471353303587)
XLA Ops:
  18.1 73.6 %all-gather.3.cloned.1.call-done = bf16[1024,2176]{1,0:T(8,128)(2,1)} async-done(((bf16[64,2176]{1,0:T(8,128)(2,1)}), bf16[1024,2176]{1,0:T(8,128)(2,1)}) %all-gather.3.cloned.1.call-update) | async-done | bytes 4456464 | tf_op jit(solution)/shard_map/all_gather | solution.py:180
  96.6 4.7 copy.135
  101.3 6.1 convolution_add_fusion.2
  107.4 2.8 fusion.142
  113.5 3.1 copy.139
  118.7 2.7 slice.224
  123.3 2.9 copy.142
  126.2 3.7 copy.143
  132.3 3.7 copy.144
  135.9 41.9 %while.24 = (s32[]{:T(128)}, bf16[8,1025,64]{1,2,0:T(8,128)(2,1)}, bf16[8,1025,64]{2,1,0:T(8,128)(2,1)S(1)}, bf16[8,1025,64]{2,1,0:T(8,128)(2,1)}, bf16[8,1025,64]{2,1,0:T(8,128)(2,1)}, /*index=5*/s32[]{:T(128)}) while((s32[]{:T(128)}, bf16[8,1025,64]{1,2,0:T(8,128)(2,1)}, bf16[8,1025,64]{2,1,0:T(8,128)(2,1)S(1)}, ...), condition=%wide.region_5.6_spmd, body=%wide.region_2.5_spmd.sunk | while | flops 276377920 | bytes 13570149 | solution.py:219
  138.5 2.6 fusion.180
  148.8 2.6 fusion.180
  159.2 2.6 fusion.180
  164.4 2.6 fusion.180
  169.6 2.6 fusion.180
  174.7 2.6 fusion.180
  177.8 3.8 fusion.99
  193.5 15.0 %all-gather.5.cloned.1.call-done = bf16[1024,4224]{1,0:T(8,128)(2,1)} async-done(((bf16[64,4224]{1,0:T(8,128)(2,1)}), bf16[1024,4224]{1,0:T(8,128)(2,1)}) %all-gather.5.cloned.1.call-update) | async-done | bytes 8650768 | tf_op jit(solution)/shard_map/all_gather | solution.py:236
  208.5 5.8 convolution_add_fusion.1
  214.4 11.9 %fusion.139 = (f32[1025]{0:T(1024)S(1)}, f32[1025,1365]{1,0:T(8,128)}, f32[1025,1365]{1,0:T(8,128)}) fusion(f32[1025,1365]{1,0:T(8,128)S(1)} %convolution_add_fusion.1, f32[1365]{0:T(1024)S(1)} %convert_element_type.222, bf16[1024,4224]{1,0:T(8,128)(2,1)} %all-gather.5.cloned.1.call-done, f32[1024]{0:T(1024)S(1)} %get-tuple-element.308, ...), kind=kOutput, calls=%fused_computation.256 | convolution fusion | flops 2884646912 | bytes 21798236 | tf_op jit(solution)/shard_map/dot_general | solution.py:248
  228.0 3.2 copy.155
  231.2 3.4 multiply_reduce_fusion.3
  236.8 8.6 %multiply_reduce_fusion.1 = (bf16[1365]{0:T(1024)(128)(2,1)S(1)}, f32[1025]{0:T(1024)S(1)}, f32[1025]{0:T(1024)S(1)}, bf16[1365]{0:T(1024)(128)(2,1)S(1)}, bf16[...) fusion(f32[1025,1365]{1,0:T(8,128)} %get-tuple-element.261, f32[1025]{0:T(1024)S(1)} %add_rsqrt_fusion, ...), kind=kOutput, calls=%fused_computation.56 | convolution fusion | flops 2886390272 | bytes 19222538 | tf_op jit(solution)/shard_map/td,df->tf/dot_general | solution.py:267
  246.0 5.7 convolution_convert_fusion
  253.4 6.5 %convert_reduce_fusion = (bf16[1365]{0:T(1024)(128)(2,1)S(1)}, bf16[1025,1365]{1,0:T(8,128)(2,1)S(1)}, bf16[1365]{0:T(1024)(128)(2,1)S(1)}, bf16[1025,1365]{1,0:T(8,128)(2,1)S(1)}) fusion(f32[1025,1365]{1,0:T(8,128)S(1)} %bitcast.220, f32[1025]{0:T(1024)S(1)} %add_multiply_fusion, f32[1025,1365]{1,0:T(8,128)S(1)} %bitcast.205, ...), kind=kLoop, calls=%fused_computation.57 | loop fusion | flops 33576260 | bytes 28009820 | tf_op jit(solution)/shard_map/reduce_sum | solution.py:282
  260.0 6.3 %fusion.80 = f32[1025,1024]{1,0:T(8,128)S(1)} fusion(bf16[1025,1365]{1,0:T(8,128)(2,1)S(1)} %get-tuple-element.269, bf16[1024,4224]{1,0:T(8,128)(2,1)} %all-gather.5.cloned.1.call-done), kind=kOutput, calls=%fused_computation.120 | convolution fusion | flops 2865408000 | bytes 9880234 | tf_op jit(solution)/shard_map/tf,df->td/dot_general | solution.py:288
  266.3 7.1 %fusion.67 = bf16[1025,1024]{1,0:T(8,128)(2,1)} fusion(f32[1025,1024]{1,0:T(8,128)S(1)} %fusion.80, bf16[1025,1365]{1,0:T(8,128)(2,1)S(1)} %get-tuple-element.254, bf16[1024,4224]{1,0:T(8,128)(2,1)} %all-gather.5.cloned.1.call-done), kind=kOutput, calls=%fused_computation.99 | convolution fusion | flops 2867507200 | bytes 11979434 | tf_op jit(solution)/shard_map/tf,df->td/dot_general | solution.py:289
  273.4 6.0 convolution_convert_fusion.2
  279.7 3.8 pad_dynamic-update-slice_fusion.2
  283.6 4.9 convolution_convert_fusion.1
  293.3 5.1 fusion.63
  298.4 6.1 fusion.137
  305.3 3.9 fusion.91
  310.8 3.1 convolution_convert_fusion.3
  317.0 101.0 %while.25 = (s32[]{:T(128)}, f32[8,1025,64]{1,2,0:T(8,128)S(1)}, f32[8,1025,64]{1,2,0:T(8,128)}, bf16[8,1025,64]{1,2,0:T(8,128)(2,1)}, bf16[8,1025,64]{2,1,0:T(8...) while((s32[]{:T(128)}, f32[8,1025,64]{1,2,0:T(8,128)S(1)}, ...), condition=%wide.region_26.27_spmd, body=%wide.region_22.26_spmd.sunk | while | flops 689338112 | bytes 38548648 | solution.py:358
  418.0 4.2 bitcast_multiply_fusion.1
  428.4 3.1 copy.154
  435.5 5.0 add_convert_fusion.3
  440.6 4.9 fusion.66
  446.1 6.4 %convolution_convert_fusion.4 = bf16[1024,3,512]{0,2,1:T(8,128)(2,1)} fusion(f32[1024]{0:T(1024)S(1)} %copy-done.46, f32[1024]{0:T(1024)S(1)} %copy-done.40, bf16[1025,1,512]{2,0,1:T(8,128)(2,1)S(1)} %copy-done.20, bf16[1025,1,512]{2,0,1:T(8,128)(2,1)S(1)} %get-tuple-element.291, bf16[1025,1,512]{2,0,1:T(8,128)(2,1)S(1)} %get-tuple-element.290, ...), kind=kOutput, calls=%fused_computation.133 | convolution fusion | flops 3244836864 | bytes 8410120 | tf_op jit(solution)/shard_map/td,tpe->dpe/dot_general | solution.py:379
  452.5 4.7 copy.164
  460.1 7.0 %fusion.135 = (f32[1025]{0:T(1024)S(1)}, f32[1025]{0:T(1024)S(1)}, bf16[1024]{0:T(1024)(128)(2,1)S(1)}, bf16[1024]{0:T(1024)(128)(2,1)S(1)}, f32[1025,1024]{1,0:T(8,128)}, /*index=5*/f32[1025,1024]{1,0:T(8,128)}) fusion(f32[1025]{0:T(1024)S(1)} %copy-done.36, f32[1025]{0:T(1024)S(1)} %copy-done.34, bf16[1025,512]{1,0:T(8,128)(2,1)S(1)} %copy-done.5, ...), kind=kLoop, calls=%fused_computation.254 | loop fusion | flops 16789502 | bytes 14718992 | tf_op jit(solution)/shard_map/reduce_sum | solution.py:31
  467.4 3.8 fusion.72
  471.2 51.9 %reduce-scatter.3.cloned.1.call-done = bf16[64,4864]{1,0:T(8,128)(2,1)} async-done(((bf16[1024,4864]{1,0:T(8,128)(2,1)}), bf16[64,4864]{1,0:T(8,128)(2,1)}) %reduce-scatter.3.cloned.1.call-update) | async-done | bytes 622608 | tf_op jit(solution)/shard_map/reduce_scatter | solution.py:329
  524.3 6.3 %fusion.74 = f32[1025,1024]{1,0:T(8,128)S(1)} fusion(bf16[1025,1365]{1,0:T(8,128)(2,1)} %copy-done.49, bf16[1024,4224]{1,0:T(8,128)(2,1)} %all-gather.5.cloned.1.call-done), kind=kOutput, calls=%fused_computation.114 | convolution fusion | flops 2865408000 | bytes 9988096 | tf_op jit(solution)/shard_map/tf,df->td/dot_general | solution.py:321
  533.6 3.6 add_convert_fusion.4
  537.2 3.1 fusion.88
  543.7 70.5 %reduce-scatter.5.cloned.1.call-done = bf16[64,1664]{1,0:T(8,128)(2,1)} async-done(((bf16[1024,1664]{1,0:T(8,128)(2,1)}), bf16[64,1664]{1,0:T(8,128)(2,1)}) %reduce-scatter.5.cloned.1.call-update) | async-done | bytes 213008 | tf_op jit(solution)/shard_map/reduce_scatter | solution.py:404
  (330 shorter events, 206.6 us)
Async XLA Ops:
  7.2 8.4 %copy-start.6 = (bf16[1025,512]{1,0:T(8,128)(2,1)S(1)}, bf16[1025,512]{1,0:T(8,128)(2,1)}, u32[]{:S(2)}) copy-start(bf16[1025,512]{1,0:T(8,128)(2,1)} %param.23) | copy-start | bytes 3148804
  7.2 6.2 copy-start.47
  7.2 6.2 copy-start.48
  7.2 84.5 %all-gather.3.cloned.1.call-start = ((), (), s32[]{:S(2)}) async-start(), calls=%async_computation.2 | async-start | bytes 4734976 | tf_op jit(solution)/shard_map/all_gather | solution.py:180
  10.8 197.8 %all-gather.5.cloned.1.call-start = ((), (), s32[]{:S(2)}) async-start(), calls=%async_computation.3 | async-start | bytes 9191424 | tf_op jit(solution)/shard_map/all_gather | solution.py:236
  10.8 4.8 collective-permute-start
  13.3 509.7 %reduce-scatter.3.cloned.1.call-start = ((), (), s32[]{:S(2)}) async-start(), calls=%async_computation.4 | async-start | bytes 10584064 | tf_op jit(solution)/shard_map/reduce_scatter | solution.py:329
  17.0 84.3 %copy-start.2 = (bf16[1025,512]{1,0:T(8,128)(2,1)}, bf16[1025,512]{1,0:T(8,128)(2,1)S(1)}, u32[]{:S(2)}) copy-start(bf16[1025,512]{1,0:T(8,128)(2,1)S(1)} %get-tuple-element.297) | copy-start | bytes 3148804
  17.0 84.3 %copy-start.4 = (bf16[1025,512]{1,0:T(8,128)(2,1)}, bf16[1025,512]{1,0:T(8,128)(2,1)S(1)}, u32[]{:S(2)}) copy-start(bf16[1025,512]{1,0:T(8,128)(2,1)S(1)} %get-tuple-element.298) | copy-start | bytes 3148804
  17.4 83.9 %copy-start.33 = (f32[1025]{0:T(1024)}, f32[1025]{0:T(1024)S(1)}, u32[]{:S(2)}) copy-start(f32[1025]{0:T(1024)S(1)} %broadcast_multiply_fusion.7) | copy-start | bytes 12304
  18.1 83.2 %copy-start.35 = (f32[1025]{0:T(1024)}, f32[1025]{0:T(1024)S(1)}, u32[]{:S(2)}) copy-start(f32[1025]{0:T(1024)S(1)} %add_rsqrt_fusion.2) | copy-start | bytes 12304
  94.6 6.7 %copy-start.39 = (f32[1024]{0:T(1024)}, f32[1024]{0:T(1024)S(1)}, u32[]{:S(2)}) copy-start(f32[1024]{0:T(1024)S(1)} %get-tuple-element.309) | copy-start | bytes 12292
  94.6 6.7 %copy-start.45 = (f32[1024]{0:T(1024)}, f32[1024]{0:T(1024)S(1)}, u32[]{:S(2)}) copy-start(f32[1024]{0:T(1024)S(1)} %get-tuple-element.306) | copy-start | bytes 12292
  184.0 5.9 copy-start.41
  184.0 5.9 copy-start.42
  184.0 2.9 collective-permute-start.1
  189.4 2.7 collective-permute-start.2
  189.6 45.5 %collective-permute-start.5 = (bf16[1025,512]{1,0:T(8,128)(2,1)}, bf16[1025,512]{1,0:T(8,128)(2,1)}, u32[]{:S(2)}, u32[]{:S(2)}) collective-permute-start(bf16[1025,512]{1,0:T(8,128)(2,1)} %param.41), channel_id=1, source_target_pairs={{0,1},{1,0},{2,3},{3,2},{4,5},{5,4},{6,7},{7,6},{8,9},{9,8},{10,11... | collective-permute-start | bytes 3148808 | tf_op jit(solution)/shard_map/ppermute | solution.py:74
  214.3 12.0 %copy-start.13 = (f32[1025,1365]{1,0:T(8,128)}, f32[1025,1365]{1,0:T(8,128)S(1)}, u32[]{:S(2)}) copy-start(f32[1025,1365]{1,0:T(8,128)S(1)} %convolution_add_fusion.1) | copy-start | bytes 16789504
  214.3 12.0 %copy-start.43 = (bf16[1365]{0:T(1024)(128)(2,1)S(1)}, bf16[1365]{0:T(1024)(128)(2,1)}, u32[]{:S(2)}) copy-start(bf16[1365]{0:T(1024)(128)(2,1)} %param.37) | copy-start | bytes 8194
  214.4 12.0 %copy-start.44 = (bf16[1365]{0:T(1024)(128)(2,1)S(1)}, bf16[1365]{0:T(1024)(128)(2,1)}, u32[]{:S(2)}) copy-start(bf16[1365]{0:T(1024)(128)(2,1)} %param.38) | copy-start | bytes 8194
  214.4 12.0 %copy-start.28 = (f32[1025,64]{0,1:T(8,128)S(1)}, f32[1025,64]{0,1:T(8,128)}, u32[]{:S(2)}) copy-start(f32[1025,64]{0,1:T(8,128)} %get-tuple-element.314) | copy-start | bytes 787204
  226.3 4.8 collective-permute-start.3
  234.6 2.2 collective-permute-start.4
  236.8 9.2 %copy-start.18 = (bf16[1025,512]{1,0:T(8,128)(2,1)}, bf16[1025,512]{1,0:T(8,128)(2,1)S(1)}, u32[]{:S(2)}) copy-start(bf16[1025,512]{1,0:T(8,128)(2,1)S(1)} %get-tuple-element.294) | copy-start | bytes 3148804
  245.4 6.3 %copy-start.49 = (bf16[1025,1365]{1,0:T(8,128)(2,1)}, bf16[1025,1365]{1,0:T(8,128)(2,1)S(1)}, u32[]{:S(2)}) copy-start(bf16[1025,1365]{1,0:T(8,128)(2,1)S(1)} %get-tuple-element.96) | copy-start | bytes 8394754
  245.4 6.3 %collective-permute-start.6 = (f32[1025]{0:T(1024)S(1)}, f32[1025]{0:T(1024)S(1)}, u32[]{:S(2)}, u32[]{:S(2)}) collective-permute-start(f32[1025]{0:T(1024)S(1)} %get-tuple-element.206), channel_id=1, source_target_pairs={{0,1},{1,0},{2,3},{3,2},{4,5},{5,4},{6,7},{7,6},{8,9},{9,8},{10,11... | collective-permute-start | bytes 12308 | tf_op jit(solution)/shard_map/ppermute | solution.py:74
  245.5 6.2 collective-permute-start.7
  246.0 5.8 slice-start
  246.0 5.8 slice-start.6
  246.0 5.8 slice-start.8
  246.0 6.5 %slice-start.1 = ((s8[5812224]{0:T(1024)(128)(4,1)}), s8[1617920]{0:T(1024)(128)(4,1)S(1)}, s32[]{:S(2)}) async-start(s8[5812224]{0:T(1024)(128)(4,1)} %bitcast.204), calls=%async_computation.7 | async-start | bytes 3235840
  246.0 7.0 %slice-start.7 = ((s8[5812224]{0:T(1024)(128)(4,1)}), s8[1617920]{0:T(1024)(128)(4,1)S(1)}, s32[]{:S(2)}) async-start(s8[5812224]{0:T(1024)(128)(4,1)} %bitcast.219), calls=%async_computation.13 | async-start | bytes 3235840
  246.0 7.4 %slice-start.9 = ((s8[5812224]{0:T(1024)(128)(4,1)}), s8[1617920]{0:T(1024)(128)(4,1)S(1)}, s32[]{:S(2)}) async-start(s8[5812224]{0:T(1024)(128)(4,1)} %bitcast.221), calls=%async_computation.15 | async-start | bytes 3235840
  260.0 6.4 %copy-start.22 = (bf16[1025,1365]{1,0:T(8,128)(2,1)}, bf16[1025,1365]{1,0:T(8,128)(2,1)S(1)}, u32[]{:S(2)}) copy-start(bf16[1025,1365]{1,0:T(8,128)(2,1)S(1)} %get-tuple-element.254) | copy-start | bytes 8394754
  273.4 19.9 %collective-permute-start.8 = (bf16[1025,1024]{1,0:T(8,128)(2,1)}, bf16[1025,1024]{1,0:T(8,128)(2,1)}, u32[]{:S(2)}, u32[]{:S(2)}) collective-permute-start(bf16[1025,1024]{1,0:T(8,128)(2,1)} %fusion.67), channel_id=1, source_target_pairs={{0,1},{1,0},{2,3},{3,2},{4,5},{5,4},{6,7},{7,6},{8,9},{9,8},{10,11... | collective-permute-start | bytes 6297608 | tf_op jit(solution)/shard_map/ppermute | solution.py:74
  315.3 298.8 %reduce-scatter.5.cloned.1.call-start = ((), (), s32[]{:S(2)}) async-start(), calls=%async_computation.5 | async-start | bytes 3620864 | tf_op jit(solution)/shard_map/reduce_scatter | solution.py:404
  317.0 101.1 %copy-start.26 = (f32[1025,64]{0,1:T(8,128)S(1)}, f32[1025,64]{0,1:T(8,128)}, u32[]{:S(2)}) copy-start(f32[1025,64]{0,1:T(8,128)} %get-tuple-element.315) | copy-start | bytes 787204
  440.5 5.6 copy-start.17
  440.5 5.6 copy-start.3
  445.5 14.6 %collective-permute-start.10 = (bf16[1025,1024]{1,0:T(8,128)(2,1)}, bf16[1025,1024]{1,0:T(8,128)(2,1)}, u32[]{:S(2)}, u32[]{:S(2)}) collective-permute-start(bf16[1025,1024]{1,0:T(8,128)(2,1)} %fusion.66), channel_id=1, source_target_pairs={{0,1},{1,0},{2,3},{3,2},{4,5},{5,4},{6,7},{7,6},{8,9},{9,8},{10,11... | collective-permute-start | bytes 6297608 | tf_op jit(solution)/shard_map/ppermute | solution.py:74
  524.2 13.0 %slice-start.4 = ((s8[4227072]{0:T(1024)(128)(4,1)}), s8[32768]{0:T(1024)(128)(4,1)S(1)}, s32[]{:S(2)}) async-start(s8[4227072]{0:T(1024)(128)(4,1)} %bitcast.212), calls=%async_computation.10 | async-start | bytes 65536
  524.3 6.6 %copy-start.32 = (f32[1024,1]{1,0:T(8,128)S(1)}, f32[1024,1]{1,0:T(8,128)}, u32[]{:S(2)}) copy-start(f32[1024,1]{1,0:T(8,128)} %get-tuple-element.304) | copy-start | bytes 12292
  524.3 9.3 %copy-start.38 = (f32[512]{0:T(512)S(1)}, f32[512]{0:T(512)}, u32[]{:S(2)}) copy-start(f32[512]{0:T(512)} %copy-done.37) | copy-start | bytes 6148
  524.3 12.9 %slice-start.5 = ((s8[4227072]{0:T(1024)(128)(4,1)}), s8[4194304]{0:T(1024)(128)(4,1)S(1)}, s32[]{:S(2)}) async-start(s8[4227072]{0:T(1024)(128)(4,1)} %bitcast.212), calls=%async_computation.11 | async-start | bytes 8388608
  530.8 2.7 collective-permute-start.9
  530.9 6.3 %slice-start.2 = ((s8[4227072]{0:T(1024)(128)(4,1)}), s8[4194304]{0:T(1024)(128)(4,1)S(1)}, s32[]{:S(2)}) async-start(s8[4227072]{0:T(1024)(128)(4,1)} %bitcast.210), calls=%async_computation.8 | async-start | bytes 8388608
  531.1 6.2 slice-start.3
  (27 other events, 108.9 us)
Sparse Core Ops, SparseCore 0:
  11.4 80.3 all-gather.2
  95.1 113.3 all-gather.4
  315.5 207.5 reduce-scatter.2
  525.2 88.8 reduce-scatter.4

commit v6 on v4

--- a/solution.py
+++ b/solution.py
@@ -234,20 +234,16 @@
         ]
     )
     ffn_full = lax.all_gather(ffn_pack, "row", axis=0, tiled=True)
-    gate_full = ffn_full[:, ffn_at[0] : ffn_at[0] + ff_local]
-    up_full = ffn_full[:, ffn_at[1] : ffn_at[1] + ff_local]
+    gate_up_full = ffn_full[:, : ffn_at[2]]
     down_t = ffn_full[:, ffn_at[2] : ffn_at[2] + ff_local]
 
     second_out, normed_two, inv_std_two = norm_forward(
         residual_full, ffn_vectors[:, 0], ffn_vectors[:, 1]
     )
     second_input = second_out.astype(narrow)
-    gate_value = jnp.dot(second_input, gate_full, preferred_element_type=single) + gate_bias.astype(
-        single
-    )
-    up_value = jnp.dot(second_input, up_full, preferred_element_type=single) + up_bias.astype(
-        single
-    )
+    gate_up_value = jnp.dot(second_input, gate_up_full, preferred_element_type=single)
+    gate_value = gate_up_value[:, :ff_local] + gate_bias.astype(single)
+    up_value = gate_up_value[:, ffn_at[1] : ffn_at[1] + ff_local] + up_bias.astype(single)
     sigmoid_gate = jax.nn.sigmoid(gate_value)
     hidden = gate_value * sigmoid_gate * up_value
     hidden_mean = hidden_totals((jnp.sum(hidden, axis=1),))[0][:, None] / FF
@@ -280,13 +276,12 @@
     up_grad = (hidden_grad * gate_value * sigmoid_gate).astype(narrow)
     gate_bias_grad = jnp.sum(gate_grad.astype(single), axis=0)
     up_bias_grad = jnp.sum(up_grad.astype(single), axis=0)
-    gate_weight_grad = jnp.einsum(
-        "td,tf->df", second_input, gate_grad, preferred_element_type=single
-    )
-    up_weight_grad = jnp.einsum("td,tf->df", second_input, up_grad, preferred_element_type=single)
+    gate_up_grad, _ = pack([gate_grad, up_grad, jnp.zeros((local_rows, 0), narrow)])
+    gate_up_weight_grad = jnp.einsum(
+        "td,tf->df", second_input, gate_up_grad, preferred_element_type=single
+    )
     second_back = join_columns(
-        jnp.einsum("tf,df->td", gate_grad, gate_full, preferred_element_type=single)
-        + jnp.einsum("tf,df->td", up_grad, up_full, preferred_element_type=single)
+        jnp.einsum("tf,df->td", gate_up_grad, gate_up_full, preferred_element_type=single)
     )
     second_delta, gain_two_grad, shift_two_grad = norm_backward(
         second_back, normed_two, inv_std_two, ffn_vectors[:, 0]
@@ -300,8 +295,7 @@
     mid_small = jnp.concatenate([gate_bias_grad, up_bias_grad, inner_gain_grad, inner_bias_grad])
     mid_pack, mid_at = pack(
         [
-            row_major(gate_weight_grad.astype(narrow)),
-            row_major(up_weight_grad.astype(narrow)),
+            row_major(gate_up_weight_grad.astype(narrow)),
             row_major(down_weight_grad_t.astype(narrow)),
             row_major(proj_weight_grad_t.astype(narrow)),
             jnp.stack(
@@ -396,8 +390,8 @@
     def cut(sums, offset, width):
         return sums[:, offset : offset + width]
 
-    mid_vectors = cut(mid_sums, mid_at[4], 4)
-    mid_small_sum = cut(mid_sums, mid_at[5], -(-mid_small.shape[0] // rows_local)).reshape(-1)
+    mid_vectors = cut(mid_sums, mid_at[3], 4)
+    mid_small_sum = cut(mid_sums, mid_at[4], -(-mid_small.shape[0] // rows_local)).reshape(-1)
     end_vectors = cut(end_sums, end_at[1], 2)
     end_small_sum = cut(end_sums, end_at[2], -(-2 * half_width // rows_local)).reshape(-1)
     return (
@@ -408,17 +402,17 @@
         cut(end_sums, end_at[0], 3 * half_width).reshape(rows_local, 3, half_width),
         end_small_sum[:half_width],
         end_small_sum[half_width : 2 * half_width],
-        cut(mid_sums, mid_at[3], half_width).T,
+        cut(mid_sums, mid_at[2], half_width).T,
         mid_vectors[:, 3],
         mid_vectors[:, 0],
         mid_vectors[:, 1],
         cut(mid_sums, mid_at[0], ff_local),
         mid_small_sum[:ff_local],
-        cut(mid_sums, mid_at[1], ff_local),
+        cut(mid_sums, mid_at[0] + ffn_at[1], ff_local),
         mid_small_sum[ff_local : 2 * ff_local],
         mid_small_sum[2 * ff_local : 3 * ff_local],
         mid_small_sum[3 * ff_local : 4 * ff_local],
-        cut(mid_sums, mid_at[2], ff_local).T,
+        cut(mid_sums, mid_at[1], ff_local).T,
         mid_vectors[:, 2],
     )
 

time: 602 us -> 588 us (0.977)
  matrix products: 213 us -> 200 us
    dot_general x6 -> x3, matrix products: 42 us -> 30.9 us  [the longest x1 11 us: body(): jnp.einsum('td,tf->df', second_input, gate_up_grad, preferred_element_typ...]
    reduce_sum x1 -> x2, other arithmetic: 6.53 us -> 13.7 us  [the longest x1 9.38 us: body(): gate_bias_grad = jnp.sum(gate_grad.astype(single), axis=0)]
    unnamed x127 -> x125, local copies, waits for them, and re-layouts: 12.3 us -> 9.82 us
where the time goes in v6:
time: 588 us; the launch traced here: 577 us
  matrix products  200 us (34%)
  waiting for transfers between devices  183 us (31%)
  other arithmetic  98.1 us (17%)
  local copies, waits for them, and re-layouts  76.2 us (13%)
  between operations  15.4 us (3%)
    all_gather x1, waiting for transfers between devices, body(): attn_full = lax.all_gather(attn_pack, 'row', axis=0, tiled=True)  73.6 us
    reduce_scatter x1, waiting for transfers between devices, body(): lax.psum_scatter(end_pack, 'row', scatter_dimension=0, tiled=True)  66.7 us
    reduce_scatter x1, waiting for transfers between devices, body(): lax.psum_scatter(mid_pack, 'row', scatter_dimension=0, tiled=True)  21.8 us
    dot_general x8, matrix products, attend(): jnp.einsum('qk,kd->qd', weights.astype(narrow), value_block, preferred_el...  20.8 us
    dot_general x8, matrix products, attend_back(): jnp.einsum('qk,qd->kd', weights.astype(narrow), grad_block, preferred_ele...  20.2 us
    dot_general x8, matrix products, attend_back(): jnp.einsum('qk,qd->kd', score_grad, query_block, preferred_element_type=s...  20.1 us
    dot_general x8, matrix products, attend_back(): jnp.einsum('qd,kd->qk', grad_block, value_block, preferred_element_type=s...  17.6 us
    dot_general x8, matrix products, attend_back(): jnp.einsum('qd,kd->qk', query_block, key_block, preferred_element_type=si...  15.6 us
  transfers between devices with their start and end apart: 15, of which 7 were waited for; matrix products, arithmetic and copies ran while one was open for 54% of the time, Pallas kernels for 0%

profile of v6, /device:TPU:0, one launch (start us, length us, event | category | flops | bytes accessed | tf_op | source)
XLA Modules:
  0.0 576.7 jit_solution(7379811589881633034)
XLA Ops:
  18.1 73.6 %all-gather.3.cloned.1.call-done = bf16[1024,2176]{1,0:T(8,128)(2,1)} async-done(((bf16[64,2176]{1,0:T(8,128)(2,1)}), bf16[1024,2176]{1,0:T(8,128)(2,1)}) %all-gather.3.cloned.1.call-update) | async-done | bytes 4456464 | tf_op jit(solution)/shard_map/all_gather | solution.py:180
  96.5 4.6 copy.166
  101.1 6.0 %convolution_add_fusion = f32[1025,3,512]{2,0,1:T(8,128)S(1)} fusion(bf16[1024,3,512]{0,2,1:T(8,128)(2,1)} %bitcast.217, f32[3,512]{1,0:T(4,128)S(1)} %pad_maximum_fusion.8, f32[1024]{0:T(1024)S(1)} %get-tuple-element.338, f32[1024]{0:T(1024)S(1)} %get-tuple-element.341, f32[1025]{0:T(1024)S(1)} %add_rsqrt_fusion.2, f32[1025]{0:T(1024)S(1)} %broadcast_multiply_fusion.7, ...), kind=kOutput, calls=%fused_computation.75 | convolution fusion | flops 3235392000 | bytes 11565064 | tf_op jit(solution)/shard_map/td,dpe->tpe/dot_general | solution.py:197
  107.2 2.7 fusion.157
  113.3 3.0 copy.170
  118.4 2.7 slice.239
  123.1 2.9 copy.173
  126.0 3.7 copy.174
  132.0 3.7 copy.175
  135.7 41.9 %while.24 = (s32[]{:T(128)}, bf16[8,1025,64]{1,2,0:T(8,128)(2,1)}, bf16[8,1025,64]{2,1,0:T(8,128)(2,1)S(1)}, bf16[8,1025,64]{2,1,0:T(8,128)(2,1)}, bf16[8,1025,64]{2,1,0:T(8,128)(2,1)}, /*index=5*/s32[]{:T(128)}) while((s32[]{:T(128)}, bf16[8,1025,64]{1,2,0:T(8,128)(2,1)}, bf16[8,1025,64]{2,1,0:T(8,128)(2,1)S(1)}, ...), condition=%wide.region_5.6_spmd, body=%wide.region_2.5_spmd.sunk | while | flops 276377920 | bytes 13570149 | solution.py:219
  138.2 2.6 fusion.191
  143.4 2.6 fusion.191
  148.6 2.6 fusion.191
  153.8 2.6 fusion.191
  159.0 2.6 fusion.191
  164.2 2.6 fusion.191
  169.4 2.6 fusion.191
  174.5 2.6 fusion.191
  177.6 3.8 fusion.108
  193.3 14.6 %all-gather.5.cloned.1.call-done = bf16[1024,4224]{1,0:T(8,128)(2,1)} async-done(((bf16[64,4224]{1,0:T(8,128)(2,1)}), bf16[1024,4224]{1,0:T(8,128)(2,1)}) %all-gather.5.cloned.1.call-update) | async-done | bytes 8650768 | tf_op jit(solution)/shard_map/all_gather | solution.py:236
  208.0 9.4 %fusion.56 = f32[1025,2816]{1,0:T(8,128)S(1)} fusion(bf16[1024,4224]{1,0:T(8,128)(2,1)} %all-gather.5.cloned.1.call-done, f32[1024]{0:T(1024)S(1)} %get-tuple-element.340, f32[1024]{0:T(1024)S(1)} %get-tuple-element.339, f32[1025]{0:T(1024)S(1)} %add_rsqrt_fusion.1, f32[1025]{0:T(1024)S(1)} %broadcast_multiply_fusion.6, ...), kind=kOutput, calls=%fused_computation.84 | convolution fusion | flops 5920793600 | bytes 19428360 | tf_op jit(solution)/shard_map/dot_general | solution.py:244
  217.4 4.3 fusion.154
  225.0 3.2 copy.183
  228.3 3.5 multiply_reduce_fusion.3
  234.2 7.0 %multiply_reduce_fusion.1 = (bf16[1365]{0:T(1024)(128)(2,1)S(1)}, f32[1025]{0:T(1024)S(1)}, f32[1025]{0:T(1024)S(1)}, bf16[1365]{0:T(1024)(128)(2,1)S(1)}, bf16[...) fusion(f32[1025,1365]{1,0:T(8,128)S(1)} %bitcast.200, f32[1025]{0:T(1024)S(1)} %add_rsqrt_fusion, ...), kind=kOutput, calls=%fused_computation.65 | convolution fusion | flops 2886390272 | bytes 19006814 | tf_op jit(solution)/shard_map/td,df->tf/dot_general | solution.py:263
  241.8 5.8 %convolution_convert_fusion = bf16[1024,1365]{1,0:T(8,128)(2,1)} fusion(bf16[1025,1365]{1,0:T(8,128)(2,1)S(1)} %get-tuple-element.96, bf16[1025,512]{1,0:T(8,128)(2,1)S(1)} %get-tuple-element.326, bf16[1025,512]{1,0:T(8,128)(2,1)S(1)} %get-tuple-element.325), kind=kOutput, calls=%fused_computation.111 | convolution fusion | flops 2871004160 | bytes 7692970 | tf_op jit(solution)/shard_map/td,tf->df/dot_general | solution.py:259
  247.7 9.4 %fusion.151 = (bf16[1365]{0:T(1024)(128)(2,1)S(1)}, bf16[1025,1365]{1,0:T(8,128)(2,1)}, bf16[1365]{0:T(1024)(128)(2,1)S(1)}, bf16[1025,1365]{1,0:T(8,128)(2,1)}) fusion(f32[1365]{0:T(1024)S(1)} %convert_element_type.236, f32[1025,2816]{1,0:T(8,128)S(1)} %bitcast.202, f32[1365]{0:T(1024)S(1)} %convert_element_type.237, f32[1025]{0:T(1024)S(1)} %add_multiply_fusion, ...), kind=kLoop, calls=%fused_computation.266 | loop fusion | flops 33576260 | bytes 28020740 | tf_op jit(solution)/shard_map/reduce_sum | solution.py:277
  257.4 10.5 %fusion.76 = bf16[1025,1024]{1,0:T(8,128)(2,1)S(1)} fusion(bf16[1024,4224]{1,0:T(8,128)(2,1)} %all-gather.5.cloned.1.call-done, bf16[1025,1365]{1,0:T(8,128)(2,1)} %get-tuple-element.301, bf16[1025,1365]{1,0:T(8,128)(2,1)} %get-tuple-element.288), kind=kOutput, calls=%fused_computation.110 | convolution fusion | flops 5935488000 | bytes 13678592 | tf_op jit(solution)/shard_map/tf,df->td/dot_general | solution.py:284
  268.1 11.0 %convert_dynamic-update-slice_fusion = bf16[1024,4992]{1,0:T(8,128)(2,1)S(1)} fusion(bf16[1025,1365]{1,0:T(8,128)(2,1)} %get-tuple-element.301, bf16[1025,1365]{1,0:T(8,128)(2,1)} %get-tuple-element.288, f32[1024]{0:T(1024)S(1)} %get-tuple-element.340, f32[1024]{0:T(1024)S(1)} %get-tuple-element.339, f32[1025]{0:T(1024)S(1)} %add_rsqrt_fusion.1, ...), kind=kOutput, calls=%fused_computation.74 | convolution fusion | flops 5946768384 | bytes 13479260 | tf_op jit(solution)/shard_map/td,tf->df/dot_general | solution.py:280
  281.3 3.7 fusion.72
  285.1 4.6 fusion.152
  290.0 4.7 fusion.98
  301.9 101.0 %while.25 = (s32[]{:T(128)}, f32[8,1025,64]{1,2,0:T(8,128)S(1)}, f32[8,1025,64]{1,2,0:T(8,128)}, bf16[8,1025,64]{1,2,0:T(8,128)(2,1)}, bf16[8,1025,64]{2,1,0:T(8...) while((s32[]{:T(128)}, f32[8,1025,64]{1,2,0:T(8,128)S(1)}, ...), condition=%wide.region_26.27_spmd, body=%wide.region_22.26_spmd.sunk | while | flops 689338112 | bytes 38548648 | solution.py:347
  317.3 2.5 fusion.202
  393.0 2.5 fusion.202
  403.0 4.3 bitcast_multiply_fusion.1
  413.4 3.2 copy.182
  420.5 5.0 add_convert_fusion.3
  425.6 4.9 fusion.75
  431.0 6.4 %convolution_convert_fusion.2 = bf16[1024,3,512]{0,2,1:T(8,128)(2,1)} fusion(f32[1024]{0:T(1024)S(1)} %copy-done.48, f32[1024]{0:T(1024)S(1)} %copy-done.42, bf16[1025,1,512]{2,0,1:T(8,128)(2,1)S(1)} %copy-done.25, bf16[1025,1,512]{2,0,1:T(8,128)(2,1)S(1)} %get-tuple-element.323, bf16[1025,1,512]{2,0,1:T(8,128)(2,1)S(1)} %get-tuple-element.322, ...), kind=kOutput, calls=%fused_computation.136 | convolution fusion | flops 3244836864 | bytes 8410120 | tf_op jit(solution)/shard_map/td,tpe->dpe/dot_general | solution.py:368
  437.4 4.7 copy.190
  444.7 6.8 %fusion.148 = (f32[1025]{0:T(1024)S(1)}, f32[1025]{0:T(1024)S(1)}, bf16[1024]{0:T(1024)(128)(2,1)S(1)}, bf16[1024]{0:T(1024)(128)(2,1)S(1)}, f32[1025,1024]{1,0:T(8,128)}, /*index=5*/f32[1025,1024]{1,0:T(8,128)}) fusion(f32[1025]{0:T(1024)S(1)} %copy-done.38, f32[1025]{0:T(1024)S(1)} %copy-done.36, bf16[1025,512]{1,0:T(8,128)(2,1)S(1)} %copy-done.8, ...), kind=kLoop, calls=%fused_computation.264 | loop fusion | flops 16789502 | bytes 14718992 | tf_op jit(solution)/shard_map/reduce_sum | solution.py:31
  451.8 3.6 fusion.84
  455.4 21.8 %reduce-scatter.3.cloned.1.call-done = bf16[64,4992]{1,0:T(8,128)(2,1)} async-done(((bf16[1024,4992]{1,0:T(8,128)(2,1)}), bf16[64,4992]{1,0:T(8,128)(2,1)}) %reduce-scatter.3.cloned.1.call-update) | async-done | bytes 638992 | tf_op jit(solution)/shard_map/reduce_scatter | solution.py:318
  478.5 6.3 %fusion.86 = f32[1025,1024]{1,0:T(8,128)S(1)} fusion(bf16[1025,1365]{1,0:T(8,128)(2,1)} %copy-done.51, bf16[1024,4224]{1,0:T(8,128)(2,1)} %all-gather.5.cloned.1.call-done), kind=kOutput, calls=%fused_computation.122 | convolution fusion | flops 2865408000 | bytes 9988096 | tf_op jit(solution)/shard_map/tf,df->td/dot_general | solution.py:310
  487.7 3.5 add_convert_fusion.4
  491.3 3.1 fusion.95
  497.6 66.7 %reduce-scatter.5.cloned.1.call-done = bf16[64,1792]{1,0:T(8,128)(2,1)} async-done(((bf16[1024,1792]{1,0:T(8,128)(2,1)}), bf16[64,1792]{1,0:T(8,128)(2,1)}) %reduce-scatter.5.cloned.1.call-update) | async-done | bytes 229392 | tf_op jit(solution)/shard_map/reduce_scatter | solution.py:388
  (326 shorter events, 195.6 us)
Async XLA Ops:
  7.2 8.4 %copy-start.10 = (bf16[1025,512]{1,0:T(8,128)(2,1)S(1)}, bf16[1025,512]{1,0:T(8,128)(2,1)}, u32[]{:S(2)}) copy-start(bf16[1025,512]{1,0:T(8,128)(2,1)} %param.23) | copy-start | bytes 3148804
  7.2 6.2 %copy-start.49 = (bf16[512]{0:T(512)(128)(2,1)S(1)}, bf16[512]{0:T(512)(128)(2,1)}, u32[]{:S(2)}) copy-start(bf16[512]{0:T(512)(128)(2,1)} %param.27) | copy-start | bytes 3076
  7.2 6.2 %copy-start.50 = (bf16[512]{0:T(512)(128)(2,1)S(1)}, bf16[512]{0:T(512)(128)(2,1)}, u32[]{:S(2)}) copy-start(bf16[512]{0:T(512)(128)(2,1)} %param.28) | copy-start | bytes 3076
  7.2 84.5 %all-gather.3.cloned.1.call-start = ((), (), s32[]{:S(2)}) async-start(), calls=%async_computation.2 | async-start | bytes 4734976 | tf_op jit(solution)/shard_map/all_gather | solution.py:180
  10.8 197.2 %all-gather.5.cloned.1.call-start = ((), (), s32[]{:S(2)}) async-start(), calls=%async_computation.3 | async-start | bytes 9191424 | tf_op jit(solution)/shard_map/all_gather | solution.py:236
  10.8 4.8 collective-permute-start
  13.3 463.9 %reduce-scatter.3.cloned.1.call-start = ((), (), s32[]{:S(2)}) async-start(), calls=%async_computation.4 | async-start | bytes 10862592 | tf_op jit(solution)/shard_map/reduce_scatter | solution.py:318
  17.0 84.1 %copy-start.5 = (bf16[1025,512]{1,0:T(8,128)(2,1)}, bf16[1025,512]{1,0:T(8,128)(2,1)S(1)}, u32[]{:S(2)}) copy-start(bf16[1025,512]{1,0:T(8,128)(2,1)S(1)} %get-tuple-element.329) | copy-start | bytes 3148804
  17.0 84.1 %copy-start.7 = (bf16[1025,512]{1,0:T(8,128)(2,1)}, bf16[1025,512]{1,0:T(8,128)(2,1)S(1)}, u32[]{:S(2)}) copy-start(bf16[1025,512]{1,0:T(8,128)(2,1)S(1)} %get-tuple-element.330) | copy-start | bytes 3148804
  17.4 83.7 %copy-start.35 = (f32[1025]{0:T(1024)}, f32[1025]{0:T(1024)S(1)}, u32[]{:S(2)}) copy-start(f32[1025]{0:T(1024)S(1)} %broadcast_multiply_fusion.7) | copy-start | bytes 12304
  18.1 83.0 %copy-start.37 = (f32[1025]{0:T(1024)}, f32[1025]{0:T(1024)S(1)}, u32[]{:S(2)}) copy-start(f32[1025]{0:T(1024)S(1)} %add_rsqrt_fusion.2) | copy-start | bytes 12304
  94.6 6.5 %copy-start.41 = (f32[1024]{0:T(1024)}, f32[1024]{0:T(1024)S(1)}, u32[]{:S(2)}) copy-start(f32[1024]{0:T(1024)S(1)} %get-tuple-element.341) | copy-start | bytes 12292
  94.6 6.5 %copy-start.47 = (f32[1024]{0:T(1024)}, f32[1024]{0:T(1024)S(1)}, u32[]{:S(2)}) copy-start(f32[1024]{0:T(1024)S(1)} %get-tuple-element.338) | copy-start | bytes 12292
  183.8 5.9 %copy-start.43 = (bf16[1365]{0:T(1024)(128)(2,1)S(1)}, bf16[1365]{0:T(1024)(128)(2,1)}, u32[]{:S(2)}) copy-start(bf16[1365]{0:T(1024)(128)(2,1)} %param.34) | copy-start | bytes 8194
  183.8 5.9 %copy-start.44 = (bf16[1365]{0:T(1024)(128)(2,1)S(1)}, bf16[1365]{0:T(1024)(128)(2,1)}, u32[]{:S(2)}) copy-start(bf16[1365]{0:T(1024)(128)(2,1)} %param.36) | copy-start | bytes 8194
  183.8 2.9 collective-permute-start.1
  184.9 7.2 %copy-start.39 = (f32[512]{0:T(512)}, f32[512]{0:T(512)S(1)}, u32[]{:S(2)}) copy-start(f32[512]{0:T(512)S(1)} %dynamic-slice_reduce_fusion.1) | copy-start | bytes 6148
  189.2 2.7 collective-permute-start.2
  189.4 43.1 %collective-permute-start.5 = (bf16[1025,512]{1,0:T(8,128)(2,1)}, bf16[1025,512]{1,0:T(8,128)(2,1)}, u32[]{:S(2)}, u32[]{:S(2)}) collective-permute-start(bf16[1025,512]{1,0:T(8,128)(2,1)} %param.41), channel_id=1, source_target_pairs={{0,1},{1,0},{2,3},{3,2},{4,5},{5,4},{6,7},{7,6},{8,9},{9,8},{10,11... | collective-permute-start | bytes 3148808 | tf_op jit(solution)/shard_map/ppermute | solution.py:74
  192.2 25.2 %copy-start.1 = (bf16[1025,512]{1,0:T(8,128)(2,1)}, bf16[1025,512]{1,0:T(8,128)(2,1)S(1)}, u32[]{:S(2)}) copy-start(bf16[1025,512]{1,0:T(8,128)(2,1)S(1)} %get-tuple-element.328) | copy-start | bytes 3148804
  217.3 6.1 %copy-start = (f32[1025,2816]{1,0:T(8,128)}, f32[1025,2816]{1,0:T(8,128)S(1)}, u32[]{:S(2)}) copy-start(f32[1025,2816]{1,0:T(8,128)S(1)} %fusion.56) | copy-start | bytes 34636804
  217.4 6.1 %copy-start.45 = (bf16[1365]{0:T(1024)(128)(2,1)S(1)}, bf16[1365]{0:T(1024)(128)(2,1)}, u32[]{:S(2)}) copy-start(bf16[1365]{0:T(1024)(128)(2,1)} %param.37) | copy-start | bytes 8194
  217.4 6.1 %copy-start.46 = (bf16[1365]{0:T(1024)(128)(2,1)S(1)}, bf16[1365]{0:T(1024)(128)(2,1)}, u32[]{:S(2)}) copy-start(bf16[1365]{0:T(1024)(128)(2,1)} %param.38) | copy-start | bytes 8194
  217.4 6.1 %copy-start.30 = (f32[1025,64]{0,1:T(8,128)S(1)}, f32[1025,64]{0,1:T(8,128)}, u32[]{:S(2)}) copy-start(f32[1025,64]{0,1:T(8,128)} %get-tuple-element.346) | copy-start | bytes 787204
  223.4 4.8 collective-permute-start.3
  225.0 9.1 %slice-start = ((s8[5812224]{0:T(1024)(128)(4,1)}), s8[1617920]{0:T(1024)(128)(4,1)S(1)}, s32[]{:S(2)}) async-start(s8[5812224]{0:T(1024)(128)(4,1)} %bitcast.199), calls=%async_computation.6 | async-start | bytes 3235840
  231.9 2.3 collective-permute-start.4
  234.1 7.7 %copy-start.21 = (bf16[1025,512]{1,0:T(8,128)(2,1)}, bf16[1025,512]{1,0:T(8,128)(2,1)S(1)}, u32[]{:S(2)}) copy-start(bf16[1025,512]{1,0:T(8,128)(2,1)S(1)} %get-tuple-element.325) | copy-start | bytes 3148804
  234.1 7.7 %copy-start.23 = (bf16[1025,512]{1,0:T(8,128)(2,1)}, bf16[1025,512]{1,0:T(8,128)(2,1)S(1)}, u32[]{:S(2)}) copy-start(bf16[1025,512]{1,0:T(8,128)(2,1)S(1)} %get-tuple-element.326) | copy-start | bytes 3148804
  241.2 6.4 %copy-start.51 = (bf16[1025,1365]{1,0:T(8,128)(2,1)}, bf16[1025,1365]{1,0:T(8,128)(2,1)S(1)}, u32[]{:S(2)}) copy-start(bf16[1025,1365]{1,0:T(8,128)(2,1)S(1)} %get-tuple-element.96) | copy-start | bytes 8394754
  241.2 6.4 %collective-permute-start.6 = (f32[1025]{0:T(1024)S(1)}, f32[1025]{0:T(1024)S(1)}, u32[]{:S(2)}, u32[]{:S(2)}) collective-permute-start(f32[1025]{0:T(1024)S(1)} %get-tuple-element.238), channel_id=1, source_target_pairs={{0,1},{1,0},{2,3},{3,2},{4,5},{5,4},{6,7},{7,6},{8,9},{9,8},{10,11... | collective-permute-start | bytes 12308 | tf_op jit(solution)/shard_map/ppermute | solution.py:74
  241.3 6.3 %collective-permute-start.7 = (f32[1025]{0:T(1024)S(1)}, f32[1025]{0:T(1024)S(1)}, u32[]{:S(2)}, u32[]{:S(2)}) collective-permute-start(f32[1025]{0:T(1024)S(1)} %get-tuple-element.233), channel_id=1, source_target_pairs={{0,1},{1,0},{2,3},{3,2},{4,5},{5,4},{6,7},{7,6},{8,9},{9,8},{10,11... | collective-permute-start | bytes 12308 | tf_op jit(solution)/shard_map/ppermute | solution.py:74
  241.8 5.9 %slice-start.3 = ((s8[11624448]{0:T(1024)(128)(4,1)}), s8[4194304]{0:T(1024)(128)(4,1)S(1)}, s32[]{:S(2)}) async-start(s8[11624448]{0:T(1024)(128)(4,1)} %bitcast.201), calls=%async_computation.9 | async-start | bytes 8388608
  241.8 5.9 %slice-start.4 = ((s8[11624448]{0:T(1024)(128)(4,1)}), s8[3235840]{0:T(1024)(128)(4,1)S(1)}, s32[]{:S(2)}) async-start(s8[11624448]{0:T(1024)(128)(4,1)} %bitcast.201), calls=%async_computation.10 | async-start | bytes 6471680
  257.4 10.7 %copy-start.2 = (bf16[1025,512]{1,0:T(8,128)(2,1)S(1)}, bf16[1025,512]{1,0:T(8,128)(2,1)}, u32[]{:S(2)}) copy-start(bf16[1025,512]{1,0:T(8,128)(2,1)} %copy-done.1) | copy-start | bytes 3148804
  267.9 13.4 %collective-permute-start.8 = (bf16[1025,1024]{1,0:T(8,128)(2,1)S(1)}, bf16[1025,1024]{1,0:T(8,128)(2,1)S(1)}, u32[]{:S(2)}, u32[]{:S(2)}) collective-permute-start(bf16[1025,1024]{1,0:T(8,128)(2,1)S(1)} %fusion.76), channel_id=1, source_target_pairs={{0,1},{1,0},{2,3},{3,2},{4,5},{5,4},{6,7},{7,6},{8,9},{9,8},{10,11... | collective-permute-start | bytes 6297608 | tf_op jit(solution)/shard_map/ppermute | solution.py:74
  281.3 8.4 %copy-start.9 = (bf16[1024,4992]{1,0:T(8,128)(2,1)}, bf16[1024,4992]{1,0:T(8,128)(2,1)S(1)}, u32[]{:S(2)}) copy-start(bf16[1024,4992]{1,0:T(8,128)(2,1)S(1)} %pad_dynamic-update-slice_fusion) | copy-start | bytes 30670852
  290.0 6.3 %copy-start.32 = (bf16[1025,1024]{1,0:T(8,128)(2,1)S(1)}, bf16[1025,1024]{1,0:T(8,128)(2,1)}, u32[]{:S(2)}) copy-start(bf16[1025,1024]{1,0:T(8,128)(2,1)} %get-tuple-element.97) | copy-start | bytes 6297604
  300.3 264.0 %reduce-scatter.5.cloned.1.call-start = ((), (), s32[]{:S(2)}) async-start(), calls=%async_computation.5 | async-start | bytes 3899392 | tf_op jit(solution)/shard_map/reduce_scatter | solution.py:388
  301.9 101.0 %copy-start.28 = (f32[1025,64]{0,1:T(8,128)S(1)}, f32[1025,64]{0,1:T(8,128)}, u32[]{:S(2)}) copy-start(f32[1025,64]{0,1:T(8,128)} %get-tuple-element.347) | copy-start | bytes 787204
  430.5 14.2 %collective-permute-start.10 = (bf16[1025,1024]{1,0:T(8,128)(2,1)}, bf16[1025,1024]{1,0:T(8,128)(2,1)}, u32[]{:S(2)}, u32[]{:S(2)}) collective-permute-start(bf16[1025,1024]{1,0:T(8,128)(2,1)} %fusion.75), channel_id=1, source_target_pairs={{0,1},{1,0},{2,3},{3,2},{4,5},{5,4},{6,7},{7,6},{8,9},{9,8},{10,11... | collective-permute-start | bytes 6297608 | tf_op jit(solution)/shard_map/ppermute | solution.py:74
  478.4 12.8 %slice-start.7 = ((s8[4227072]{0:T(1024)(128)(4,1)}), s8[32768]{0:T(1024)(128)(4,1)S(1)}, s32[]{:S(2)}) async-start(s8[4227072]{0:T(1024)(128)(4,1)} %bitcast.209), calls=%async_computation.13 | async-start | bytes 65536
  478.4 6.6 %copy-start.34 = (f32[1024,1]{1,0:T(8,128)S(1)}, f32[1024,1]{1,0:T(8,128)}, u32[]{:S(2)}) copy-start(f32[1024,1]{1,0:T(8,128)} %get-tuple-element.336) | copy-start | bytes 12292
  478.4 9.3 %copy-start.40 = (f32[512]{0:T(512)S(1)}, f32[512]{0:T(512)}, u32[]{:S(2)}) copy-start(f32[512]{0:T(512)} %copy-done.39) | copy-start | bytes 6148
  478.4 12.8 %slice-start.8 = ((s8[4227072]{0:T(1024)(128)(4,1)}), s8[4194304]{0:T(1024)(128)(4,1)S(1)}, s32[]{:S(2)}) async-start(s8[4227072]{0:T(1024)(128)(4,1)} %bitcast.209), calls=%async_computation.14 | async-start | bytes 8388608
  485.0 2.7 collective-permute-start.9
  485.1 6.2 %slice-start.5 = ((s8[4227072]{0:T(1024)(128)(4,1)}), s8[4194304]{0:T(1024)(128)(4,1)S(1)}, s32[]{:S(2)}) async-start(s8[4227072]{0:T(1024)(128)(4,1)} %bitcast.207), calls=%async_computation.11 | async-start | bytes 8388608
  485.2 6.0 %slice-start.6 = ((s8[4227072]{0:T(1024)(128)(4,1)}), s8[32768]{0:T(1024)(128)(4,1)S(1)}, s32[]{:S(2)}) async-start(s8[4227072]{0:T(1024)(128)(4,1)} %bitcast.207), calls=%async_computation.12 | async-start | bytes 65536
  (28 other events, 117.0 us)
Sparse Core Ops, SparseCore 0:
  11.4 80.3 all-gather.2
  94.5 113.3 all-gather.4
  300.4 176.7 reduce-scatter.2
  479.4 84.8 reduce-scatter.4

commit v7 on v1

--- a/solution.py
+++ b/solution.py
@@ -4,6 +4,7 @@
 import jax
 import jax.numpy as jnp
 from jax import lax
+from jax.experimental.layout import Layout, with_layout_constraint
 from jax.sharding import PartitionSpec as P
 
 
@@ -96,6 +97,10 @@
 
 def hidden_totals(row_sums):
     return tuple(part + swap_columns(part) for part in row_sums)
+
+
+def row_major(values):
+    return with_layout_constraint(values, Layout((0, 1)))
 
 
 def lane_round(width):
@@ -167,7 +172,9 @@
         [
             qkv_weight.reshape(rows_local, 3 * half_width),
             proj_weight.T,
-            jnp.stack([norm1_gain, norm1_bias, proj_bias], axis=1),
+            jnp.stack(
+                [norm1_gain, norm1_bias, proj_bias, norm2_gain, norm2_bias, down_bias], axis=1
+            ),
         ]
     )
     attn_full = lax.all_gather(attn_pack, "row", axis=0, tiled=True)
@@ -175,7 +182,8 @@
         model_width, 3, half_width
     )
     proj_t = attn_full[:, attn_at[1] : attn_at[1] + half_width]
-    attn_vectors = attn_full[:, attn_at[2] : attn_at[2] + 3].astype(single)
+    attn_vectors = attn_full[:, attn_at[2] : attn_at[2] + 6].astype(single)
+    ffn_vectors = attn_vectors[:, 3:]
 
     whole_input = gather_columns(tokens).astype(single)
     normed_out, normed_one, inv_std_one = norm_forward(
@@ -223,25 +231,19 @@
             gate_weight,
             up_weight,
             down_weight.T,
-            jnp.stack([norm2_gain, norm2_bias, down_bias], axis=1),
         ]
     )
     ffn_full = lax.all_gather(ffn_pack, "row", axis=0, tiled=True)
-    gate_full = ffn_full[:, ffn_at[0] : ffn_at[0] + ff_local]
-    up_full = ffn_full[:, ffn_at[1] : ffn_at[1] + ff_local]
+    gate_up_full = ffn_full[:, : ffn_at[2]]
     down_t = ffn_full[:, ffn_at[2] : ffn_at[2] + ff_local]
-    ffn_vectors = ffn_full[:, ffn_at[3] : ffn_at[3] + 3].astype(single)
 
     second_out, normed_two, inv_std_two = norm_forward(
         residual_full, ffn_vectors[:, 0], ffn_vectors[:, 1]
     )
     second_input = second_out.astype(narrow)
-    gate_value = jnp.dot(second_input, gate_full, preferred_element_type=single) + gate_bias.astype(
-        single
-    )
-    up_value = jnp.dot(second_input, up_full, preferred_element_type=single) + up_bias.astype(
-        single
-    )
+    gate_up_value = jnp.dot(second_input, gate_up_full, preferred_element_type=single)
+    gate_value = gate_up_value[:, :ff_local] + gate_bias.astype(single)
+    up_value = gate_up_value[:, ffn_at[1] : ffn_at[1] + ff_local] + up_bias.astype(single)
     sigmoid_gate = jax.nn.sigmoid(gate_value)
     hidden = gate_value * sigmoid_gate * up_value
     hidden_mean = hidden_totals((jnp.sum(hidden, axis=1),))[0][:, None] / FF
@@ -252,12 +254,6 @@
     down_input = (hidden_normed * inner_gain.astype(single) + inner_bias.astype(single)).astype(
         narrow
     )
-    ffn_partial = jnp.einsum("tf,df->td", down_input, down_t, preferred_element_type=single)
-    layer_out = (
-        residual_half
-        + share_columns(ffn_partial)
-        + own_half(ffn_vectors[:, 2], column, half_width)
-    ).astype(narrow)
     out_full = gather_columns(cotangent)
     out_float = out_full.astype(single)
     down_weight_grad_t = jnp.einsum(
@@ -280,26 +276,27 @@
     up_grad = (hidden_grad * gate_value * sigmoid_gate).astype(narrow)
     gate_bias_grad = jnp.sum(gate_grad.astype(single), axis=0)
     up_bias_grad = jnp.sum(up_grad.astype(single), axis=0)
-    gate_weight_grad = jnp.einsum(
-        "td,tf->df", second_input, gate_grad, preferred_element_type=single
-    )
-    up_weight_grad = jnp.einsum("td,tf->df", second_input, up_grad, preferred_element_type=single)
+    gate_up_grad, _ = pack([gate_grad, up_grad, jnp.zeros((local_rows, 0), narrow)])
+    gate_up_weight_grad = jnp.einsum(
+        "td,tf->df", second_input, gate_up_grad, preferred_element_type=single
+    )
     mid_small = jnp.concatenate([gate_bias_grad, up_bias_grad, inner_gain_grad, inner_bias_grad])
     mid_pack, mid_at = pack(
         [
-            gate_weight_grad.astype(narrow),
-            up_weight_grad.astype(narrow),
-            down_weight_grad_t.astype(narrow),
+            row_major(gate_up_weight_grad.astype(narrow)),
+            row_major(down_weight_grad_t.astype(narrow)),
             jnp.concatenate(
                 [down_bias_grad[:, None], spread(mid_small, rows_local, row_count)], axis=1
             ).astype(narrow),
+            jnp.zeros((model_width, 256), narrow),
         ]
     )
-    mid_pack, gate_grad, up_grad = lax.optimization_barrier((mid_pack, gate_grad, up_grad))
+    mid_pack, gate_up_grad, down_input_held = lax.optimization_barrier(
+        (mid_pack, gate_up_grad, down_input)
+    )
     mid_sums = lax.psum_scatter(mid_pack, "row", scatter_dimension=0, tiled=True).astype(single)
     second_back = join_columns(
-        jnp.einsum("tf,df->td", gate_grad, gate_full, preferred_element_type=single)
-        + jnp.einsum("tf,df->td", up_grad, up_full, preferred_element_type=single)
+        jnp.einsum("tf,df->td", gate_up_grad, gate_up_full, preferred_element_type=single)
     )
     second_delta, gain_two_grad, shift_two_grad = norm_backward(
         second_back, normed_two, inv_std_two, ffn_vectors[:, 0]
@@ -310,6 +307,14 @@
     proj_weight_grad_t = jnp.einsum(
         "td,te->de", attn_grad, attended, preferred_element_type=single
     )
+    ffn_partial = jnp.einsum(
+        "tf,df->td", down_input_held, down_t, preferred_element_type=single
+    )
+    layer_out = (
+        residual_half
+        + share_columns(ffn_partial)
+        + own_half(ffn_vectors[:, 2], column, half_width)
+    ).astype(narrow)
     attended_grad = jnp.einsum(
         "td,de->te", attn_grad, proj_t, preferred_element_type=single
     ).astype(narrow)
@@ -372,7 +377,7 @@
     end_pack, end_at = pack(
         [
             qkv_weight_grad.reshape(model_width, 3 * half_width).astype(narrow),
-            proj_weight_grad_t.astype(narrow),
+            row_major(proj_weight_grad_t.astype(narrow)),
             jnp.concatenate(
                 [
                     jnp.stack(
@@ -393,7 +398,7 @@
     def cut(sums, offset, width):
         return sums[:, offset : offset + width]
 
-    mid_tail = cut(mid_sums, mid_at[3], 1 + -(-mid_small.shape[0] // rows_local))
+    mid_tail = cut(mid_sums, mid_at[2], 1 + -(-mid_small.shape[0] // rows_local))
     mid_small_sum = mid_tail[:, 1:].reshape(-1)
     end_tail = cut(end_sums, end_at[2], 5 + -(-2 * half_width // rows_local))
     end_small_sum = end_tail[:, 5:].reshape(-1)
@@ -411,11 +416,11 @@
         end_tail[:, 4],
         cut(mid_sums, mid_at[0], ff_local),
         mid_small_sum[:ff_local],
-        cut(mid_sums, mid_at[1], ff_local),
+        cut(mid_sums, mid_at[0] + ffn_at[1], ff_local),
         mid_small_sum[ff_local : 2 * ff_local],
         mid_small_sum[2 * ff_local : 3 * ff_local],
         mid_small_sum[3 * ff_local : 4 * ff_local],
-        cut(mid_sums, mid_at[2], ff_local).T,
+        cut(mid_sums, mid_at[1], ff_local).T,
         mid_tail[:, 0],
     )
 

time: 621 us -> 593 us (0.955)
  local copies, waits for them, and re-layouts: 95 us -> 73.8 us
  waiting for transfers between devices: 186 us -> 176 us
  other arithmetic: 101 us -> 108 us
    unnamed x123 -> x103, local copies, waits for them, and re-layouts: 22.9 us -> 7.6 us
    unnamed x5 -> x4, waiting for transfers between devices: 9.31 us -> 0.07 us
    reduce_sum x1 -> x2, other arithmetic: 7.56 us -> 13.4 us  [the longest x1 10.9 us: body(): up_bias_grad = jnp.sum(up_grad.astype(single), axis=0)]
    dot_general x7 -> x4, matrix products: 43.5 us -> 40.3 us  [the longest x1 13.6 us: body(): jnp.einsum('td,tf->df', second_input, gate_up_grad, preferred_element_typ...]
    concatenate x4 -> x5, other arithmetic: 14.7 us -> 16 us  [pack(): return (jnp.concatenate(padded, axis=1), offsets)]
  transfers between devices with their start and end apart: 15 -> 15, of which waited for: 9 -> 8; matrix products, arithmetic and copies ran while one was open for 56% -> 53% of each run, Pallas kernels for 0% -> 0%
where the time goes in v7:
time: 593 us; the launch traced here: 582 us
  matrix products  205 us (35%)
  waiting for transfers between devices  176 us (30%)
  other arithmetic  108 us (18%)
  local copies, waits for them, and re-layouts  73.8 us (12%)
  between operations  15.2 us (3%)
    reduce_scatter x1, waiting for transfers between devices, body(): lax.psum_scatter(end_pack, 'row', scatter_dimension=0, tiled=True)  79.8 us
    all_gather x1, waiting for transfers between devices, body(): attn_full = lax.all_gather(attn_pack, 'row', axis=0, tiled=True)  72.3 us
    dot_general x8, matrix products, attend(): jnp.einsum('qk,kd->qd', weights.astype(narrow), value_block, preferred_el...  20.8 us
    dot_general x8, matrix products, attend_back(): jnp.einsum('qk,qd->kd', weights.astype(narrow), grad_block, preferred_ele...  20.3 us
    dot_general x8, matrix products, attend_back(): jnp.einsum('qk,qd->kd', score_grad, query_block, preferred_element_type=s...  20.1 us
    dot_general x8, matrix products, attend_back(): jnp.einsum('qd,kd->qk', grad_block, value_block, preferred_element_type=s...  17.6 us
    concatenate x5, other arithmetic, pack(): return (jnp.concatenate(padded, axis=1), offsets)  16 us
    dot_general x8, matrix products, attend_back(): jnp.einsum('qd,kd->qk', query_block, key_block, preferred_element_type=si...  15.6 us
  transfers between devices with their start and end apart: 15, of which 8 were waited for; matrix products, arithmetic and copies ran while one was open for 53% of the time, Pallas kernels for 0%

profile of v7, /device:TPU:0, one launch (start us, length us, event | category | flops | bytes accessed | tf_op | source)
XLA Modules:
  0.0 581.6 jit_solution(12247563442174556681)
XLA Ops:
  19.4 72.3 %all-gather.3.cloned.1.call-done = bf16[1024,2176]{1,0:T(8,128)(2,1)} async-done(((bf16[64,2176]{1,0:T(8,128)(2,1)}), bf16[1024,2176]{1,0:T(8,128)(2,1)}) %all-gather.3.cloned.1.call-update) | async-done | bytes 4456464 | tf_op jit(solution)/shard_map/all_gather | solution.py:180
  96.5 4.7 copy.100
  101.2 6.1 %convolution_add_fusion = f32[1025,3,512]{2,0,1:T(8,128)S(1)} fusion(bf16[1024,3,512]{0,2,1:T(8,128)(2,1)} %bitcast.215, f32[3,512]{1,0:T(4,128)S(1)} %pad_maximum_fusion.7, f32[1024]{0:T(1024)S(1)} %get-tuple-element.272, f32[1024]{0:T(1024)S(1)} %get-tuple-element.275, f32[1025]{0:T(1024)S(1)} %add_rsqrt_fusion.2, f32[1025]{0:T(1024)S(1)} %broadcast_multiply_fusion.7, ...), kind=kOutput, calls=%fused_computation.79 | convolution fusion | flops 3235392000 | bytes 11565064 | tf_op jit(solution)/shard_map/td,dpe->tpe/dot_general | solution.py:197
  107.3 2.8 fusion.153
  113.4 3.1 copy.104
  118.6 2.7 slice.245
  123.2 2.9 copy.107
  126.1 3.6 copy.108
  132.1 3.6 copy.109
  135.8 41.6 %while.24 = (s32[]{:T(128)}, bf16[8,1025,64]{1,2,0:T(8,128)(2,1)}, bf16[8,1025,64]{2,1,0:T(8,128)(2,1)S(1)}, bf16[8,1025,64]{2,1,0:T(8,128)(2,1)}, bf16[8,1025,64]{2,1,0:T(8,128)(2,1)}, /*index=5*/s32[]{:T(128)}) while((s32[]{:T(128)}, bf16[8,1025,64]{1,2,0:T(8,128)(2,1)}, bf16[8,1025,64]{2,1,0:T(8,128)(2,1)S(1)}, ...), condition=%wide.region_5.6_spmd, body=%wide.region_2.5_spmd.sunk | while | flops 276377920 | bytes 13570149 | solution.py:219
  138.4 2.6 fusion.186
  143.5 2.6 fusion.186
  148.7 2.6 fusion.186
  153.9 2.6 fusion.186
  159.1 2.6 fusion.186
  164.3 2.6 fusion.186
  169.5 2.6 fusion.186
  174.6 2.6 fusion.186
  177.4 3.8 fusion.107
  193.1 15.5 %all-gather.5.cloned.1.call-done = bf16[1024,4224]{1,0:T(8,128)(2,1)} async-done(((bf16[64,4224]{1,0:T(8,128)(2,1)}), bf16[1024,4224]{1,0:T(8,128)(2,1)}) %all-gather.5.cloned.1.call-update) | async-done | bytes 8650768 | tf_op jit(solution)/shard_map/all_gather | solution.py:236
  208.5 9.4 %fusion.59 = f32[1025,2816]{1,0:T(8,128)S(1)} fusion(bf16[1024,4224]{1,0:T(8,128)(2,1)} %all-gather.5.cloned.1.call-done, f32[1024]{0:T(1024)S(1)} %get-tuple-element.274, f32[1024]{0:T(1024)S(1)} %get-tuple-element.273, f32[1025]{0:T(1024)S(1)} %add_rsqrt_fusion.1, f32[1025]{0:T(1024)S(1)} %broadcast_multiply_fusion.6, ...), kind=kOutput, calls=%fused_computation.89 | convolution fusion | flops 5920793600 | bytes 19428360 | tf_op jit(solution)/shard_map/dot_general | solution.py:244
  224.3 8.7 %multiply_reduce_fusion.1 = (bf16[1365]{0:T(1024)(128)(2,1)S(1)}, f32[1025]{0:T(1024)S(1)}, f32[1025]{0:T(1024)S(1)}, bf16[1365]{0:T(1024)(128)(2,1)S(1)}, f32[1025,1365]{1,0:T(8,128)}) fusion(f32[1025,1365]{1,0:T(8,128)S(1)} %get-tuple-element.225, f32[1025]{0:T(1024)S(1)} %add_rsqrt_fusion, f32[1025]{0:T(1024)S(1)} %add_multiply_fusion.2, ...), kind=kOutput, calls=%fused_computation.68 | convolution fusion | flops 2882193152 | bytes 16203104 | tf_op jit(solution)/shard_map/td,df->tf/dot_general | solution.py:263
  235.2 10.9 %convert_reduce_fusion = (bf16[1365]{0:T(1024)(128)(2,1)S(1)}, bf16[1025,1365]{1,0:T(8,128)(2,1)S(1)}, bf16[1365]{0:T(1024)(128)(2,1)S(1)}, bf16[1025,1365]{1,0:T(8,128)(2,1)S(1)}, bf16[1025,1365]{1,0:T(8,128)(2,1)}) fusion(f32[1365]{0:T(1024)S(1)} %convert_element_type.219, f32[1025,2816]{1,0:T(8,128)S(1)} %fusion.59, f32[1025]{0:T(1024)S(1)} %add_multiply_fusion, ...), kind=kLoop, calls=%fused_computation.69 | loop fusion | flops 40571880 | bytes 30824450 | tf_op jit(solution)/shard_map/reduce_sum | solution.py:278
  248.6 4.1 fusion.56
  252.7 13.6 %convolution_convert_fusion = bf16[1024,2816]{1,0:T(8,128)(2,1)} fusion(f32[1024]{0:T(1024)S(1)} %get-tuple-element.274, f32[1024]{0:T(1024)S(1)} %get-tuple-element.273, f32[1025]{0:T(1024)S(1)} %add_rsqrt_fusion.1, f32[1025]{0:T(1024)S(1)} %broadcast_multiply_fusion.6, bf16[1025,512]{1,0:T(8,128)(2,1)S(1)} %get-tuple-element.262, ...), kind=kOutput, calls=%fused_computation.80 | convolution fusion | flops 5946768384 | bytes 13479260 | tf_op jit(solution)/shard_map/td,tf->df/dot_general | solution.py:280
  266.6 6.7 %convolution_convert_fusion.1 = bf16[1024,1365]{1,0:T(8,128)(2,1)S(1)} fusion(bf16[1025,1365]{1,0:T(8,128)(2,1)} %get-tuple-element.96, bf16[1025,512]{1,0:T(8,128)(2,1)} %copy-done.10, bf16[1025,512]{1,0:T(8,128)(2,1)S(1)} %get-tuple-element.259), kind=kOutput, calls=%fused_computation.117 | convolution fusion | flops 2871004160 | bytes 7692970 | tf_op jit(solution)/shard_map/td,tf->df/dot_general | solution.py:259
  273.6 4.8 fusion.54
  278.4 11.1 %fusion.80 = bf16[1025,1024]{1,0:T(8,128)(2,1)} fusion(bf16[1025,2816]{1,0:T(8,128)(2,1)} %fusion.56, bf16[1024,4224]{1,0:T(8,128)(2,1)} %all-gather.5.cloned.1.call-done), kind=kOutput, calls=%fused_computation.116 | convolution fusion | flops 5912396800 | bytes 13678592 | tf_op jit(solution)/shard_map/tf,df->td/dot_general | solution.py:299
  291.2 3.0 copy.117
  294.3 5.1 fusion.76
  299.4 4.7 convert_reduce_fusion.4
  306.1 2.6 convolution_convert_fusion.2
  310.1 101.0 %while.25 = (s32[]{:T(128)}, f32[8,1025,64]{1,2,0:T(8,128)S(1)}, f32[8,1025,64]{1,2,0:T(8,128)}, bf16[8,1025,64]{1,2,0:T(8,128)(2,1)}, bf16[8,1025,64]{2,1,0:T(8...) while((s32[]{:T(128)}, f32[8,1025,64]{1,2,0:T(8,128)S(1)}, ...), condition=%wide.region_23.24_spmd, body=%wide.region_19.23_spmd.sunk | while | flops 689338112 | bytes 38548648 | solution.py:346
  331.4 2.6 fusion.196
  363.4 2.5 fusion.197
  411.2 4.3 bitcast_multiply_fusion.1
  421.7 3.2 copy.116
  428.8 5.0 add_convert_fusion.3
  433.9 4.7 fusion.79
  439.1 6.4 %convolution_convert_fusion.3 = bf16[1024,3,512]{0,2,1:T(8,128)(2,1)} fusion(f32[1024]{0:T(1024)S(1)} %copy-done.44, f32[1024]{0:T(1024)S(1)} %copy-done.38, bf16[1025,1,512]{2,0,1:T(8,128)(2,1)S(1)} %copy-done.22, bf16[1025,1,512]{2,0,1:T(8,128)(2,1)S(1)} %get-tuple-element.258, bf16[1025,1,512]{2,0,1:T(8,128)(2,1)S(1)} %get-tuple-element.257, ...), kind=kOutput, calls=%fused_computation.139 | convolution fusion | flops 3244836864 | bytes 8410120 | tf_op jit(solution)/shard_map/td,tpe->dpe/dot_general | solution.py:367
  445.5 4.7 copy.126
  453.1 4.2 convolution_convert_fusion.4
  457.3 7.4 %fusion.85 = (bf16[1024]{0:T(1024)(128)(2,1)S(1)}, bf16[1024]{0:T(1024)(128)(2,1)S(1)}, f32[1025]{0:T(1024)S(1)}, f32[1025]{0:T(1024)S(1)}, f32[1025,1024]{1,0:T(8,128)}, /*index=5*/f32[1025,1024]{1,0:T(8,128)}) fusion(bf16[1025,1024]{1,0:T(8,128)(2,1)} %collective-permute-done.10, bf16[1025,1024]{1,0:T(8,128)(2,1)} %fusion.79, f32[1025]{0:T(1024)S(1)} %copy-done.34, ...), kind=kLoop, calls=%fused_computation.120 | loop fusion | flops 16789502 | bytes 14718992 | tf_op jit(solution)/shard_map/reduce_sum | solution.py:34
  465.2 3.6 fusion.69
  470.0 6.3 %fusion.88 = f32[1025,1024]{1,0:T(8,128)S(1)} fusion(bf16[1025,1365]{1,0:T(8,128)(2,1)} %get-tuple-element.96, bf16[1024,4224]{1,0:T(8,128)(2,1)} %all-gather.5.cloned.1.call-done), kind=kOutput, calls=%fused_computation.125 | convolution fusion | flops 2865408000 | bytes 9988096 | tf_op jit(solution)/shard_map/tf,df->td/dot_general | solution.py:310
  479.3 3.5 add_convert_fusion.4
  482.8 3.1 fusion.97
  488.5 79.8 %reduce-scatter.5.cloned.1.call-done = bf16[64,2176]{1,0:T(8,128)(2,1)} async-done(((bf16[1024,2176]{1,0:T(8,128)(2,1)}), bf16[64,2176]{1,0:T(8,128)(2,1)}) %reduce-scatter.5.cloned.1.call-update) | async-done | bytes 278544 | tf_op jit(solution)/shard_map/reduce_scatter | solution.py:396
  (309 shorter events, 197.9 us)
Async XLA Ops:
  7.2 9.7 %copy-start.8 = (bf16[1025,512]{1,0:T(8,128)(2,1)S(1)}, bf16[1025,512]{1,0:T(8,128)(2,1)}, u32[]{:S(2)}) copy-start(bf16[1025,512]{1,0:T(8,128)(2,1)} %param.23) | copy-start | bytes 3148804
  7.2 84.5 %all-gather.3.cloned.1.call-start = ((), (), s32[]{:S(2)}) async-start(), calls=%async_computation.2 | async-start | bytes 4734976 | tf_op jit(solution)/shard_map/all_gather | solution.py:180
  10.7 197.8 %all-gather.5.cloned.1.call-start = ((), (), s32[]{:S(2)}) async-start(), calls=%async_computation.3 | async-start | bytes 9191424 | tf_op jit(solution)/shard_map/all_gather | solution.py:236
  10.8 6.1 %collective-permute-start = (bf16[1025,512]{1,0:T(8,128)(2,1)}, bf16[1025,512]{1,0:T(8,128)(2,1)}, u32[]{:S(2)}, u32[]{:S(2)}) collective-permute-start(bf16[1025,512]{1,0:T(8,128)(2,1)} %param.23), channel_id=1, source_target_pairs={{0,1},{1,0},{2,3},{3,2},{4,5},{5,4},{6,7},{7,6},{8,9},{9,8},{10,11... | collective-permute-start | bytes 3148808 | tf_op jit(solution)/shard_map/ppermute | solution.py:74
  13.3 455.5 %reduce-scatter.3.cloned.1.call-start = ((), (), s32[]{:S(2)}) async-start(), calls=%async_computation.4 | async-start | bytes 10027008 | tf_op jit(solution)/shard_map/reduce_scatter | solution.py:297
  18.3 82.9 %copy-start.2 = (bf16[1025,512]{1,0:T(8,128)(2,1)}, bf16[1025,512]{1,0:T(8,128)(2,1)S(1)}, u32[]{:S(2)}) copy-start(bf16[1025,512]{1,0:T(8,128)(2,1)S(1)} %get-tuple-element.263) | copy-start | bytes 3148804
  18.3 82.9 %copy-start.4 = (bf16[1025,512]{1,0:T(8,128)(2,1)}, bf16[1025,512]{1,0:T(8,128)(2,1)S(1)}, u32[]{:S(2)}) copy-start(bf16[1025,512]{1,0:T(8,128)(2,1)S(1)} %get-tuple-element.264) | copy-start | bytes 3148804
  18.7 82.5 %copy-start.31 = (f32[1025]{0:T(1024)}, f32[1025]{0:T(1024)S(1)}, u32[]{:S(2)}) copy-start(f32[1025]{0:T(1024)S(1)} %broadcast_multiply_fusion.7) | copy-start | bytes 12304
  19.4 81.8 %copy-start.33 = (f32[1025]{0:T(1024)}, f32[1025]{0:T(1024)S(1)}, u32[]{:S(2)}) copy-start(f32[1025]{0:T(1024)S(1)} %add_rsqrt_fusion.2) | copy-start | bytes 12304
  94.6 6.6 %copy-start.37 = (f32[1024]{0:T(1024)}, f32[1024]{0:T(1024)S(1)}, u32[]{:S(2)}) copy-start(f32[1024]{0:T(1024)S(1)} %get-tuple-element.275) | copy-start | bytes 12292
  94.6 6.6 %copy-start.43 = (f32[1024]{0:T(1024)}, f32[1024]{0:T(1024)S(1)}, u32[]{:S(2)}) copy-start(f32[1024]{0:T(1024)S(1)} %get-tuple-element.272) | copy-start | bytes 12292
  183.6 5.9 %copy-start.39 = (bf16[1365]{0:T(1024)(128)(2,1)S(1)}, bf16[1365]{0:T(1024)(128)(2,1)}, u32[]{:S(2)}) copy-start(bf16[1365]{0:T(1024)(128)(2,1)} %param.34) | copy-start | bytes 8194
  183.6 5.9 %copy-start.40 = (bf16[1365]{0:T(1024)(128)(2,1)S(1)}, bf16[1365]{0:T(1024)(128)(2,1)}, u32[]{:S(2)}) copy-start(bf16[1365]{0:T(1024)(128)(2,1)} %param.36) | copy-start | bytes 8194
  183.6 2.9 collective-permute-start.1
  184.7 7.2 %copy-start.35 = (f32[512]{0:T(512)}, f32[512]{0:T(512)S(1)}, u32[]{:S(2)}) copy-start(f32[512]{0:T(512)S(1)} %dynamic-slice_reduce_fusion.1) | copy-start | bytes 6148
  188.9 2.7 collective-permute-start.2
  189.1 33.5 %collective-permute-start.5 = (bf16[1025,512]{1,0:T(8,128)(2,1)}, bf16[1025,512]{1,0:T(8,128)(2,1)}, u32[]{:S(2)}, u32[]{:S(2)}) collective-permute-start(bf16[1025,512]{1,0:T(8,128)(2,1)} %param.41), channel_id=1, source_target_pairs={{0,1},{1,0},{2,3},{3,2},{4,5},{5,4},{6,7},{7,6},{8,9},{9,8},{10,11... | collective-permute-start | bytes 3148808 | tf_op jit(solution)/shard_map/ppermute | solution.py:74
  220.4 1.2 collective-permute-start.3
  222.4 1.9 collective-permute-start.4
  224.3 9.1 %copy-start.10 = (bf16[1025,512]{1,0:T(8,128)(2,1)}, bf16[1025,512]{1,0:T(8,128)(2,1)S(1)}, u32[]{:S(2)}) copy-start(bf16[1025,512]{1,0:T(8,128)(2,1)S(1)} %get-tuple-element.260) | copy-start | bytes 3148804
  233.0 1.2 collective-permute-start.6
  233.9 1.2 collective-permute-start.7
  266.5 7.0 %slice-start.4 = ((s8[5767168]{0:T(1024)(128)(4,1)}), s8[4194304]{0:T(1024)(128)(4,1)S(1)}, s32[]{:S(2)}) async-start(s8[5767168]{0:T(1024)(128)(4,1)} %bitcast.212), calls=%async_computation.10 | async-start | bytes 8388608
  266.6 7.0 %slice-start.5 = ((s8[5767168]{0:T(1024)(128)(4,1)}), s8[1572864]{0:T(1024)(128)(4,1)S(1)}, s32[]{:S(2)}) async-start(s8[5767168]{0:T(1024)(128)(4,1)} %bitcast.212), calls=%async_computation.11 | async-start | bytes 3145728
  278.4 11.2 %copy-start.27 = (f32[1025,64]{0,1:T(8,128)S(1)}, f32[1025,64]{0,1:T(8,128)}, u32[]{:S(2)}) copy-start(f32[1025,64]{0,1:T(8,128)} %get-tuple-element.280) | copy-start | bytes 787204
  289.5 4.8 collective-permute-start.9
  294.2 274.1 %reduce-scatter.5.cloned.1.call-start = ((), (), s32[]{:S(2)}) async-start(), calls=%async_computation.5 | async-start | bytes 4734976 | tf_op jit(solution)/shard_map/reduce_scatter | solution.py:396
  294.2 5.1 copy-start.11
  310.1 101.0 %copy-start.25 = (f32[1025,64]{0,1:T(8,128)S(1)}, f32[1025,64]{0,1:T(8,128)}, u32[]{:S(2)}) copy-start(f32[1025,64]{0,1:T(8,128)} %get-tuple-element.281) | copy-start | bytes 787204
  428.8 5.1 copy-start.22
  428.8 5.1 copy-start.23
  433.9 5.3 copy-start.21
  433.9 5.2 copy-start.3
  433.9 5.2 copy-start.5
  433.9 5.2 copy-start.32
  433.9 5.2 copy-start.34
  433.9 5.2 copy-start.38
  433.9 5.2 copy-start.44
  438.7 18.6 %collective-permute-start.10 = (bf16[1025,1024]{1,0:T(8,128)(2,1)}, bf16[1025,1024]{1,0:T(8,128)(2,1)}, u32[]{:S(2)}, u32[]{:S(2)}) collective-permute-start(bf16[1025,1024]{1,0:T(8,128)(2,1)} %fusion.79), channel_id=1, source_target_pairs={{0,1},{1,0},{2,3},{3,2},{4,5},{5,4},{6,7},{7,6},{8,9},{9,8},{10,11... | collective-permute-start | bytes 6297608 | tf_op jit(solution)/shard_map/ppermute | solution.py:74
  469.9 12.8 %slice-start.2 = ((s8[4227072]{0:T(1024)(128)(4,1)}), s8[32768]{0:T(1024)(128)(4,1)S(1)}, s32[]{:S(2)}) async-start(s8[4227072]{0:T(1024)(128)(4,1)} %bitcast.205), calls=%async_computation.8 | async-start | bytes 65536
  470.0 6.7 %copy-start.30 = (f32[1024,1]{1,0:T(8,128)S(1)}, f32[1024,1]{1,0:T(8,128)}, u32[]{:S(2)}) copy-start(f32[1024,1]{1,0:T(8,128)} %get-tuple-element.270) | copy-start | bytes 12292
  470.0 9.3 %copy-start.9 = (bf16[1025,512]{1,0:T(8,128)(2,1)S(1)}, bf16[1025,512]{1,0:T(8,128)(2,1)}, u32[]{:S(2)}) copy-start(bf16[1025,512]{1,0:T(8,128)(2,1)} %param.23) | copy-start | bytes 3148804
  470.0 9.3 %copy-start.20 = (bf16[1025,512]{1,0:T(8,128)(2,1)S(1)}, bf16[1025,512]{1,0:T(8,128)(2,1)}, u32[]{:S(2)}) copy-start(bf16[1025,512]{1,0:T(8,128)(2,1)} %copy-done.19) | copy-start | bytes 3148804
  470.0 9.3 %copy-start.36 = (f32[512]{0:T(512)S(1)}, f32[512]{0:T(512)}, u32[]{:S(2)}) copy-start(f32[512]{0:T(512)} %copy-done.35) | copy-start | bytes 6148
  470.0 12.8 %slice-start.3 = ((s8[4227072]{0:T(1024)(128)(4,1)}), s8[4194304]{0:T(1024)(128)(4,1)S(1)}, s32[]{:S(2)}) async-start(s8[4227072]{0:T(1024)(128)(4,1)} %bitcast.205), calls=%async_computation.9 | async-start | bytes 8388608
  476.5 2.7 collective-permute-start.8
  476.7 6.1 %slice-start = ((s8[4227072]{0:T(1024)(128)(4,1)}), s8[4194304]{0:T(1024)(128)(4,1)S(1)}, s32[]{:S(2)}) async-start(s8[4227072]{0:T(1024)(128)(4,1)} %bitcast.203), calls=%async_computation.6 | async-start | bytes 8388608
  476.8 5.9 %slice-start.1 = ((s8[4227072]{0:T(1024)(128)(4,1)}), s8[32768]{0:T(1024)(128)(4,1)S(1)}, s32[]{:S(2)}) async-start(s8[4227072]{0:T(1024)(128)(4,1)} %bitcast.203), calls=%async_computation.7 | async-start | bytes 65536
  (18 other events, 57.4 us)
Sparse Core Ops, SparseCore 0:
  11.3 80.3 all-gather.2
  95.1 113.3 all-gather.4
  294.3 169.7 reduce-scatter.2
  470.1 98.1 reduce-scatter.4

commit v8 on v6

--- a/solution.py
+++ b/solution.py
@@ -348,11 +348,14 @@
         attend_back,
         (by_head(queries), by_head(keys_all), by_head(values_all), by_head(attended_grad)),
     )
+    back_cosine, back_sine, query_grads = lax.optimization_barrier(
+        (cosine_table, sine_table, query_grads)
+    )
     query_pre = rotary_back(
-        from_head(query_grads).reshape(local_rows, head_local, HD), cosine_table, sine_table
+        from_head(query_grads).reshape(local_rows, head_local, HD), back_cosine, back_sine
     )
     key_pre = rotary_back(
-        from_head(key_grads).reshape(local_rows, head_local, HD), cosine_table, sine_table
+        from_head(key_grads).reshape(local_rows, head_local, HD), back_cosine, back_sine
     )
     qkv_grad = jnp.stack(
         [

time: 588 us -> 591 us (level)
  transfers between devices with their start and end apart: 15 -> 15, of which waited for: 7 -> 8; matrix products, arithmetic and copies ran while one was open for 54% -> 54% of each run, Pallas kernels for 0% -> 0%
where the time goes in v8:
time: 591 us; the launch traced here: 580 us
  matrix products  203 us (34%)
  waiting for transfers between devices  183 us (31%)
  other arithmetic  102 us (17%)
  local copies, waits for them, and re-layouts  73.1 us (12%)
  between operations  15.3 us (3%)
    all_gather x1, waiting for transfers between devices, body(): attn_full = lax.all_gather(attn_pack, 'row', axis=0, tiled=True)  73.6 us
    reduce_scatter x1, waiting for transfers between devices, body(): lax.psum_scatter(end_pack, 'row', scatter_dimension=0, tiled=True)  66.9 us
    dot_general x8, matrix products, attend(): jnp.einsum('qk,kd->qd', weights.astype(narrow), value_block, preferred_el...  20.8 us
    dot_general x8, matrix products, attend_back(): jnp.einsum('qk,qd->kd', weights.astype(narrow), grad_block, preferred_ele...  20.2 us
    dot_general x8, matrix products, attend_back(): jnp.einsum('qk,qd->kd', score_grad, query_block, preferred_element_type=s...  20.1 us
    reduce_scatter x1, waiting for transfers between devices, body(): lax.psum_scatter(mid_pack, 'row', scatter_dimension=0, tiled=True)  19.7 us
    dot_general x8, matrix products, attend_back(): jnp.einsum('qd,kd->qk', grad_block, value_block, preferred_element_type=s...  17.6 us
    dot_general x8, matrix products, attend_back(): jnp.einsum('qd,kd->qk', query_block, key_block, preferred_element_type=si...  15.6 us
  transfers between devices with their start and end apart: 15, of which 8 were waited for; matrix products, arithmetic and copies ran while one was open for 54% of the time, Pallas kernels for 0%

profile of v8, /device:TPU:0, one launch (start us, length us, event | category | flops | bytes accessed | tf_op | source)
XLA Modules:
  0.0 579.8 jit_solution(12739138523324134108)
XLA Ops:
  18.1 73.6 %all-gather.3.cloned.1.call-done = bf16[1024,2176]{1,0:T(8,128)(2,1)} async-done(((bf16[64,2176]{1,0:T(8,128)(2,1)}), bf16[1024,2176]{1,0:T(8,128)(2,1)}) %all-gather.3.cloned.1.call-update) | async-done | bytes 4456464 | tf_op jit(solution)/shard_map/all_gather | solution.py:180
  96.5 4.6 copy.166
  101.2 6.1 %convolution_add_fusion = f32[1025,3,512]{2,0,1:T(8,128)S(1)} fusion(bf16[1024,3,512]{0,2,1:T(8,128)(2,1)} %bitcast.215, f32[3,512]{1,0:T(4,128)S(1)} %pad_maximum_fusion.8, f32[1024]{0:T(1024)S(1)} %get-tuple-element.344, f32[1024]{0:T(1024)S(1)} %get-tuple-element.347, f32[1025]{0:T(1024)S(1)} %add_rsqrt_fusion.2, f32[1025]{0:T(1024)S(1)} %broadcast_multiply_fusion.7, ...), kind=kOutput, calls=%fused_computation.75 | convolution fusion | flops 3235392000 | bytes 11565064 | tf_op jit(solution)/shard_map/td,dpe->tpe/dot_general | solution.py:197
  107.4 2.8 fusion.157
  113.3 3.1 copy.170
  118.5 2.7 slice.239
  123.2 2.9 copy.173
  126.1 3.7 copy.174
  132.1 3.7 copy.175
  135.8 41.9 %while.24 = (s32[]{:T(128)}, bf16[8,1025,64]{1,2,0:T(8,128)(2,1)}, bf16[8,1025,64]{2,1,0:T(8,128)(2,1)S(1)}, bf16[8,1025,64]{2,1,0:T(8,128)(2,1)}, bf16[8,1025,64]{2,1,0:T(8,128)(2,1)}, /*index=5*/s32[]{:T(128)}) while((s32[]{:T(128)}, bf16[8,1025,64]{1,2,0:T(8,128)(2,1)}, bf16[8,1025,64]{2,1,0:T(8,128)(2,1)S(1)}, ...), condition=%wide.region_5.6_spmd, body=%wide.region_2.5_spmd.sunk | while | flops 276377920 | bytes 13570149 | solution.py:219
  138.4 2.6 fusion.191
  143.6 2.6 fusion.191
  148.7 2.6 fusion.191
  153.9 2.6 fusion.191
  159.1 2.6 fusion.191
  164.3 2.6 fusion.191
  169.5 2.6 fusion.191
  174.6 2.6 fusion.191
  177.7 3.8 fusion.108
  193.4 15.2 %all-gather.5.cloned.1.call-done = bf16[1024,4224]{1,0:T(8,128)(2,1)} async-done(((bf16[64,4224]{1,0:T(8,128)(2,1)}), bf16[1024,4224]{1,0:T(8,128)(2,1)}) %all-gather.5.cloned.1.call-update) | async-done | bytes 8650768 | tf_op jit(solution)/shard_map/all_gather | solution.py:236
  208.5 9.4 %fusion.56 = f32[1025,2816]{1,0:T(8,128)S(1)} fusion(bf16[1024,4224]{1,0:T(8,128)(2,1)} %all-gather.5.cloned.1.call-done, f32[1024]{0:T(1024)S(1)} %get-tuple-element.346, f32[1024]{0:T(1024)S(1)} %get-tuple-element.345, f32[1025]{0:T(1024)S(1)} %add_rsqrt_fusion.1, f32[1025]{0:T(1024)S(1)} %broadcast_multiply_fusion.6, ...), kind=kOutput, calls=%fused_computation.84 | convolution fusion | flops 5920793600 | bytes 19428360 | tf_op jit(solution)/shard_map/dot_general | solution.py:244
  218.0 4.5 fusion.154
  225.2 3.5 multiply_reduce_fusion.3
  230.7 8.5 %multiply_reduce_fusion.1 = (bf16[1365]{0:T(1024)(128)(2,1)S(1)}, f32[1025]{0:T(1024)S(1)}, f32[1025]{0:T(1024)S(1)}, bf16[1365]{0:T(1024)(128)(2,1)S(1)}, bf16[...) fusion(f32[1025,1365]{1,0:T(8,128)S(1)} %copy-done, f32[1025]{0:T(1024)S(1)} %add_rsqrt_fusion, ...), kind=kOutput, calls=%fused_computation.65 | convolution fusion | flops 2886390272 | bytes 19006814 | tf_op jit(solution)/shard_map/td,df->tf/dot_general | solution.py:263
  239.7 7.7 %convolution_convert_fusion = bf16[1024,1365]{1,0:T(8,128)(2,1)} fusion(bf16[1025,1365]{1,0:T(8,128)(2,1)} %get-tuple-element.99, bf16[1025,512]{1,0:T(8,128)(2,1)S(1)} %get-tuple-element.332, bf16[1025,512]{1,0:T(8,128)(2,1)S(1)} %get-tuple-element.331), kind=kOutput, calls=%fused_computation.111 | convolution fusion | flops 2871004160 | bytes 7692970 | tf_op jit(solution)/shard_map/td,tf->df/dot_general | solution.py:259
  247.5 9.4 %fusion.151 = (bf16[1365]{0:T(1024)(128)(2,1)S(1)}, bf16[1025,1365]{1,0:T(8,128)(2,1)}, bf16[1365]{0:T(1024)(128)(2,1)S(1)}, bf16[1025,1365]{1,0:T(8,128)(2,1)}) fusion(f32[1365]{0:T(1024)S(1)} %convert_element_type.236, f32[1025,2816]{1,0:T(8,128)S(1)} %bitcast.200, f32[1365]{0:T(1024)S(1)} %convert_element_type.237, f32[1025]{0:T(1024)S(1)} %add_multiply_fusion, ...), kind=kLoop, calls=%fused_computation.266 | loop fusion | flops 33576260 | bytes 28020740 | tf_op jit(solution)/shard_map/reduce_sum | solution.py:277
  257.1 10.4 %fusion.76 = bf16[1025,1024]{1,0:T(8,128)(2,1)S(1)} fusion(bf16[1024,4224]{1,0:T(8,128)(2,1)} %all-gather.5.cloned.1.call-done, bf16[1025,1365]{1,0:T(8,128)(2,1)} %get-tuple-element.307, bf16[1025,1365]{1,0:T(8,128)(2,1)} %get-tuple-element.294), kind=kOutput, calls=%fused_computation.110 | convolution fusion | flops 5935488000 | bytes 13678592 | tf_op jit(solution)/shard_map/tf,df->td/dot_general | solution.py:284
  267.9 11.0 %convert_dynamic-update-slice_fusion = bf16[1024,4992]{1,0:T(8,128)(2,1)S(1)} fusion(bf16[1025,1365]{1,0:T(8,128)(2,1)} %get-tuple-element.307, bf16[1025,1365]{1,0:T(8,128)(2,1)} %get-tuple-element.294, f32[1024]{0:T(1024)S(1)} %get-tuple-element.346, f32[1024]{0:T(1024)S(1)} %get-tuple-element.345, f32[1025]{0:T(1024)S(1)} %add_rsqrt_fusion.1, ...), kind=kOutput, calls=%fused_computation.74 | convolution fusion | flops 5946768384 | bytes 13479260 | tf_op jit(solution)/shard_map/td,tf->df/dot_general | solution.py:280
  281.2 5.6 fusion.72
  286.8 6.2 %fusion.152 = (bf16[1024]{0:T(1024)(128)(2,1)S(1)}, bf16[1025,1024]{1,0:T(8,128)(2,1)}, f32[1025,1024]{1,0:T(8,128)}, bf16[1024]{0:T(1024)(128)(2,1)S(1)}) fusion(f32[1025]{0:T(1024)S(1)} %broadcast_multiply_fusion.4, f32[1025]{0:T(1024)S(1)} %broadcast_multiply_fusion.6, bf16[1025,512]{1,0:T(8,128)(2,1)S(1)} %get-tuple-element.334, ...), kind=kLoop, calls=%fused_computation.267 | loop fusion | flops 24138752 | bytes 14718992 | tf_op jit(solution)/shard_map/reduce_sum | solution.py:291
  293.3 4.7 fusion.98
  305.2 100.9 %while.25 = (s32[]{:T(128)}, f32[8,1025,64]{1,2,0:T(8,128)S(1)}, f32[8,1025,64]{1,2,0:T(8,128)}, bf16[8,1025,64]{1,2,0:T(8,128)(2,1)}, bf16[8,1025,64]{2,1,0:T(8...) while((s32[]{:T(128)}, f32[8,1025,64]{1,2,0:T(8,128)S(1)}, ...), condition=%wide.region_26.27_spmd, body=%wide.region_22.26_spmd.sunk | while | flops 689338112 | bytes 38548648 | solution.py:347
  320.4 2.5 fusion.202
  326.4 2.5 fusion.201
  396.1 2.5 fusion.202
  406.1 4.3 bitcast_multiply_fusion.1
  418.6 3.2 copy.182
  425.7 5.0 add_convert_fusion.3
  430.7 4.9 fusion.75
  436.0 6.4 %convolution_convert_fusion.2 = bf16[1024,3,512]{0,2,1:T(8,128)(2,1)} fusion(f32[1024]{0:T(1024)S(1)} %copy-done.45, f32[1024]{0:T(1024)S(1)} %copy-done.39, bf16[1025,1,512]{2,0,1:T(8,128)(2,1)S(1)} %copy-done.22, bf16[1025,1,512]{2,0,1:T(8,128)(2,1)S(1)} %get-tuple-element.329, bf16[1025,1,512]{2,0,1:T(8,128)(2,1)S(1)} %get-tuple-element.328, ...), kind=kOutput, calls=%fused_computation.136 | convolution fusion | flops 3244836864 | bytes 8410120 | tf_op jit(solution)/shard_map/td,tpe->dpe/dot_general | solution.py:371
  442.3 4.7 copy.190
  449.6 6.9 %fusion.148 = (f32[1025]{0:T(1024)S(1)}, f32[1025]{0:T(1024)S(1)}, bf16[1024]{0:T(1024)(128)(2,1)S(1)}, bf16[1024]{0:T(1024)(128)(2,1)S(1)}, f32[1025,1024]{1,0:T(8,128)}, /*index=5*/f32[1025,1024]{1,0:T(8,128)}) fusion(f32[1025]{0:T(1024)S(1)} %copy-done.35, f32[1025]{0:T(1024)S(1)} %copy-done.33, bf16[1025,512]{1,0:T(8,128)(2,1)S(1)} %copy-done.7, ...), kind=kLoop, calls=%fused_computation.264 | loop fusion | flops 16789502 | bytes 14718992 | tf_op jit(solution)/shard_map/reduce_sum | solution.py:31
  456.8 3.6 fusion.84
  460.4 19.7 %reduce-scatter.3.cloned.1.call-done = bf16[64,4992]{1,0:T(8,128)(2,1)} async-done(((bf16[1024,4992]{1,0:T(8,128)(2,1)}), bf16[64,4992]{1,0:T(8,128)(2,1)}) %reduce-scatter.3.cloned.1.call-update) | async-done | bytes 638992 | tf_op jit(solution)/shard_map/reduce_scatter | solution.py:318
  481.3 6.3 %fusion.86 = f32[1025,1024]{1,0:T(8,128)S(1)} fusion(bf16[1025,1365]{1,0:T(8,128)(2,1)} %get-tuple-element.99, bf16[1024,4224]{1,0:T(8,128)(2,1)} %all-gather.5.cloned.1.call-done), kind=kOutput, calls=%fused_computation.122 | convolution fusion | flops 2865408000 | bytes 9988096 | tf_op jit(solution)/shard_map/tf,df->td/dot_general | solution.py:310
  490.5 3.5 add_convert_fusion.4
  494.1 3.1 fusion.95
  500.4 66.9 %reduce-scatter.5.cloned.1.call-done = bf16[64,1792]{1,0:T(8,128)(2,1)} async-done(((bf16[1024,1792]{1,0:T(8,128)(2,1)}), bf16[64,1792]{1,0:T(8,128)(2,1)}) %reduce-scatter.5.cloned.1.call-update) | async-done | bytes 229392 | tf_op jit(solution)/shard_map/reduce_scatter | solution.py:391
  (313 shorter events, 193.9 us)
Async XLA Ops:
  7.2 8.4 %copy-start.9 = (bf16[1025,512]{1,0:T(8,128)(2,1)S(1)}, bf16[1025,512]{1,0:T(8,128)(2,1)}, u32[]{:S(2)}) copy-start(bf16[1025,512]{1,0:T(8,128)(2,1)} %param.23) | copy-start | bytes 3148804
  7.2 6.2 %copy-start.46 = (bf16[512]{0:T(512)(128)(2,1)S(1)}, bf16[512]{0:T(512)(128)(2,1)}, u32[]{:S(2)}) copy-start(bf16[512]{0:T(512)(128)(2,1)} %param.27) | copy-start | bytes 3076
  7.2 6.2 %copy-start.47 = (bf16[512]{0:T(512)(128)(2,1)S(1)}, bf16[512]{0:T(512)(128)(2,1)}, u32[]{:S(2)}) copy-start(bf16[512]{0:T(512)(128)(2,1)} %param.28) | copy-start | bytes 3076
  7.2 84.5 %all-gather.3.cloned.1.call-start = ((), (), s32[]{:S(2)}) async-start(), calls=%async_computation.2 | async-start | bytes 4734976 | tf_op jit(solution)/shard_map/all_gather | solution.py:180
  10.8 197.8 %all-gather.5.cloned.1.call-start = ((), (), s32[]{:S(2)}) async-start(), calls=%async_computation.3 | async-start | bytes 9191424 | tf_op jit(solution)/shard_map/all_gather | solution.py:236
  10.8 4.8 collective-permute-start
  13.3 466.7 %reduce-scatter.3.cloned.1.call-start = ((), (), s32[]{:S(2)}) async-start(), calls=%async_computation.4 | async-start | bytes 10862592 | tf_op jit(solution)/shard_map/reduce_scatter | solution.py:318
  17.0 84.2 %copy-start.4 = (bf16[1025,512]{1,0:T(8,128)(2,1)}, bf16[1025,512]{1,0:T(8,128)(2,1)S(1)}, u32[]{:S(2)}) copy-start(bf16[1025,512]{1,0:T(8,128)(2,1)S(1)} %get-tuple-element.335) | copy-start | bytes 3148804
  17.0 84.2 %copy-start.6 = (bf16[1025,512]{1,0:T(8,128)(2,1)}, bf16[1025,512]{1,0:T(8,128)(2,1)S(1)}, u32[]{:S(2)}) copy-start(bf16[1025,512]{1,0:T(8,128)(2,1)S(1)} %get-tuple-element.336) | copy-start | bytes 3148804
  17.4 83.8 %copy-start.32 = (f32[1025]{0:T(1024)}, f32[1025]{0:T(1024)S(1)}, u32[]{:S(2)}) copy-start(f32[1025]{0:T(1024)S(1)} %broadcast_multiply_fusion.7) | copy-start | bytes 12304
  18.1 83.1 %copy-start.34 = (f32[1025]{0:T(1024)}, f32[1025]{0:T(1024)S(1)}, u32[]{:S(2)}) copy-start(f32[1025]{0:T(1024)S(1)} %add_rsqrt_fusion.2) | copy-start | bytes 12304
  94.6 6.6 %copy-start.38 = (f32[1024]{0:T(1024)}, f32[1024]{0:T(1024)S(1)}, u32[]{:S(2)}) copy-start(f32[1024]{0:T(1024)S(1)} %get-tuple-element.347) | copy-start | bytes 12292
  94.6 6.6 %copy-start.44 = (f32[1024]{0:T(1024)}, f32[1024]{0:T(1024)S(1)}, u32[]{:S(2)}) copy-start(f32[1024]{0:T(1024)S(1)} %get-tuple-element.344) | copy-start | bytes 12292
  183.9 5.9 %copy-start.40 = (bf16[1365]{0:T(1024)(128)(2,1)S(1)}, bf16[1365]{0:T(1024)(128)(2,1)}, u32[]{:S(2)}) copy-start(bf16[1365]{0:T(1024)(128)(2,1)} %param.34) | copy-start | bytes 8194
  183.9 5.9 %copy-start.41 = (bf16[1365]{0:T(1024)(128)(2,1)S(1)}, bf16[1365]{0:T(1024)(128)(2,1)}, u32[]{:S(2)}) copy-start(bf16[1365]{0:T(1024)(128)(2,1)} %param.36) | copy-start | bytes 8194
  183.9 2.9 collective-permute-start.1
  189.2 2.7 collective-permute-start.2
  189.4 39.5 %collective-permute-start.5 = (bf16[1025,512]{1,0:T(8,128)(2,1)}, bf16[1025,512]{1,0:T(8,128)(2,1)}, u32[]{:S(2)}, u32[]{:S(2)}) collective-permute-start(bf16[1025,512]{1,0:T(8,128)(2,1)} %param.41), channel_id=1, source_target_pairs={{0,1},{1,0},{2,3},{3,2},{4,5},{5,4},{6,7},{7,6},{8,9},{9,8},{10,11... | collective-permute-start | bytes 3148808 | tf_op jit(solution)/shard_map/ppermute | solution.py:74
  217.9 6.0 %copy-start.1 = (f32[1025,2816]{1,0:T(8,128)}, f32[1025,2816]{1,0:T(8,128)S(1)}, u32[]{:S(2)}) copy-start(f32[1025,2816]{1,0:T(8,128)S(1)} %fusion.56) | copy-start | bytes 34636804
  217.9 6.0 %copy-start.42 = (bf16[1365]{0:T(1024)(128)(2,1)S(1)}, bf16[1365]{0:T(1024)(128)(2,1)}, u32[]{:S(2)}) copy-start(bf16[1365]{0:T(1024)(128)(2,1)} %param.37) | copy-start | bytes 8194
  217.9 6.1 %copy-start.43 = (bf16[1365]{0:T(1024)(128)(2,1)S(1)}, bf16[1365]{0:T(1024)(128)(2,1)}, u32[]{:S(2)}) copy-start(bf16[1365]{0:T(1024)(128)(2,1)} %param.38) | copy-start | bytes 8194
  224.0 1.2 collective-permute-start.3
  225.2 5.5 copy-start
  228.7 1.9 collective-permute-start.4
  230.6 9.1 %copy-start.20 = (bf16[1025,512]{1,0:T(8,128)(2,1)}, bf16[1025,512]{1,0:T(8,128)(2,1)S(1)}, u32[]{:S(2)}) copy-start(bf16[1025,512]{1,0:T(8,128)(2,1)S(1)} %get-tuple-element.332) | copy-start | bytes 3148804
  239.2 8.2 %collective-permute-start.6 = (f32[1025]{0:T(1024)S(1)}, f32[1025]{0:T(1024)S(1)}, u32[]{:S(2)}, u32[]{:S(2)}) collective-permute-start(f32[1025]{0:T(1024)S(1)} %get-tuple-element.244), channel_id=1, source_target_pairs={{0,1},{1,0},{2,3},{3,2},{4,5},{5,4},{6,7},{7,6},{8,9},{9,8},{10,11... | collective-permute-start | bytes 12308 | tf_op jit(solution)/shard_map/ppermute | solution.py:74
  239.5 7.9 %collective-permute-start.7 = (f32[1025]{0:T(1024)S(1)}, f32[1025]{0:T(1024)S(1)}, u32[]{:S(2)}, u32[]{:S(2)}) collective-permute-start(f32[1025]{0:T(1024)S(1)} %get-tuple-element.239), channel_id=1, source_target_pairs={{0,1},{1,0},{2,3},{3,2},{4,5},{5,4},{6,7},{7,6},{8,9},{9,8},{10,11... | collective-permute-start | bytes 12308 | tf_op jit(solution)/shard_map/ppermute | solution.py:74
  239.7 7.7 %slice-start = ((s8[11624448]{0:T(1024)(128)(4,1)}), s8[4194304]{0:T(1024)(128)(4,1)S(1)}, s32[]{:S(2)}) async-start(s8[11624448]{0:T(1024)(128)(4,1)} %bitcast.199), calls=%async_computation.6 | async-start | bytes 8388608
  239.7 7.7 %slice-start.1 = ((s8[11624448]{0:T(1024)(128)(4,1)}), s8[4194304]{0:T(1024)(128)(4,1)S(1)}, s32[]{:S(2)}) async-start(s8[11624448]{0:T(1024)(128)(4,1)} %bitcast.199), calls=%async_computation.7 | async-start | bytes 8388608
  239.7 7.7 %slice-start.2 = ((s8[11624448]{0:T(1024)(128)(4,1)}), s8[3235840]{0:T(1024)(128)(4,1)S(1)}, s32[]{:S(2)}) async-start(s8[11624448]{0:T(1024)(128)(4,1)} %bitcast.199), calls=%async_computation.8 | async-start | bytes 6471680
  267.5 13.7 %collective-permute-start.8 = (bf16[1025,1024]{1,0:T(8,128)(2,1)S(1)}, bf16[1025,1024]{1,0:T(8,128)(2,1)}, u32[]{:S(2)}, u32[]{:S(2)}) collective-permute-start(bf16[1025,1024]{1,0:T(8,128)(2,1)S(1)} %fusion.76), channel_id=1, source_target_pairs={{0,1},{1,0},{2,3},{3,2},{4,5},{5,4},{6,7},{7,6},{8,9},{9,8},{10,11... | collective-permute-start | bytes 6297608 | tf_op jit(solution)/shard_map/ppermute | solution.py:74
  281.2 11.8 %copy-start.8 = (bf16[1024,4992]{1,0:T(8,128)(2,1)}, bf16[1024,4992]{1,0:T(8,128)(2,1)S(1)}, u32[]{:S(2)}) copy-start(bf16[1024,4992]{1,0:T(8,128)(2,1)S(1)} %pad_dynamic-update-slice_fusion) | copy-start | bytes 30670852
  281.2 5.6 copy-start.21
  293.3 6.4 %copy-start.29 = (bf16[1025,1024]{1,0:T(8,128)(2,1)S(1)}, bf16[1025,1024]{1,0:T(8,128)(2,1)}, u32[]{:S(2)}) copy-start(bf16[1025,1024]{1,0:T(8,128)(2,1)} %get-tuple-element.100) | copy-start | bytes 6297604
  303.5 263.8 %reduce-scatter.5.cloned.1.call-start = ((), (), s32[]{:S(2)}) async-start(), calls=%async_computation.5 | async-start | bytes 3899392 | tf_op jit(solution)/shard_map/reduce_scatter | solution.py:391
  305.2 100.9 %copy-start.25 = (f32[1025,64]{0,1:T(8,128)S(1)}, f32[1025,64]{0,1:T(8,128)}, u32[]{:S(2)}) copy-start(f32[1025,64]{0,1:T(8,128)} %get-tuple-element.104) | copy-start | bytes 787204
  430.6 5.3 copy-start.19
  430.7 5.3 copy-start.5
  430.7 5.3 copy-start.7
  430.7 5.3 copy-start.33
  435.7 13.9 %collective-permute-start.10 = (bf16[1025,1024]{1,0:T(8,128)(2,1)}, bf16[1025,1024]{1,0:T(8,128)(2,1)}, u32[]{:S(2)}, u32[]{:S(2)}) collective-permute-start(bf16[1025,1024]{1,0:T(8,128)(2,1)} %fusion.75), channel_id=1, source_target_pairs={{0,1},{1,0},{2,3},{3,2},{4,5},{5,4},{6,7},{7,6},{8,9},{9,8},{10,11... | collective-permute-start | bytes 6297608 | tf_op jit(solution)/shard_map/ppermute | solution.py:74
  481.2 12.8 %slice-start.5 = ((s8[4227072]{0:T(1024)(128)(4,1)}), s8[32768]{0:T(1024)(128)(4,1)S(1)}, s32[]{:S(2)}) async-start(s8[4227072]{0:T(1024)(128)(4,1)} %bitcast.207), calls=%async_computation.11 | async-start | bytes 65536
  481.2 6.6 %copy-start.31 = (f32[1024,1]{1,0:T(8,128)S(1)}, f32[1024,1]{1,0:T(8,128)}, u32[]{:S(2)}) copy-start(f32[1024,1]{1,0:T(8,128)} %get-tuple-element.342) | copy-start | bytes 12292
  481.2 9.3 %copy-start.37 = (f32[512]{0:T(512)S(1)}, f32[512]{0:T(512)}, u32[]{:S(2)}) copy-start(f32[512]{0:T(512)} %copy-done.36) | copy-start | bytes 6148
  481.2 12.8 %slice-start.6 = ((s8[4227072]{0:T(1024)(128)(4,1)}), s8[4194304]{0:T(1024)(128)(4,1)S(1)}, s32[]{:S(2)}) async-start(s8[4227072]{0:T(1024)(128)(4,1)} %bitcast.207), calls=%async_computation.12 | async-start | bytes 8388608
  487.8 2.7 collective-permute-start.9
  487.9 6.2 %slice-start.3 = ((s8[4227072]{0:T(1024)(128)(4,1)}), s8[4194304]{0:T(1024)(128)(4,1)S(1)}, s32[]{:S(2)}) async-start(s8[4227072]{0:T(1024)(128)(4,1)} %bitcast.205), calls=%async_computation.9 | async-start | bytes 8388608
  488.0 6.0 %slice-start.4 = ((s8[4227072]{0:T(1024)(128)(4,1)}), s8[32768]{0:T(1024)(128)(4,1)S(1)}, s32[]{:S(2)}) async-start(s8[4227072]{0:T(1024)(128)(4,1)} %bitcast.205), calls=%async_computation.10 | async-start | bytes 65536
  (22 other events, 81.9 us)
Sparse Core Ops, SparseCore 0:
  11.4 80.3 all-gather.2
  95.1 113.3 all-gather.4
  303.7 176.3 reduce-scatter.2
  482.2 85.1 reduce-scatter.4

commit v9 on v6

--- a/solution.py
+++ b/solution.py
@@ -89,10 +89,11 @@
 
 def gather_columns(values):
     other = swap_columns(values)
-    first = lax.axis_index("col") == 0
-    return jnp.concatenate(
-        [jnp.where(first, values, other), jnp.where(first, other, values)], axis=1
-    )
+    half = values.shape[1]
+    column = lax.axis_index("col")
+    full = jnp.zeros((values.shape[0], 2 * half), values.dtype)
+    full = lax.dynamic_update_slice_in_dim(full, values, column * half, axis=1)
+    return lax.dynamic_update_slice_in_dim(full, other, (1 - column) * half, axis=1)
 
 
 def hidden_totals(row_sums):

time: 588 us -> 596 us (1.014)
  waiting for transfers between devices: 183 us -> 190 us
    all_gather x1, waiting for transfers between devices: 14.6 us -> 21.7 us  [body(): ffn_full = lax.all_gather(ffn_pack, 'row', axis=0, tiled=True)]
  transfers between devices with their start and end apart: 15 -> 15, of which waited for: 7 -> 7; matrix products, arithmetic and copies ran while one was open for 54% -> 53% of each run, Pallas kernels for 0% -> 0%
where the time goes in v9:
time: 596 us; the launch traced here: 584 us
  matrix products  203 us (34%)
  waiting for transfers between devices  190 us (32%)
  other arithmetic  93.5 us (16%)
  local copies, waits for them, and re-layouts  77.6 us (13%)
  between operations  15.1 us (3%)
    all_gather x1, waiting for transfers between devices, body(): attn_full = lax.all_gather(attn_pack, 'row', axis=0, tiled=True)  73.1 us
    reduce_scatter x1, waiting for transfers between devices, body(): lax.psum_scatter(end_pack, 'row', scatter_dimension=0, tiled=True)  66.9 us
    all_gather x1, waiting for transfers between devices, body(): ffn_full = lax.all_gather(ffn_pack, 'row', axis=0, tiled=True)  21.7 us
    reduce_scatter x1, waiting for transfers between devices, body(): lax.psum_scatter(mid_pack, 'row', scatter_dimension=0, tiled=True)  21.2 us
    dot_general x8, matrix products, attend(): jnp.einsum('qk,kd->qd', weights.astype(narrow), value_block, preferred_el...  20.9 us
    dot_general x8, matrix products, attend_back(): jnp.einsum('qk,qd->kd', weights.astype(narrow), grad_block, preferred_ele...  20.3 us
    dot_general x8, matrix products, attend_back(): jnp.einsum('qk,qd->kd', score_grad, query_block, preferred_element_type=s...  20.2 us
    dot_general x8, matrix products, attend_back(): jnp.einsum('qd,kd->qk', grad_block, value_block, preferred_element_type=s...  17.6 us
  transfers between devices with their start and end apart: 15, of which 7 were waited for; matrix products, arithmetic and copies ran while one was open for 53% of the time, Pallas kernels for 0%

profile of v9, /device:TPU:0, one launch (start us, length us, event | category | flops | bytes accessed | tf_op | source)
XLA Modules:
  0.0 584.0 jit_solution(12025009597534203599)
XLA Ops:
  18.6 73.1 %all-gather.3.cloned.1.call-done = bf16[1024,2176]{1,0:T(8,128)(2,1)} async-done(((bf16[64,2176]{1,0:T(8,128)(2,1)}), bf16[1024,2176]{1,0:T(8,128)(2,1)}) %all-gather.3.cloned.1.call-update) | async-done | bytes 4456464 | tf_op jit(solution)/shard_map/all_gather | solution.py:181
  96.8 4.7 copy.166
  101.5 6.1 %convolution_add_fusion = f32[1025,3,512]{2,0,1:T(8,128)S(1)} fusion(bf16[1024,3,512]{0,2,1:T(8,128)(2,1)} %bitcast.219, f32[3,512]{1,0:T(4,128)S(1)} %pad_maximum_fusion.5, f32[1024]{0:T(1024)S(1)} %get-tuple-element.335, f32[1024]{0:T(1024)S(1)} %get-tuple-element.334, bf16[1025,1024]{1,0:T(8,128)(2,1)S(1)} %constant_dynamic-update-slice_fusion.4, ...), kind=kOutput, calls=%fused_computation.75 | convolution fusion | flops 3232243200 | bytes 11565064 | tf_op jit(solution)/shard_map/td,dpe->tpe/dot_general | solution.py:198
  113.2 3.0 copy.170
  120.6 2.9 copy.173
  123.5 3.7 copy.174
  129.5 3.7 copy.175
  133.2 41.9 %while.24 = (s32[]{:T(128)}, bf16[8,1025,64]{1,2,0:T(8,128)(2,1)}, bf16[8,1025,64]{2,1,0:T(8,128)(2,1)S(1)}, bf16[8,1025,64]{2,1,0:T(8,128)(2,1)}, bf16[8,1025,64]{2,1,0:T(8,128)(2,1)}, /*index=5*/s32[]{:T(128)}) while((s32[]{:T(128)}, bf16[8,1025,64]{1,2,0:T(8,128)(2,1)}, bf16[8,1025,64]{2,1,0:T(8,128)(2,1)S(1)}, ...), condition=%wide.region_5.6_spmd, body=%wide.region_2.5_spmd.sunk | while | flops 276377920 | bytes 13570149 | solution.py:220
  135.7 2.6 fusion.193
  140.9 2.6 fusion.193
  146.1 2.6 fusion.193
  151.3 2.6 fusion.193
  156.5 2.7 fusion.193
  161.7 2.6 fusion.193
  166.9 2.6 fusion.193
  172.1 2.6 fusion.193
  175.1 3.9 fusion.108
  186.8 21.7 %all-gather.5.cloned.1.call-done = bf16[1024,4224]{1,0:T(8,128)(2,1)} async-done(((bf16[64,4224]{1,0:T(8,128)(2,1)}), bf16[1024,4224]{1,0:T(8,128)(2,1)}) %all-gather.5.cloned.1.call-update) | async-done | bytes 8650768 | tf_op jit(solution)/shard_map/all_gather | solution.py:237
  208.5 9.4 %fusion.56 = f32[1025,2816]{1,0:T(8,128)S(1)} fusion(bf16[1024,4224]{1,0:T(8,128)(2,1)} %all-gather.5.cloned.1.call-done, bf16[1025,1024]{1,0:T(8,128)(2,1)S(1)} %constant_dynamic-update-slice_fusion.2, f32[1024]{0:T(1024)S(1)} %get-tuple-element.336, f32[1024]{0:T(1024)S(1)} %get-tuple-element.337, f32[1025]{0:T(1024)S(1)} %add_rsqrt_fusion.1, ...), kind=kOutput, calls=%fused_computation.84 | convolution fusion | flops 5917644800 | bytes 19428360 | tf_op jit(solution)/shard_map/dot_general | solution.py:245
  217.9 4.5 fusion.153
  229.7 3.1 copy.183
  232.8 3.4 multiply_reduce_fusion.3
  238.0 9.0 %multiply_reduce_fusion.1 = (bf16[1365]{0:T(1024)(128)(2,1)S(1)}, f32[1025]{0:T(1024)S(1)}, f32[1025]{0:T(1024)S(1)}, bf16[1365]{0:T(1024)(128)(2,1)S(1)}, bf16[...) fusion(f32[1025,1365]{1,0:T(8,128)} %get-tuple-element.293, f32[1025]{0:T(1024)S(1)} %add_rsqrt_fusion, ...), kind=kOutput, calls=%fused_computation.65 | convolution fusion | flops 2882191872 | bytes 19236874 | tf_op jit(solution)/shard_map/td,df->tf/dot_general | solution.py:264
  247.6 7.9 %convolution_convert_fusion = bf16[1024,1365]{1,0:T(8,128)(2,1)} fusion(bf16[1025,1024]{1,0:T(8,128)(2,1)} %constant_dynamic-update-slice_fusion, bf16[1025,1365]{1,0:T(8,128)(2,1)S(1)} %get-tuple-element.96), kind=kOutput, calls=%fused_computation.111 | convolution fusion | flops 2866805760 | bytes 7692970 | tf_op jit(solution)/shard_map/td,tf->df/dot_general | solution.py:260
  255.6 9.4 %fusion.150 = (bf16[1365]{0:T(1024)(128)(2,1)S(1)}, bf16[1025,1365]{1,0:T(8,128)(2,1)}, bf16[1365]{0:T(1024)(128)(2,1)S(1)}, bf16[1025,1365]{1,0:T(8,128)(2,1)}) fusion(f32[1365]{0:T(1024)S(1)} %convert_element_type.236, f32[1025,2816]{1,0:T(8,128)S(1)} %bitcast.204, f32[1365]{0:T(1024)S(1)} %convert_element_type.237, f32[1025]{0:T(1024)S(1)} %add_multiply_fusion, ...), kind=kLoop, calls=%fused_computation.262 | loop fusion | flops 33576260 | bytes 28020740 | tf_op jit(solution)/shard_map/reduce_sum | solution.py:278
  265.3 10.2 %fusion.76 = bf16[1025,1024]{1,0:T(8,128)(2,1)S(1)} fusion(bf16[1024,4224]{1,0:T(8,128)(2,1)} %all-gather.5.cloned.1.call-done, bf16[1025,1365]{1,0:T(8,128)(2,1)} %get-tuple-element.303, bf16[1025,1365]{1,0:T(8,128)(2,1)} %get-tuple-element.288), kind=kOutput, calls=%fused_computation.110 | convolution fusion | flops 5935488000 | bytes 13678592 | tf_op jit(solution)/shard_map/tf,df->td/dot_general | solution.py:285
  275.6 10.6 %convert_dynamic-update-slice_fusion = bf16[1024,4992]{1,0:T(8,128)(2,1)S(1)} fusion(bf16[1025,1365]{1,0:T(8,128)(2,1)S(1)} %copy-done.19, bf16[1025,1365]{1,0:T(8,128)(2,1)S(1)} %copy-done.18, bf16[1025,1024]{1,0:T(8,128)(2,1)S(1)} %constant_dynamic-update-slice_fusion.2, f32[1024]{0:T(1024)S(1)} %get-tuple-element.336, f32[1024]{0:T(1024)S(1)} %get-tuple-element.337, ...), kind=kOutput, calls=%fused_computation.74 | convolution fusion | flops 5943619584 | bytes 13479260 | tf_op jit(solution)/shard_map/td,tf->df/dot_general | solution.py:281
  290.7 7.2 %fusion.151 = (bf16[1024]{0:T(1024)(128)(2,1)S(1)}, bf16[1025,1024]{1,0:T(8,128)(2,1)}, f32[1025,1024]{1,0:T(8,128)}, bf16[1024]{0:T(1024)(128)(2,1)S(1)}) fusion(f32[1025]{0:T(1024)S(1)} %broadcast_multiply_fusion.4, f32[1025]{0:T(1024)S(1)} %broadcast_multiply_fusion.6, bf16[1025,1024]{1,0:T(8,128)(2,1)S(1)} %constant_dynamic-update-slice_fusion.2, ...), kind=kLoop, calls=%fused_computation.263 | loop fusion | flops 16791552 | bytes 14718992 | tf_op jit(solution)/shard_map/reduce_sum | solution.py:292
  298.2 4.7 fusion.98
  310.0 101.4 %while.25 = (s32[]{:T(128)}, f32[8,1025,64]{1,2,0:T(8,128)S(1)}, f32[8,1025,64]{1,2,0:T(8,128)}, bf16[8,1025,64]{1,2,0:T(8,128)(2,1)}, bf16[8,1025,64]{2,1,0:T(8...) while((s32[]{:T(128)}, f32[8,1025,64]{1,2,0:T(8,128)S(1)}, ...), condition=%wide.region_26.27_spmd, body=%wide.region_22.26_spmd.sunk | while | flops 689338112 | bytes 38548648 | solution.py:348
  325.7 2.5 fusion.204
  331.6 2.6 fusion.203
  338.4 2.6 fusion.204
  363.6 2.5 fusion.204
  401.5 2.5 fusion.204
  411.5 4.2 bitcast_multiply_fusion.1
  421.8 3.2 copy.182
  428.8 5.0 add_convert_fusion.3
  433.9 4.9 fusion.75
  439.3 6.4 %convolution_convert_fusion.2 = bf16[1024,3,512]{0,2,1:T(8,128)(2,1)} fusion(f32[1024]{0:T(1024)S(1)} %copy-done.42, f32[1024]{0:T(1024)S(1)} %copy-done.36, bf16[1025,1,512]{2,0,1:T(8,128)(2,1)S(1)} %copy-done.14, bf16[1025,1,512]{2,0,1:T(8,128)(2,1)S(1)} %get-tuple-element.325, bf16[1025,1,512]{2,0,1:T(8,128)(2,1)S(1)} %get-tuple-element.324, ...), kind=kOutput, calls=%fused_computation.136 | convolution fusion | flops 3241688064 | bytes 8410120 | tf_op jit(solution)/shard_map/td,tpe->dpe/dot_general | solution.py:369
  445.8 4.6 copy.190
  453.0 6.4 %fusion.147 = (f32[1025]{0:T(1024)S(1)}, f32[1025]{0:T(1024)S(1)}, bf16[1024]{0:T(1024)(128)(2,1)S(1)}, bf16[1024]{0:T(1024)(128)(2,1)S(1)}, f32[1025,1024]{1,0:T(8,128)}, /*index=5*/f32[1025,1024]{1,0:T(8,128)}) fusion(f32[1025]{0:T(1024)S(1)} %copy-done.32, f32[1025]{0:T(1024)S(1)} %copy-done.30, bf16[1025,1024]{1,0:T(8,128)(2,1)S(1)} %copy-done.2, ...), kind=kLoop, calls=%fused_computation.260 | loop fusion | flops 13640702 | bytes 14718992 | tf_op jit(solution)/shard_map/reduce_sum | solution.py:31
  459.7 3.6 fusion.84
  463.3 21.2 %reduce-scatter.3.cloned.1.call-done = bf16[64,4992]{1,0:T(8,128)(2,1)} async-done(((bf16[1024,4992]{1,0:T(8,128)(2,1)}), bf16[64,4992]{1,0:T(8,128)(2,1)}) %reduce-scatter.3.cloned.1.call-update) | async-done | bytes 638992 | tf_op jit(solution)/shard_map/reduce_scatter | solution.py:319
  485.7 6.3 %fusion.86 = f32[1025,1024]{1,0:T(8,128)S(1)} fusion(bf16[1025,1365]{1,0:T(8,128)(2,1)} %copy-done.45, bf16[1024,4224]{1,0:T(8,128)(2,1)} %all-gather.5.cloned.1.call-done), kind=kOutput, calls=%fused_computation.122 | convolution fusion | flops 2865408000 | bytes 9988096 | tf_op jit(solution)/shard_map/tf,df->td/dot_general | solution.py:311
  495.0 3.5 add_convert_fusion.4
  498.5 3.1 fusion.95
  504.9 66.9 %reduce-scatter.5.cloned.1.call-done = bf16[64,1792]{1,0:T(8,128)(2,1)} async-done(((bf16[1024,1792]{1,0:T(8,128)(2,1)}), bf16[64,1792]{1,0:T(8,128)(2,1)}) %reduce-scatter.5.cloned.1.call-update) | async-done | bytes 229392 | tf_op jit(solution)/shard_map/reduce_scatter | solution.py:389
  (319 shorter events, 192.6 us)
Async XLA Ops:
  7.2 6.2 %copy-start.43 = (bf16[512]{0:T(512)(128)(2,1)S(1)}, bf16[512]{0:T(512)(128)(2,1)}, u32[]{:S(2)}) copy-start(bf16[512]{0:T(512)(128)(2,1)} %param.27) | copy-start | bytes 3076
  7.2 6.2 %copy-start.44 = (bf16[512]{0:T(512)(128)(2,1)S(1)}, bf16[512]{0:T(512)(128)(2,1)}, u32[]{:S(2)}) copy-start(bf16[512]{0:T(512)(128)(2,1)} %param.28) | copy-start | bytes 3076
  7.2 84.5 %all-gather.3.cloned.1.call-start = ((), (), s32[]{:S(2)}) async-start(), calls=%async_computation.2 | async-start | bytes 4734976 | tf_op jit(solution)/shard_map/all_gather | solution.py:181
  7.3 8.6 %copy-start.6 = (bf16[1025,512]{1,0:T(8,128)(2,1)S(1)}, bf16[1025,512]{1,0:T(8,128)(2,1)}, u32[]{:S(2)}) copy-start(bf16[1025,512]{1,0:T(8,128)(2,1)} %param.23) | copy-start | bytes 3148804
  10.8 197.7 %all-gather.5.cloned.1.call-start = ((), (), s32[]{:S(2)}) async-start(), calls=%async_computation.3 | async-start | bytes 9191424 | tf_op jit(solution)/shard_map/all_gather | solution.py:237
  10.8 5.2 collective-permute-start
  13.3 471.1 %reduce-scatter.3.cloned.1.call-start = ((), (), s32[]{:S(2)}) async-start(), calls=%async_computation.4 | async-start | bytes 10862592 | tf_op jit(solution)/shard_map/reduce_scatter | solution.py:319
  17.4 84.1 %copy-start.1 = (bf16[1025,1024]{1,0:T(8,128)(2,1)}, bf16[1025,1024]{1,0:T(8,128)(2,1)S(1)}, u32[]{:S(2)}) copy-start(bf16[1025,1024]{1,0:T(8,128)(2,1)S(1)} %constant_dynamic-update-slice_fusion.4) | copy-start | bytes 6297604
  17.8 83.7 %copy-start.29 = (f32[1025]{0:T(1024)}, f32[1025]{0:T(1024)S(1)}, u32[]{:S(2)}) copy-start(f32[1025]{0:T(1024)S(1)} %broadcast_multiply_fusion.7) | copy-start | bytes 12304
  18.6 82.9 %copy-start.31 = (f32[1025]{0:T(1024)}, f32[1025]{0:T(1024)S(1)}, u32[]{:S(2)}) copy-start(f32[1025]{0:T(1024)S(1)} %add_rsqrt_fusion.2) | copy-start | bytes 12304
  94.9 6.6 %copy-start.35 = (f32[1024]{0:T(1024)}, f32[1024]{0:T(1024)S(1)}, u32[]{:S(2)}) copy-start(f32[1024]{0:T(1024)S(1)} %get-tuple-element.334) | copy-start | bytes 12292
  94.9 6.6 %copy-start.41 = (f32[1024]{0:T(1024)}, f32[1024]{0:T(1024)S(1)}, u32[]{:S(2)}) copy-start(f32[1024]{0:T(1024)S(1)} %get-tuple-element.335) | copy-start | bytes 12292
  179.2 2.7 collective-permute-start.1
  182.9 2.7 collective-permute-start.2
  183.0 53.8 %collective-permute-start.5 = (bf16[1025,512]{1,0:T(8,128)(2,1)}, bf16[1025,512]{1,0:T(8,128)(2,1)S(1)}, u32[]{:S(2)}, u32[]{:S(2)}) collective-permute-start(bf16[1025,512]{1,0:T(8,128)(2,1)} %param.41), channel_id=1, source_target_pairs={{0,1},{1,0},{2,3},{3,2},{4,5},{5,4},{6,7},{7,6},{8,9},{9,8},{10,11... | collective-permute-start | bytes 3148808 | tf_op jit(solution)/shard_map/ppermute | solution.py:74
  217.9 6.3 %copy-start = (f32[1025,2816]{1,0:T(8,128)}, f32[1025,2816]{1,0:T(8,128)S(1)}, u32[]{:S(2)}) copy-start(f32[1025,2816]{1,0:T(8,128)S(1)} %fusion.56) | copy-start | bytes 34636804
  224.1 8.7 %collective-permute-start.3 = (f32[1025]{0:T(1024)S(1)}, f32[1025]{0:T(1024)S(1)}, u32[]{:S(2)}, u32[]{:S(2)}) collective-permute-start(f32[1025]{0:T(1024)S(1)} %get-tuple-element.292), channel_id=1, source_target_pairs={{0,1},{1,0},{2,3},{3,2},{4,5},{5,4},{6,7},{7,6},{8,9},{9,8},{10,11... | collective-permute-start | bytes 12308 | tf_op jit(solution)/shard_map/ppermute | solution.py:74
  236.2 1.7 collective-permute-start.4
  238.0 17.5 %slice-start.2 = ((s8[11624448]{0:T(1024)(128)(4,1)}), s8[4194304]{0:T(1024)(128)(4,1)S(1)}, s32[]{:S(2)}) async-start(s8[11624448]{0:T(1024)(128)(4,1)} %bitcast.203), calls=%async_computation.8 | async-start | bytes 8388608
  238.0 17.5 %slice-start.3 = ((s8[11624448]{0:T(1024)(128)(4,1)}), s8[4194304]{0:T(1024)(128)(4,1)S(1)}, s32[]{:S(2)}) async-start(s8[11624448]{0:T(1024)(128)(4,1)} %bitcast.203), calls=%async_computation.9 | async-start | bytes 8388608
  247.0 8.5 %copy-start.45 = (bf16[1025,1365]{1,0:T(8,128)(2,1)}, bf16[1025,1365]{1,0:T(8,128)(2,1)S(1)}, u32[]{:S(2)}) copy-start(bf16[1025,1365]{1,0:T(8,128)(2,1)S(1)} %get-tuple-element.96) | copy-start | bytes 8394754
  247.0 8.5 %collective-permute-start.6 = (f32[1025]{0:T(1024)S(1)}, f32[1025]{0:T(1024)S(1)}, u32[]{:S(2)}, u32[]{:S(2)}) collective-permute-start(f32[1025]{0:T(1024)S(1)} %get-tuple-element.238), channel_id=1, source_target_pairs={{0,1},{1,0},{2,3},{3,2},{4,5},{5,4},{6,7},{7,6},{8,9},{9,8},{10,11... | collective-permute-start | bytes 12308 | tf_op jit(solution)/shard_map/ppermute | solution.py:74
  247.1 8.4 %collective-permute-start.7 = (f32[1025]{0:T(1024)S(1)}, f32[1025]{0:T(1024)S(1)}, u32[]{:S(2)}, u32[]{:S(2)}) collective-permute-start(f32[1025]{0:T(1024)S(1)} %get-tuple-element.233), channel_id=1, source_target_pairs={{0,1},{1,0},{2,3},{3,2},{4,5},{5,4},{6,7},{7,6},{8,9},{9,8},{10,11... | collective-permute-start | bytes 12308 | tf_op jit(solution)/shard_map/ppermute | solution.py:74
  247.6 7.9 %slice-start = ((s8[5812224]{0:T(1024)(128)(4,1)}), s8[4194304]{0:T(1024)(128)(4,1)S(1)}, s32[]{:S(2)}) async-start(s8[5812224]{0:T(1024)(128)(4,1)} %bitcast.201), calls=%async_computation.6 | async-start | bytes 8388608
  247.6 8.0 %slice-start.1 = ((s8[5812224]{0:T(1024)(128)(4,1)}), s8[1617920]{0:T(1024)(128)(4,1)S(1)}, s32[]{:S(2)}) async-start(s8[5812224]{0:T(1024)(128)(4,1)} %bitcast.201), calls=%async_computation.7 | async-start | bytes 3235840
  247.6 8.0 %slice-start.4 = ((s8[11624448]{0:T(1024)(128)(4,1)}), s8[3235840]{0:T(1024)(128)(4,1)S(1)}, s32[]{:S(2)}) async-start(s8[11624448]{0:T(1024)(128)(4,1)} %bitcast.203), calls=%async_computation.10 | async-start | bytes 6471680
  265.3 10.3 %copy-start.18 = (bf16[1025,1365]{1,0:T(8,128)(2,1)S(1)}, bf16[1025,1365]{1,0:T(8,128)(2,1)}, u32[]{:S(2)}) copy-start(bf16[1025,1365]{1,0:T(8,128)(2,1)} %get-tuple-element.288) | copy-start | bytes 8394754
  265.3 10.3 %copy-start.19 = (bf16[1025,1365]{1,0:T(8,128)(2,1)S(1)}, bf16[1025,1365]{1,0:T(8,128)(2,1)}, u32[]{:S(2)}) copy-start(bf16[1025,1365]{1,0:T(8,128)(2,1)} %get-tuple-element.303) | copy-start | bytes 8394754
  275.5 13.0 %collective-permute-start.8 = (bf16[1025,1024]{1,0:T(8,128)(2,1)S(1)}, bf16[1025,1024]{1,0:T(8,128)(2,1)S(1)}, u32[]{:S(2)}, u32[]{:S(2)}) collective-permute-start(bf16[1025,1024]{1,0:T(8,128)(2,1)S(1)} %fusion.76), channel_id=1, source_target_pairs={{0,1},{1,0},{2,3},{3,2},{4,5},{5,4},{6,7},{7,6},{8,9},{9,8},{10,11... | collective-permute-start | bytes 6297608 | tf_op jit(solution)/shard_map/ppermute | solution.py:74
  288.4 9.4 %copy-start.5 = (bf16[1024,4992]{1,0:T(8,128)(2,1)}, bf16[1024,4992]{1,0:T(8,128)(2,1)S(1)}, u32[]{:S(2)}) copy-start(bf16[1024,4992]{1,0:T(8,128)(2,1)S(1)} %pad_dynamic-update-slice_fusion) | copy-start | bytes 30670852
  298.2 6.3 %copy-start.25 = (bf16[1025,1024]{1,0:T(8,128)(2,1)S(1)}, bf16[1025,1024]{1,0:T(8,128)(2,1)}, u32[]{:S(2)}) copy-start(bf16[1025,1024]{1,0:T(8,128)(2,1)} %get-tuple-element.97) | copy-start | bytes 6297604
  308.4 263.4 %reduce-scatter.5.cloned.1.call-start = ((), (), s32[]{:S(2)}) async-start(), calls=%async_computation.5 | async-start | bytes 3899392 | tf_op jit(solution)/shard_map/reduce_scatter | solution.py:389
  310.0 101.4 %copy-start.21 = (f32[1025,64]{0,1:T(8,128)S(1)}, f32[1025,64]{0,1:T(8,128)}, u32[]{:S(2)}) copy-start(f32[1025,64]{0,1:T(8,128)} %get-tuple-element.343) | copy-start | bytes 787204
  428.8 5.0 copy-start.17
  433.8 5.5 copy-start.13
  433.9 5.5 copy-start.2
  433.9 5.5 copy-start.30
  433.9 5.4 copy-start.32
  433.9 5.4 copy-start.36
  433.9 5.4 copy-start.42
  438.9 14.1 %collective-permute-start.10 = (bf16[1025,1024]{1,0:T(8,128)(2,1)}, bf16[1025,1024]{1,0:T(8,128)(2,1)}, u32[]{:S(2)}, u32[]{:S(2)}) collective-permute-start(bf16[1025,1024]{1,0:T(8,128)(2,1)} %fusion.75), channel_id=1, source_target_pairs={{0,1},{1,0},{2,3},{3,2},{4,5},{5,4},{6,7},{7,6},{8,9},{9,8},{10,11... | collective-permute-start | bytes 6297608 | tf_op jit(solution)/shard_map/ppermute | solution.py:74
  485.6 12.8 %slice-start.7 = ((s8[4227072]{0:T(1024)(128)(4,1)}), s8[32768]{0:T(1024)(128)(4,1)S(1)}, s32[]{:S(2)}) async-start(s8[4227072]{0:T(1024)(128)(4,1)} %bitcast.211), calls=%async_computation.13 | async-start | bytes 65536
  485.7 6.6 %copy-start.27 = (f32[1024,1]{1,0:T(8,128)S(1)}, f32[1024,1]{1,0:T(8,128)}, u32[]{:S(2)}) copy-start(f32[1024,1]{1,0:T(8,128)} %get-tuple-element.332) | copy-start | bytes 12292
  485.7 9.3 %copy-start.34 = (f32[512]{0:T(512)S(1)}, f32[512]{0:T(512)}, u32[]{:S(2)}) copy-start(f32[512]{0:T(512)} %copy-done.33) | copy-start | bytes 6148
  485.7 12.8 %slice-start.8 = ((s8[4227072]{0:T(1024)(128)(4,1)}), s8[4194304]{0:T(1024)(128)(4,1)S(1)}, s32[]{:S(2)}) async-start(s8[4227072]{0:T(1024)(128)(4,1)} %bitcast.211), calls=%async_computation.14 | async-start | bytes 8388608
  492.2 2.7 collective-permute-start.9
  492.3 6.2 %slice-start.5 = ((s8[4227072]{0:T(1024)(128)(4,1)}), s8[4194304]{0:T(1024)(128)(4,1)S(1)}, s32[]{:S(2)}) async-start(s8[4227072]{0:T(1024)(128)(4,1)} %bitcast.209), calls=%async_computation.11 | async-start | bytes 8388608
  492.5 6.0 %slice-start.6 = ((s8[4227072]{0:T(1024)(128)(4,1)}), s8[32768]{0:T(1024)(128)(4,1)S(1)}, s32[]{:S(2)}) async-start(s8[4227072]{0:T(1024)(128)(4,1)} %bitcast.209), calls=%async_computation.12 | async-start | bytes 65536
  (22 other events, 64.8 us)
Sparse Core Ops, SparseCore 0:
  11.3 80.3 all-gather.2
  95.1 113.3 all-gather.4
  308.5 175.9 reduce-scatter.2
  486.6 85.0 reduce-scatter.4

commit v10 on v6

--- a/solution.py
+++ b/solution.py
@@ -236,6 +236,7 @@
     ffn_full = lax.all_gather(ffn_pack, "row", axis=0, tiled=True)
     gate_up_full = ffn_full[:, : ffn_at[2]]
     down_t = ffn_full[:, ffn_at[2] : ffn_at[2] + ff_local]
+    down_t_padded = ffn_full[:, ffn_at[2] : ffn_at[2] + lane_round(ff_local)]
 
     second_out, normed_two, inv_std_two = norm_forward(
         residual_full, ffn_vectors[:, 0], ffn_vectors[:, 1]
@@ -254,10 +255,11 @@
     down_input = (hidden_normed * inner_gain.astype(single) + inner_bias.astype(single)).astype(
         narrow
     )
+    down_padded = jnp.pad(down_input, ((0, 0), (0, lane_round(ff_local) - ff_local)))
     out_full = gather_columns(cotangent)
     out_float = out_full.astype(single)
     down_weight_grad_t = jnp.einsum(
-        "td,tf->df", out_full, down_input, preferred_element_type=single
+        "td,tf->df", out_full, down_padded, preferred_element_type=single
     )
     down_bias_grad = jnp.sum(out_float, axis=0)
     normed_grad = jnp.einsum("td,df->tf", out_full, down_t, preferred_element_type=single)
@@ -305,10 +307,10 @@
         ]
     )
     mid_pack, attn_grad_held, down_input_held = lax.optimization_barrier(
-        (mid_pack, attn_grad, down_input)
+        (mid_pack, attn_grad, down_padded)
     )
     ffn_partial = jnp.einsum(
-        "tf,df->td", down_input_held, down_t, preferred_element_type=single
+        "tf,df->td", down_input_held, down_t_padded, preferred_element_type=single
     )
     layer_out = (
         residual_half

time: 588 us -> 596 us (1.014)
  transfers between devices with their start and end apart: 15 -> 15, of which waited for: 7 -> 8; matrix products, arithmetic and copies ran while one was open for 54% -> 53% of each run, Pallas kernels for 0% -> 0%
where the time goes in v10:
time: 596 us; the launch traced here: 584 us
  matrix products  204 us (34%)
  waiting for transfers between devices  184 us (31%)
  other arithmetic  99.2 us (17%)
  local copies, waits for them, and re-layouts  78.1 us (13%)
  between operations  15.2 us (3%)
    all_gather x1, waiting for transfers between devices, body(): attn_full = lax.all_gather(attn_pack, 'row', axis=0, tiled=True)  73.6 us
    reduce_scatter x1, waiting for transfers between devices, body(): lax.psum_scatter(end_pack, 'row', scatter_dimension=0, tiled=True)  66.5 us
    reduce_scatter x1, waiting for transfers between devices, body(): lax.psum_scatter(mid_pack, 'row', scatter_dimension=0, tiled=True)  21.1 us
    dot_general x8, matrix products, attend(): jnp.einsum('qk,kd->qd', weights.astype(narrow), value_block, preferred_el...  20.9 us
    dot_general x8, matrix products, attend_back(): jnp.einsum('qk,qd->kd', weights.astype(narrow), grad_block, preferred_ele...  20.3 us
    dot_general x8, matrix products, attend_back(): jnp.einsum('qk,qd->kd', score_grad, query_block, preferred_element_type=s...  20.1 us
    dot_general x8, matrix products, attend_back(): jnp.einsum('qd,kd->qk', grad_block, value_block, preferred_element_type=s...  17.6 us
    dot_general x8, matrix products, attend_back(): jnp.einsum('qd,kd->qk', query_block, key_block, preferred_element_type=si...  15.6 us
  transfers between devices with their start and end apart: 15, of which 8 were waited for; matrix products, arithmetic and copies ran while one was open for 53% of the time, Pallas kernels for 0%

profile of v10, /device:TPU:0, one launch (start us, length us, event | category | flops | bytes accessed | tf_op | source)
XLA Modules:
  0.0 584.4 jit_solution(4747130689787797455)
XLA Ops:
  18.1 73.6 %all-gather.3.cloned.1.call-done = bf16[1024,2176]{1,0:T(8,128)(2,1)} async-done(((bf16[64,2176]{1,0:T(8,128)(2,1)}), bf16[1024,2176]{1,0:T(8,128)(2,1)}) %all-gather.3.cloned.1.call-update) | async-done | bytes 4456464 | tf_op jit(solution)/shard_map/all_gather | solution.py:180
  96.5 4.7 copy.166
  101.2 6.1 %convolution_add_fusion = f32[1025,3,512]{2,0,1:T(8,128)S(1)} fusion(bf16[1024,3,512]{0,2,1:T(8,128)(2,1)} %bitcast.212, f32[3,512]{1,0:T(4,128)S(1)} %pad_maximum_fusion.8, f32[1024]{0:T(1024)S(1)} %get-tuple-element.338, f32[1024]{0:T(1024)S(1)} %get-tuple-element.341, f32[1025]{0:T(1024)S(1)} %add_rsqrt_fusion.2, f32[1025]{0:T(1024)S(1)} %broadcast_multiply_fusion.7, ...), kind=kOutput, calls=%fused_computation.75 | convolution fusion | flops 3235392000 | bytes 11565064 | tf_op jit(solution)/shard_map/td,dpe->tpe/dot_general | solution.py:197
  107.3 2.8 fusion.159
  113.4 3.1 copy.170
  118.6 2.7 slice.244
  123.3 2.9 copy.173
  126.2 3.7 copy.174
  132.2 3.6 copy.175
  135.9 42.0 %while.24 = (s32[]{:T(128)}, bf16[8,1025,64]{1,2,0:T(8,128)(2,1)}, bf16[8,1025,64]{2,1,0:T(8,128)(2,1)S(1)}, bf16[8,1025,64]{2,1,0:T(8,128)(2,1)}, bf16[8,1025,64]{2,1,0:T(8,128)(2,1)}, /*index=5*/s32[]{:T(128)}) while((s32[]{:T(128)}, bf16[8,1025,64]{1,2,0:T(8,128)(2,1)}, bf16[8,1025,64]{2,1,0:T(8,128)(2,1)S(1)}, ...), condition=%wide.region_5.6_spmd, body=%wide.region_2.5_spmd.sunk | while | flops 276377920 | bytes 13570149 | solution.py:219
  138.4 2.6 fusion.193
  143.6 2.6 fusion.193
  148.8 2.6 fusion.193
  153.9 2.6 fusion.193
  159.2 2.6 fusion.193
  164.4 2.6 fusion.193
  169.6 2.6 fusion.193
  174.8 2.6 fusion.193
  177.8 3.8 fusion.109
  193.5 15.0 %all-gather.5.cloned.1.call-done = bf16[1024,4224]{1,0:T(8,128)(2,1)} async-done(((bf16[64,4224]{1,0:T(8,128)(2,1)}), bf16[1024,4224]{1,0:T(8,128)(2,1)}) %all-gather.5.cloned.1.call-update) | async-done | bytes 8650768 | tf_op jit(solution)/shard_map/all_gather | solution.py:236
  208.5 9.4 %fusion.56 = f32[1025,2816]{1,0:T(8,128)S(1)} fusion(bf16[1024,4224]{1,0:T(8,128)(2,1)} %all-gather.5.cloned.1.call-done, f32[1024]{0:T(1024)S(1)} %get-tuple-element.340, f32[1024]{0:T(1024)S(1)} %get-tuple-element.339, f32[1025]{0:T(1024)S(1)} %add_rsqrt_fusion.1, f32[1025]{0:T(1024)S(1)} %broadcast_multiply_fusion.6, ...), kind=kOutput, calls=%fused_computation.84 | convolution fusion | flops 5920793600 | bytes 19428360 | tf_op jit(solution)/shard_map/dot_general | solution.py:245
  226.2 10.7 %multiply_reduce_fusion.1 = (bf16[1365]{0:T(1024)(128)(2,1)S(1)}, f32[1025]{0:T(1024)S(1)}, f32[1025]{0:T(1024)S(1)}, bf16[1365]{0:T(1024)(128)(2,1)}, bf16[1025,1365]{1,0:T(8,128)(2,1)}, /*index=5*/f32[1025,1365]{1,0:T(8,128)}) fusion(f32[1025,1365]{1,0:T(8,128)S(1)} %get-tuple-element.293, f32[1025]{0:T(1024)S(1)} %add_rsqrt_fusion, ...), kind=kOutput, calls=%fused_computation.65 | convolution fusion | flops 2886390272 | bytes 19006814 | tf_op jit(solution)/shard_map/td,df->tf/dot_general | solution.py:265
  238.8 3.0 copy.183
  241.9 3.8 pad.51
  246.4 12.2 %fusion.153 = (bf16[1365]{0:T(1024)(128)(2,1)S(1)}, bf16[1025,1365]{1,0:T(8,128)(2,1)}, bf16[1365]{0:T(1024)(128)(2,1)S(1)}, bf16[1025,1365]{1,0:T(8,128)(2,1)}) fusion(f32[1365]{0:T(1024)S(1)} %convert_element_type.235, f32[1025,2816]{1,0:T(8,128)} %copy-done.2, f32[1365]{0:T(1024)S(1)} %convert_element_type.236, f32[1025]{0:T(1024)S(1)} %add_multiply_fusion, ...), kind=kLoop, calls=%fused_computation.267 | loop fusion | flops 33576260 | bytes 28020740 | tf_op jit(solution)/shard_map/reduce_sum | solution.py:279
  258.9 10.4 %fusion.76 = bf16[1025,1024]{1,0:T(8,128)(2,1)S(1)} fusion(bf16[1024,4224]{1,0:T(8,128)(2,1)} %all-gather.5.cloned.1.call-done, bf16[1025,1365]{1,0:T(8,128)(2,1)} %get-tuple-element.301, bf16[1025,1365]{1,0:T(8,128)(2,1)} %get-tuple-element.288), kind=kOutput, calls=%fused_computation.110 | convolution fusion | flops 5935488000 | bytes 13678592 | tf_op jit(solution)/shard_map/tf,df->td/dot_general | solution.py:286
  269.7 11.0 %convert_dynamic-update-slice_fusion = bf16[1024,4992]{1,0:T(8,128)(2,1)S(1)} fusion(bf16[1025,1365]{1,0:T(8,128)(2,1)} %get-tuple-element.301, bf16[1025,1365]{1,0:T(8,128)(2,1)} %get-tuple-element.288, f32[1024]{0:T(1024)S(1)} %copy-done.49, f32[1024]{0:T(1024)S(1)} %get-tuple-element.339, f32[1025]{0:T(1024)S(1)} %add_rsqrt_fusion.1, ...), kind=kOutput, calls=%fused_computation.74 | convolution fusion | flops 5946768384 | bytes 13479260 | tf_op jit(solution)/shard_map/td,tf->df/dot_general | solution.py:282
  280.7 6.5 %fusion.79 = bf16[1024,4992]{1,0:T(8,128)(2,1)S(1)} fusion(bf16[1024,4992]{1,0:T(8,128)(2,1)S(1)} %convert_dynamic-update-slice_fusion, bf16[1025,512]{1,0:T(8,128)(2,1)S(1)} %copy-done.22, bf16[1025,512]{1,0:T(8,128)(2,1)S(1)} %get-tuple-element.325, bf16[1025,1365]{1,0:T(8,128)(2,1)} %get-tuple-element.304), kind=kOutput, calls=%fused_computation.112 | convolution fusion | flops 2961313792 | bytes 7795370 | tf_op jit(solution)/shard_map/td,tf->df/dot_general | solution.py:261
  287.2 5.4 fusion.72
  292.7 6.0 %fusion.154 = (bf16[1024]{0:T(1024)(128)(2,1)S(1)}, bf16[1025,1024]{1,0:T(8,128)(2,1)}, f32[1025,1024]{1,0:T(8,128)}, bf16[1024]{0:T(1024)(128)(2,1)S(1)}) fusion(f32[1025]{0:T(1024)S(1)} %broadcast_multiply_fusion.4, f32[1025]{0:T(1024)S(1)} %broadcast_multiply_fusion.6, bf16[1025,512]{1,0:T(8,128)(2,1)S(1)} %get-tuple-element.328, ...), kind=kLoop, calls=%fused_computation.268 | loop fusion | flops 24138752 | bytes 14718992 | tf_op jit(solution)/shard_map/reduce_sum | solution.py:293
  299.0 4.7 fusion.99
  310.8 101.0 %while.25 = (s32[]{:T(128)}, f32[8,1025,64]{1,2,0:T(8,128)S(1)}, f32[8,1025,64]{1,2,0:T(8,128)}, bf16[8,1025,64]{1,2,0:T(8,128)(2,1)}, bf16[8,1025,64]{2,1,0:T(8...) while((s32[]{:T(128)}, f32[8,1025,64]{1,2,0:T(8,128)S(1)}, ...), condition=%wide.region_26.27_spmd, body=%wide.region_22.26_spmd.sunk | while | flops 689338112 | bytes 38548648 | solution.py:349
  313.6 2.5 fusion.204
  351.4 2.5 fusion.204
  376.7 2.5 fusion.204
  411.9 4.2 bitcast_multiply_fusion.1
  422.3 3.1 copy.182
  429.3 5.0 add_convert_fusion.3
  434.4 4.9 fusion.75
  439.6 6.5 %convolution_convert_fusion.2 = bf16[1024,3,512]{0,2,1:T(8,128)(2,1)} fusion(f32[1024]{0:T(1024)S(1)} %copy-done.47, f32[1024]{0:T(1024)S(1)} %copy-done.40, bf16[1025,1,512]{2,0,1:T(8,128)(2,1)S(1)} %copy-done.23, bf16[1025,1,512]{2,0,1:T(8,128)(2,1)S(1)} %get-tuple-element.323, bf16[1025,1,512]{2,0,1:T(8,128)(2,1)S(1)} %get-tuple-element.322, ...), kind=kOutput, calls=%fused_computation.136 | convolution fusion | flops 3244836864 | bytes 8410120 | tf_op jit(solution)/shard_map/td,tpe->dpe/dot_general | solution.py:370
  446.1 4.7 copy.190
  453.3 6.7 %fusion.150 = (f32[1025]{0:T(1024)S(1)}, f32[1025]{0:T(1024)S(1)}, bf16[1024]{0:T(1024)(128)(2,1)S(1)}, bf16[1024]{0:T(1024)(128)(2,1)S(1)}, f32[1025,1024]{1,0:T(8,128)}, /*index=5*/f32[1025,1024]{1,0:T(8,128)}) fusion(f32[1025]{0:T(1024)S(1)} %copy-done.36, f32[1025]{0:T(1024)S(1)} %copy-done.34, bf16[1025,512]{1,0:T(8,128)(2,1)S(1)} %copy-done.8, ...), kind=kLoop, calls=%fused_computation.265 | loop fusion | flops 16789502 | bytes 14718992 | tf_op jit(solution)/shard_map/reduce_sum | solution.py:31
  460.3 3.6 fusion.85
  463.9 21.1 %reduce-scatter.3.cloned.1.call-done = bf16[64,4992]{1,0:T(8,128)(2,1)} async-done(((bf16[1024,4992]{1,0:T(8,128)(2,1)}), bf16[64,4992]{1,0:T(8,128)(2,1)}) %reduce-scatter.3.cloned.1.call-update) | async-done | bytes 638992 | tf_op jit(solution)/shard_map/reduce_scatter | solution.py:320
  486.3 6.3 %fusion.87 = f32[1025,1024]{1,0:T(8,128)S(1)} fusion(bf16[1025,1408]{1,0:T(8,128)(2,1)} %pad.51, bf16[1024,4224]{1,0:T(8,128)(2,1)} %all-gather.5.cloned.1.call-done), kind=kOutput, calls=%fused_computation.122 | convolution fusion | flops 2955673600 | bytes 9988096 | tf_op jit(solution)/shard_map/tf,df->td/dot_general | solution.py:312
  495.6 3.5 add_convert_fusion.4
  499.1 3.1 fusion.96
  505.5 66.5 %reduce-scatter.5.cloned.1.call-done = bf16[64,1792]{1,0:T(8,128)(2,1)} async-done(((bf16[1024,1792]{1,0:T(8,128)(2,1)}), bf16[64,1792]{1,0:T(8,128)(2,1)}) %reduce-scatter.5.cloned.1.call-update) | async-done | bytes 229392 | tf_op jit(solution)/shard_map/reduce_scatter | solution.py:390
  (314 shorter events, 195.4 us)
Async XLA Ops:
  7.2 8.4 %copy-start.10 = (bf16[1025,512]{1,0:T(8,128)(2,1)S(1)}, bf16[1025,512]{1,0:T(8,128)(2,1)}, u32[]{:S(2)}) copy-start(bf16[1025,512]{1,0:T(8,128)(2,1)} %param.23) | copy-start | bytes 3148804
  7.2 6.2 %copy-start.50 = (bf16[512]{0:T(512)(128)(2,1)S(1)}, bf16[512]{0:T(512)(128)(2,1)}, u32[]{:S(2)}) copy-start(bf16[512]{0:T(512)(128)(2,1)} %param.27) | copy-start | bytes 3076
  7.2 6.2 %copy-start.51 = (bf16[512]{0:T(512)(128)(2,1)S(1)}, bf16[512]{0:T(512)(128)(2,1)}, u32[]{:S(2)}) copy-start(bf16[512]{0:T(512)(128)(2,1)} %param.28) | copy-start | bytes 3076
  7.2 84.5 %all-gather.3.cloned.1.call-start = ((), (), s32[]{:S(2)}) async-start(), calls=%async_computation.2 | async-start | bytes 4734976 | tf_op jit(solution)/shard_map/all_gather | solution.py:180
  10.8 197.8 %all-gather.5.cloned.1.call-start = ((), (), s32[]{:S(2)}) async-start(), calls=%async_computation.3 | async-start | bytes 9191424 | tf_op jit(solution)/shard_map/all_gather | solution.py:236
  10.8 4.8 collective-permute-start
  13.3 471.7 %reduce-scatter.3.cloned.1.call-start = ((), (), s32[]{:S(2)}) async-start(), calls=%async_computation.4 | async-start | bytes 10862592 | tf_op jit(solution)/shard_map/reduce_scatter | solution.py:320
  17.0 84.2 %copy-start.5 = (bf16[1025,512]{1,0:T(8,128)(2,1)}, bf16[1025,512]{1,0:T(8,128)(2,1)S(1)}, u32[]{:S(2)}) copy-start(bf16[1025,512]{1,0:T(8,128)(2,1)S(1)} %get-tuple-element.329) | copy-start | bytes 3148804
  17.0 84.2 %copy-start.7 = (bf16[1025,512]{1,0:T(8,128)(2,1)}, bf16[1025,512]{1,0:T(8,128)(2,1)S(1)}, u32[]{:S(2)}) copy-start(bf16[1025,512]{1,0:T(8,128)(2,1)S(1)} %get-tuple-element.330) | copy-start | bytes 3148804
  17.4 83.8 %copy-start.33 = (f32[1025]{0:T(1024)}, f32[1025]{0:T(1024)S(1)}, u32[]{:S(2)}) copy-start(f32[1025]{0:T(1024)S(1)} %broadcast_multiply_fusion.7) | copy-start | bytes 12304
  18.1 83.1 %copy-start.35 = (f32[1025]{0:T(1024)}, f32[1025]{0:T(1024)S(1)}, u32[]{:S(2)}) copy-start(f32[1025]{0:T(1024)S(1)} %add_rsqrt_fusion.2) | copy-start | bytes 12304
  94.6 6.6 %copy-start.39 = (f32[1024]{0:T(1024)}, f32[1024]{0:T(1024)S(1)}, u32[]{:S(2)}) copy-start(f32[1024]{0:T(1024)S(1)} %get-tuple-element.341) | copy-start | bytes 12292
  94.6 6.6 %copy-start.46 = (f32[1024]{0:T(1024)}, f32[1024]{0:T(1024)S(1)}, u32[]{:S(2)}) copy-start(f32[1024]{0:T(1024)S(1)} %get-tuple-element.338) | copy-start | bytes 12292
  94.6 113.9 %copy-start.48 = (f32[1024]{0:T(1024)}, f32[1024]{0:T(1024)S(1)}, u32[]{:S(2)}) copy-start(f32[1024]{0:T(1024)S(1)} %get-tuple-element.340) | copy-start | bytes 12292
  184.0 5.9 %copy-start.41 = (bf16[1365]{0:T(1024)(128)(2,1)S(1)}, bf16[1365]{0:T(1024)(128)(2,1)}, u32[]{:S(2)}) copy-start(bf16[1365]{0:T(1024)(128)(2,1)} %param.34) | copy-start | bytes 8194
  184.0 5.9 %copy-start.42 = (bf16[1365]{0:T(1024)(128)(2,1)S(1)}, bf16[1365]{0:T(1024)(128)(2,1)}, u32[]{:S(2)}) copy-start(bf16[1365]{0:T(1024)(128)(2,1)} %param.36) | copy-start | bytes 8194
  184.0 2.9 collective-permute-start.1
  185.1 7.2 %copy-start.37 = (f32[512]{0:T(512)}, f32[512]{0:T(512)S(1)}, u32[]{:S(2)}) copy-start(f32[512]{0:T(512)S(1)} %dynamic-slice_reduce_fusion.1) | copy-start | bytes 6148
  189.4 2.7 collective-permute-start.2
  189.6 34.9 %collective-permute-start.5 = (bf16[1025,512]{1,0:T(8,128)(2,1)}, bf16[1025,512]{1,0:T(8,128)(2,1)}, u32[]{:S(2)}, u32[]{:S(2)}) collective-permute-start(bf16[1025,512]{1,0:T(8,128)(2,1)} %param.41), channel_id=1, source_target_pairs={{0,1},{1,0},{2,3},{3,2},{4,5},{5,4},{6,7},{7,6},{8,9},{9,8},{10,11... | collective-permute-start | bytes 3148808 | tf_op jit(solution)/shard_map/ppermute | solution.py:74
  222.3 1.2 collective-permute-start.3
  224.2 1.9 collective-permute-start.4
  226.1 10.7 %copy-start.21 = (bf16[1025,512]{1,0:T(8,128)(2,1)}, bf16[1025,512]{1,0:T(8,128)(2,1)S(1)}, u32[]{:S(2)}) copy-start(bf16[1025,512]{1,0:T(8,128)(2,1)S(1)} %get-tuple-element.326) | copy-start | bytes 3148804
  226.2 11.1 %copy-start.28 = (f32[1025,64]{0,1:T(8,128)S(1)}, f32[1025,64]{0,1:T(8,128)}, u32[]{:S(2)}) copy-start(f32[1025,64]{0,1:T(8,128)} %get-tuple-element.346) | copy-start | bytes 787204
  236.9 8.9 %collective-permute-start.6 = (f32[1025]{0:T(1024)S(1)}, f32[1025]{0:T(1024)S(1)}, u32[]{:S(2)}, u32[]{:S(2)}) collective-permute-start(f32[1025]{0:T(1024)S(1)} %get-tuple-element.238), channel_id=1, source_target_pairs={{0,1},{1,0},{2,3},{3,2},{4,5},{5,4},{6,7},{7,6},{8,9},{9,8},{10,11... | collective-permute-start | bytes 12308 | tf_op jit(solution)/shard_map/ppermute | solution.py:74
  241.8 4.0 collective-permute-start.7
  246.4 12.2 %copy-start.45 = (bf16[1365]{0:T(1024)(128)(2,1)S(1)}, bf16[1365]{0:T(1024)(128)(2,1)}, u32[]{:S(2)}) copy-start(bf16[1365]{0:T(1024)(128)(2,1)} %get-tuple-element.239) | copy-start | bytes 8194
  258.9 10.9 %copy-start.49 = (f32[1024]{0:T(1024)S(1)}, f32[1024]{0:T(1024)}, u32[]{:S(2)}) copy-start(f32[1024]{0:T(1024)} %copy-done.48) | copy-start | bytes 12292
  269.3 11.4 %copy-start.22 = (bf16[1025,512]{1,0:T(8,128)(2,1)S(1)}, bf16[1025,512]{1,0:T(8,128)(2,1)}, u32[]{:S(2)}) copy-start(bf16[1025,512]{1,0:T(8,128)(2,1)} %copy-done.21) | copy-start | bytes 3148804
  269.3 17.9 %collective-permute-start.8 = (bf16[1025,1024]{1,0:T(8,128)(2,1)S(1)}, bf16[1025,1024]{1,0:T(8,128)(2,1)}, u32[]{:S(2)}, u32[]{:S(2)}) collective-permute-start(bf16[1025,1024]{1,0:T(8,128)(2,1)S(1)} %fusion.76), channel_id=1, source_target_pairs={{0,1},{1,0},{2,3},{3,2},{4,5},{5,4},{6,7},{7,6},{8,9},{9,8},{10,11... | collective-permute-start | bytes 6297608 | tf_op jit(solution)/shard_map/ppermute | solution.py:74
  287.2 11.5 %copy-start.9 = (bf16[1024,4992]{1,0:T(8,128)(2,1)}, bf16[1024,4992]{1,0:T(8,128)(2,1)S(1)}, u32[]{:S(2)}) copy-start(bf16[1024,4992]{1,0:T(8,128)(2,1)S(1)} %fusion.79) | copy-start | bytes 30670852
  299.0 6.3 %copy-start.30 = (bf16[1025,1024]{1,0:T(8,128)(2,1)S(1)}, bf16[1025,1024]{1,0:T(8,128)(2,1)}, u32[]{:S(2)}) copy-start(bf16[1025,1024]{1,0:T(8,128)(2,1)} %get-tuple-element.97) | copy-start | bytes 6297604
  309.2 262.8 %reduce-scatter.5.cloned.1.call-start = ((), (), s32[]{:S(2)}) async-start(), calls=%async_computation.5 | async-start | bytes 3899392 | tf_op jit(solution)/shard_map/reduce_scatter | solution.py:390
  310.8 101.1 %copy-start.26 = (f32[1025,64]{0,1:T(8,128)S(1)}, f32[1025,64]{0,1:T(8,128)}, u32[]{:S(2)}) copy-start(f32[1025,64]{0,1:T(8,128)} %get-tuple-element.347) | copy-start | bytes 787204
  434.3 5.3 copy-start.20
  434.3 5.3 copy-start.6
  434.3 5.3 copy-start.8
  434.3 5.3 copy-start.34
  434.3 5.3 copy-start.36
  434.3 5.3 copy-start.40
  439.3 14.0 %collective-permute-start.10 = (bf16[1025,1024]{1,0:T(8,128)(2,1)}, bf16[1025,1024]{1,0:T(8,128)(2,1)}, u32[]{:S(2)}, u32[]{:S(2)}) collective-permute-start(bf16[1025,1024]{1,0:T(8,128)(2,1)} %fusion.75), channel_id=1, source_target_pairs={{0,1},{1,0},{2,3},{3,2},{4,5},{5,4},{6,7},{7,6},{8,9},{9,8},{10,11... | collective-permute-start | bytes 6297608 | tf_op jit(solution)/shard_map/ppermute | solution.py:74
  486.2 12.9 %slice-start.2 = ((s8[4227072]{0:T(1024)(128)(4,1)}), s8[32768]{0:T(1024)(128)(4,1)S(1)}, s32[]{:S(2)}) async-start(s8[4227072]{0:T(1024)(128)(4,1)} %bitcast.204), calls=%async_computation.8 | async-start | bytes 65536
  486.2 6.7 %copy-start.32 = (f32[1024,1]{1,0:T(8,128)S(1)}, f32[1024,1]{1,0:T(8,128)}, u32[]{:S(2)}) copy-start(f32[1024,1]{1,0:T(8,128)} %get-tuple-element.336) | copy-start | bytes 12292
  486.2 9.3 %copy-start.38 = (f32[512]{0:T(512)S(1)}, f32[512]{0:T(512)}, u32[]{:S(2)}) copy-start(f32[512]{0:T(512)} %copy-done.37) | copy-start | bytes 6148
  486.2 12.8 %slice-start.3 = ((s8[4227072]{0:T(1024)(128)(4,1)}), s8[4194304]{0:T(1024)(128)(4,1)S(1)}, s32[]{:S(2)}) async-start(s8[4227072]{0:T(1024)(128)(4,1)} %bitcast.204), calls=%async_computation.9 | async-start | bytes 8388608
  492.8 2.7 collective-permute-start.9
  492.9 6.2 %slice-start = ((s8[4227072]{0:T(1024)(128)(4,1)}), s8[4194304]{0:T(1024)(128)(4,1)S(1)}, s32[]{:S(2)}) async-start(s8[4227072]{0:T(1024)(128)(4,1)} %bitcast.202), calls=%async_computation.6 | async-start | bytes 8388608
  493.1 6.0 %slice-start.1 = ((s8[4227072]{0:T(1024)(128)(4,1)}), s8[32768]{0:T(1024)(128)(4,1)S(1)}, s32[]{:S(2)}) async-start(s8[4227072]{0:T(1024)(128)(4,1)} %bitcast.202), calls=%async_computation.7 | async-start | bytes 65536
  (23 other events, 86.3 us)
Sparse Core Ops, SparseCore 0:
  11.4 80.3 all-gather.2
  95.1 113.3 all-gather.4
  309.3 175.6 reduce-scatter.2
  487.2 84.7 reduce-scatter.4

commit v11 on v6

--- a/solution.py
+++ b/solution.py
@@ -241,9 +241,12 @@
         residual_full, ffn_vectors[:, 0], ffn_vectors[:, 1]
     )
     second_input = second_out.astype(narrow)
-    gate_up_value = jnp.dot(second_input, gate_up_full, preferred_element_type=single)
-    gate_value = gate_up_value[:, :ff_local] + gate_bias.astype(single)
-    up_value = gate_up_value[:, ffn_at[1] : ffn_at[1] + ff_local] + up_bias.astype(single)
+    gate_value = jnp.dot(
+        second_input, gate_up_full[:, :ff_local], preferred_element_type=single
+    ) + gate_bias.astype(single)
+    up_value = jnp.dot(
+        second_input, gate_up_full[:, ffn_at[1] : ffn_at[1] + ff_local], preferred_element_type=single
+    ) + up_bias.astype(single)
     sigmoid_gate = jax.nn.sigmoid(gate_value)
     hidden = gate_value * sigmoid_gate * up_value
     hidden_mean = hidden_totals((jnp.sum(hidden, axis=1),))[0][:, None] / FF

time: 588 us -> 595 us (1.012)
  matrix products: 200 us -> 210 us
    dot_general x1 -> x2, matrix products: 9.38 us -> 17.7 us  [the longest x1 11.9 us: body(): jnp.dot(second_input, gate_up_full[:, ffn_at[1]:ffn_at[1] + ff_local], pr...]
where the time goes in v11:
time: 595 us; the launch traced here: 583 us
  matrix products  210 us (35%)
  waiting for transfers between devices  183 us (31%)
  other arithmetic  95.1 us (16%)
  local copies, waits for them, and re-layouts  76.1 us (13%)
  between operations  15.3 us (3%)
    all_gather x1, waiting for transfers between devices, body(): attn_full = lax.all_gather(attn_pack, 'row', axis=0, tiled=True)  73.6 us
    reduce_scatter x1, waiting for transfers between devices, body(): lax.psum_scatter(end_pack, 'row', scatter_dimension=0, tiled=True)  67 us
    reduce_scatter x1, waiting for transfers between devices, body(): lax.psum_scatter(mid_pack, 'row', scatter_dimension=0, tiled=True)  21 us
    dot_general x8, matrix products, attend(): jnp.einsum('qk,kd->qd', weights.astype(narrow), value_block, preferred_el...  20.8 us
    dot_general x8, matrix products, attend_back(): jnp.einsum('qk,qd->kd', weights.astype(narrow), grad_block, preferred_ele...  20.3 us
    dot_general x8, matrix products, attend_back(): jnp.einsum('qk,qd->kd', score_grad, query_block, preferred_element_type=s...  20 us
    dot_general x8, matrix products, attend_back(): jnp.einsum('qd,kd->qk', grad_block, value_block, preferred_element_type=s...  17.6 us
    dot_general x8, matrix products, attend_back(): jnp.einsum('qd,kd->qk', query_block, key_block, preferred_element_type=si...  15.6 us
  transfers between devices with their start and end apart: 15, of which 7 were waited for; matrix products, arithmetic and copies ran while one was open for 54% of the time, Pallas kernels for 0%

profile of v11, /device:TPU:0, one launch (start us, length us, event | category | flops | bytes accessed | tf_op | source)
XLA Modules:
  0.0 583.2 jit_solution(6860342048383707438)
XLA Ops:
  18.1 73.6 %all-gather.3.cloned.1.call-done = bf16[1024,2176]{1,0:T(8,128)(2,1)} async-done(((bf16[64,2176]{1,0:T(8,128)(2,1)}), bf16[1024,2176]{1,0:T(8,128)(2,1)}) %all-gather.3.cloned.1.call-update) | async-done | bytes 4456464 | tf_op jit(solution)/shard_map/all_gather | solution.py:180
  96.6 4.7 copy.166
  101.3 6.1 %convolution_add_fusion.2 = f32[1025,3,512]{2,0,1:T(8,128)S(1)} fusion(bf16[1024,3,512]{0,2,1:T(8,128)(2,1)} %bitcast.219, f32[3,512]{1,0:T(4,128)S(1)} %pad_maximum_fusion.8, f32[1024]{0:T(1024)S(1)} %get-tuple-element.338, f32[1024]{0:T(1024)S(1)} %get-tuple-element.341, f32[1025]{0:T(1024)S(1)} %add_rsqrt_fusion.2, ...), kind=kOutput, calls=%fused_computation.77 | convolution fusion | flops 3235392000 | bytes 11565064 | tf_op jit(solution)/shard_map/td,dpe->tpe/dot_general | solution.py:197
  107.4 2.8 fusion.158
  113.5 3.1 copy.170
  118.7 2.7 slice.231
  123.3 2.9 copy.173
  126.2 3.7 copy.174
  132.3 3.7 copy.175
  135.9 41.9 %while.24 = (s32[]{:T(128)}, bf16[8,1025,64]{1,2,0:T(8,128)(2,1)}, bf16[8,1025,64]{2,1,0:T(8,128)(2,1)S(1)}, bf16[8,1025,64]{2,1,0:T(8,128)(2,1)}, bf16[8,1025,64]{2,1,0:T(8,128)(2,1)}, /*index=5*/s32[]{:T(128)}) while((s32[]{:T(128)}, bf16[8,1025,64]{1,2,0:T(8,128)(2,1)}, bf16[8,1025,64]{2,1,0:T(8,128)(2,1)S(1)}, ...), condition=%wide.region_5.6_spmd, body=%wide.region_2.5_spmd.sunk | while | flops 276377920 | bytes 13570149 | solution.py:219
  138.5 2.6 fusion.192
  143.7 2.6 fusion.192
  148.9 2.6 fusion.192
  154.1 2.6 fusion.192
  159.3 2.6 fusion.192
  164.5 2.6 fusion.192
  169.7 2.6 fusion.192
  174.8 2.6 fusion.192
  177.9 3.8 fusion.108
  193.6 15.0 %all-gather.5.cloned.1.call-done = bf16[1024,4224]{1,0:T(8,128)(2,1)} async-done(((bf16[64,4224]{1,0:T(8,128)(2,1)}), bf16[1024,4224]{1,0:T(8,128)(2,1)}) %all-gather.5.cloned.1.call-update) | async-done | bytes 8650768 | tf_op jit(solution)/shard_map/all_gather | solution.py:236
  208.5 5.8 convolution_add_fusion.1
  214.4 11.9 %fusion.155 = (f32[1025]{0:T(1024)S(1)}, f32[1025,1365]{1,0:T(8,128)}, f32[1025,1365]{1,0:T(8,128)}) fusion(f32[1025,1365]{1,0:T(8,128)S(1)} %convolution_add_fusion.1, f32[1365]{0:T(1024)S(1)} %convert_element_type.237, bf16[1024,4224]{1,0:T(8,128)(2,1)} %all-gather.5.cloned.1.call-done, f32[1024]{0:T(1024)S(1)} %get-tuple-element.340, ...), kind=kOutput, calls=%fused_computation.268 | convolution fusion | flops 2884646912 | bytes 21798236 | tf_op jit(solution)/shard_map/dot_general | solution.py:247
  228.0 3.1 copy.183
  231.2 3.4 multiply_reduce_fusion.3
  236.8 8.6 %multiply_reduce_fusion.1 = (bf16[1365]{0:T(1024)(128)(2,1)S(1)}, f32[1025]{0:T(1024)S(1)}, f32[1025]{0:T(1024)S(1)}, bf16[1365]{0:T(1024)(128)(2,1)S(1)}, bf16[...) fusion(f32[1025,1365]{1,0:T(8,128)} %get-tuple-element.293, f32[1025]{0:T(1024)S(1)} %add_rsqrt_fusion, ...), kind=kOutput, calls=%fused_computation.65 | convolution fusion | flops 2886390272 | bytes 19222538 | tf_op jit(solution)/shard_map/td,df->tf/dot_general | solution.py:266
  246.0 5.8 convolution_convert_fusion
  253.5 7.5 %fusion.152 = (bf16[1365]{0:T(1024)(128)(2,1)S(1)}, bf16[1025,1365]{1,0:T(8,128)(2,1)}, bf16[1365]{0:T(1024)(128)(2,1)S(1)}, bf16[1025,1365]{1,0:T(8,128)(2,1)}) fusion(f32[1025,1365]{1,0:T(8,128)S(1)} %bitcast.215, f32[1025,1365]{1,0:T(8,128)S(1)} %bitcast.217, f32[1025]{0:T(1024)S(1)} %add_multiply_fusion, f32[1025,1365]{1,0:T(8,128)S(1)} %bitcast.200, ...), kind=kLoop, calls=%fused_computation.266 | loop fusion | flops 30778012 | bytes 28009820 | tf_op jit(solution)/shard_map/reduce_sum | solution.py:280
  261.3 10.4 %fusion.74 = bf16[1025,1024]{1,0:T(8,128)(2,1)S(1)} fusion(bf16[1024,4224]{1,0:T(8,128)(2,1)} %all-gather.5.cloned.1.call-done, bf16[1025,1365]{1,0:T(8,128)(2,1)} %get-tuple-element.301, bf16[1025,1365]{1,0:T(8,128)(2,1)} %get-tuple-element.288), kind=kOutput, calls=%fused_computation.108 | convolution fusion | flops 5935488000 | bytes 13678592 | tf_op jit(solution)/shard_map/tf,df->td/dot_general | solution.py:287
  271.8 11.0 %convert_dynamic-update-slice_fusion = bf16[1024,4992]{1,0:T(8,128)(2,1)S(1)} fusion(bf16[1025,1365]{1,0:T(8,128)(2,1)} %get-tuple-element.301, bf16[1025,1365]{1,0:T(8,128)(2,1)} %get-tuple-element.288, f32[1024]{0:T(1024)S(1)} %get-tuple-element.340, f32[1024]{0:T(1024)S(1)} %get-tuple-element.339, f32[1025]{0:T(1024)S(1)} %add_rsqrt_fusion.1, ...), kind=kOutput, calls=%fused_computation.76 | convolution fusion | flops 5946768384 | bytes 13479260 | tf_op jit(solution)/shard_map/td,tf->df/dot_general | solution.py:283
  285.1 5.6 fusion.70
  290.7 6.2 %fusion.153 = (bf16[1024]{0:T(1024)(128)(2,1)S(1)}, bf16[1025,1024]{1,0:T(8,128)(2,1)}, f32[1025,1024]{1,0:T(8,128)}, bf16[1024]{0:T(1024)(128)(2,1)S(1)}) fusion(f32[1025]{0:T(1024)S(1)} %broadcast_multiply_fusion.4, f32[1025]{0:T(1024)S(1)} %broadcast_multiply_fusion.6, bf16[1025,512]{1,0:T(8,128)(2,1)S(1)} %get-tuple-element.328, ...), kind=kLoop, calls=%fused_computation.267 | loop fusion | flops 24138752 | bytes 14718992 | tf_op jit(solution)/shard_map/reduce_sum | solution.py:294
  297.1 4.7 fusion.98
  309.0 100.9 %while.25 = (s32[]{:T(128)}, f32[8,1025,64]{1,2,0:T(8,128)S(1)}, f32[8,1025,64]{1,2,0:T(8,128)}, bf16[8,1025,64]{1,2,0:T(8,128)(2,1)}, bf16[8,1025,64]{2,1,0:T(8...) while((s32[]{:T(128)}, f32[8,1025,64]{1,2,0:T(8,128)S(1)}, ...), condition=%wide.region_26.27_spmd, body=%wide.region_22.26_spmd.sunk | while | flops 689338112 | bytes 38548648 | solution.py:350
  311.7 2.5 fusion.203
  362.1 2.5 fusion.203
  409.9 4.3 bitcast_multiply_fusion.1
  420.4 3.2 copy.182
  427.5 5.0 add_convert_fusion.3
  432.5 5.0 fusion.73
  438.1 6.4 %convolution_convert_fusion.2 = bf16[1024,3,512]{0,2,1:T(8,128)(2,1)} fusion(f32[1024]{0:T(1024)S(1)} %copy-done.44, f32[1024]{0:T(1024)S(1)} %copy-done.38, bf16[1025,1,512]{2,0,1:T(8,128)(2,1)S(1)} %copy-done.21, bf16[1025,1,512]{2,0,1:T(8,128)(2,1)S(1)} %get-tuple-element.323, bf16[1025,1,512]{2,0,1:T(8,128)(2,1)S(1)} %get-tuple-element.322, ...), kind=kOutput, calls=%fused_computation.136 | convolution fusion | flops 3244836864 | bytes 8410120 | tf_op jit(solution)/shard_map/td,tpe->dpe/dot_general | solution.py:371
  444.5 4.7 copy.190
  451.6 6.7 %fusion.149 = (f32[1025]{0:T(1024)S(1)}, f32[1025]{0:T(1024)S(1)}, bf16[1024]{0:T(1024)(128)(2,1)S(1)}, bf16[1024]{0:T(1024)(128)(2,1)S(1)}, f32[1025,1024]{1,0:T(8,128)}, /*index=5*/f32[1025,1024]{1,0:T(8,128)}) fusion(f32[1025]{0:T(1024)S(1)} %copy-done.34, f32[1025]{0:T(1024)S(1)} %copy-done.32, bf16[1025,512]{1,0:T(8,128)(2,1)S(1)} %copy-done.5, ...), kind=kLoop, calls=%fused_computation.264 | loop fusion | flops 16789502 | bytes 14718992 | tf_op jit(solution)/shard_map/reduce_sum | solution.py:31
  458.7 3.6 fusion.82
  462.3 21.0 %reduce-scatter.3.cloned.1.call-done = bf16[64,4992]{1,0:T(8,128)(2,1)} async-done(((bf16[1024,4992]{1,0:T(8,128)(2,1)}), bf16[64,4992]{1,0:T(8,128)(2,1)}) %reduce-scatter.3.cloned.1.call-update) | async-done | bytes 638992 | tf_op jit(solution)/shard_map/reduce_scatter | solution.py:321
  484.6 6.3 %fusion.86 = f32[1025,1024]{1,0:T(8,128)S(1)} fusion(bf16[1025,1365]{1,0:T(8,128)(2,1)} %copy-done.47, bf16[1024,4224]{1,0:T(8,128)(2,1)} %all-gather.5.cloned.1.call-done), kind=kOutput, calls=%fused_computation.122 | convolution fusion | flops 2865408000 | bytes 9988096 | tf_op jit(solution)/shard_map/tf,df->td/dot_general | solution.py:313
  493.9 3.5 add_convert_fusion.4
  497.4 3.1 fusion.95
  503.7 67.0 %reduce-scatter.5.cloned.1.call-done = bf16[64,1792]{1,0:T(8,128)(2,1)} async-done(((bf16[1024,1792]{1,0:T(8,128)(2,1)}), bf16[64,1792]{1,0:T(8,128)(2,1)}) %reduce-scatter.5.cloned.1.call-update) | async-done | bytes 229392 | tf_op jit(solution)/shard_map/reduce_scatter | solution.py:391
  (321 shorter events, 195.4 us)
Async XLA Ops:
  7.2 8.4 %copy-start.7 = (bf16[1025,512]{1,0:T(8,128)(2,1)S(1)}, bf16[1025,512]{1,0:T(8,128)(2,1)}, u32[]{:S(2)}) copy-start(bf16[1025,512]{1,0:T(8,128)(2,1)} %param.23) | copy-start | bytes 3148804
  7.2 6.2 %copy-start.45 = (bf16[512]{0:T(512)(128)(2,1)S(1)}, bf16[512]{0:T(512)(128)(2,1)}, u32[]{:S(2)}) copy-start(bf16[512]{0:T(512)(128)(2,1)} %param.27) | copy-start | bytes 3076
  7.2 6.2 %copy-start.46 = (bf16[512]{0:T(512)(128)(2,1)S(1)}, bf16[512]{0:T(512)(128)(2,1)}, u32[]{:S(2)}) copy-start(bf16[512]{0:T(512)(128)(2,1)} %param.28) | copy-start | bytes 3076
  7.2 84.5 %all-gather.3.cloned.1.call-start = ((), (), s32[]{:S(2)}) async-start(), calls=%async_computation.2 | async-start | bytes 4734976 | tf_op jit(solution)/shard_map/all_gather | solution.py:180
  10.8 197.8 %all-gather.5.cloned.1.call-start = ((), (), s32[]{:S(2)}) async-start(), calls=%async_computation.3 | async-start | bytes 9191424 | tf_op jit(solution)/shard_map/all_gather | solution.py:236
  10.8 4.8 collective-permute-start
  13.3 470.0 %reduce-scatter.3.cloned.1.call-start = ((), (), s32[]{:S(2)}) async-start(), calls=%async_computation.4 | async-start | bytes 10862592 | tf_op jit(solution)/shard_map/reduce_scatter | solution.py:321
  17.0 84.3 %copy-start.2 = (bf16[1025,512]{1,0:T(8,128)(2,1)}, bf16[1025,512]{1,0:T(8,128)(2,1)S(1)}, u32[]{:S(2)}) copy-start(bf16[1025,512]{1,0:T(8,128)(2,1)S(1)} %get-tuple-element.329) | copy-start | bytes 3148804
  17.0 84.3 %copy-start.4 = (bf16[1025,512]{1,0:T(8,128)(2,1)}, bf16[1025,512]{1,0:T(8,128)(2,1)S(1)}, u32[]{:S(2)}) copy-start(bf16[1025,512]{1,0:T(8,128)(2,1)S(1)} %get-tuple-element.330) | copy-start | bytes 3148804
  17.4 83.9 %copy-start.31 = (f32[1025]{0:T(1024)}, f32[1025]{0:T(1024)S(1)}, u32[]{:S(2)}) copy-start(f32[1025]{0:T(1024)S(1)} %broadcast_multiply_fusion.7) | copy-start | bytes 12304
  18.1 83.2 %copy-start.33 = (f32[1025]{0:T(1024)}, f32[1025]{0:T(1024)S(1)}, u32[]{:S(2)}) copy-start(f32[1025]{0:T(1024)S(1)} %add_rsqrt_fusion.2) | copy-start | bytes 12304
  94.6 6.7 %copy-start.37 = (f32[1024]{0:T(1024)}, f32[1024]{0:T(1024)S(1)}, u32[]{:S(2)}) copy-start(f32[1024]{0:T(1024)S(1)} %get-tuple-element.341) | copy-start | bytes 12292
  94.6 6.7 %copy-start.43 = (f32[1024]{0:T(1024)}, f32[1024]{0:T(1024)S(1)}, u32[]{:S(2)}) copy-start(f32[1024]{0:T(1024)S(1)} %get-tuple-element.338) | copy-start | bytes 12292
  184.1 5.9 %copy-start.39 = (bf16[1365]{0:T(1024)(128)(2,1)S(1)}, bf16[1365]{0:T(1024)(128)(2,1)}, u32[]{:S(2)}) copy-start(bf16[1365]{0:T(1024)(128)(2,1)} %param.34) | copy-start | bytes 8194
  184.1 5.9 %copy-start.40 = (bf16[1365]{0:T(1024)(128)(2,1)S(1)}, bf16[1365]{0:T(1024)(128)(2,1)}, u32[]{:S(2)}) copy-start(bf16[1365]{0:T(1024)(128)(2,1)} %param.36) | copy-start | bytes 8194
  184.1 2.9 collective-permute-start.1
  189.4 2.7 collective-permute-start.2
  189.6 45.5 %collective-permute-start.5 = (bf16[1025,512]{1,0:T(8,128)(2,1)}, bf16[1025,512]{1,0:T(8,128)(2,1)}, u32[]{:S(2)}, u32[]{:S(2)}) collective-permute-start(bf16[1025,512]{1,0:T(8,128)(2,1)} %param.41), channel_id=1, source_target_pairs={{0,1},{1,0},{2,3},{3,2},{4,5},{5,4},{6,7},{7,6},{8,9},{9,8},{10,11... | collective-permute-start | bytes 3148808 | tf_op jit(solution)/shard_map/ppermute | solution.py:74
  214.3 12.0 %copy-start.14 = (f32[1025,1365]{1,0:T(8,128)}, f32[1025,1365]{1,0:T(8,128)S(1)}, u32[]{:S(2)}) copy-start(f32[1025,1365]{1,0:T(8,128)S(1)} %convolution_add_fusion.1) | copy-start | bytes 16789504
  214.3 12.0 %copy-start.41 = (bf16[1365]{0:T(1024)(128)(2,1)S(1)}, bf16[1365]{0:T(1024)(128)(2,1)}, u32[]{:S(2)}) copy-start(bf16[1365]{0:T(1024)(128)(2,1)} %param.37) | copy-start | bytes 8194
  214.4 12.0 %copy-start.42 = (bf16[1365]{0:T(1024)(128)(2,1)S(1)}, bf16[1365]{0:T(1024)(128)(2,1)}, u32[]{:S(2)}) copy-start(bf16[1365]{0:T(1024)(128)(2,1)} %param.38) | copy-start | bytes 8194
  214.4 12.0 %copy-start.26 = (f32[1025,64]{0,1:T(8,128)S(1)}, f32[1025,64]{0,1:T(8,128)}, u32[]{:S(2)}) copy-start(f32[1025,64]{0,1:T(8,128)} %get-tuple-element.346) | copy-start | bytes 787204
  226.3 4.8 collective-permute-start.3
  234.6 2.2 collective-permute-start.4
  236.8 9.2 %copy-start.19 = (bf16[1025,512]{1,0:T(8,128)(2,1)}, bf16[1025,512]{1,0:T(8,128)(2,1)S(1)}, u32[]{:S(2)}) copy-start(bf16[1025,512]{1,0:T(8,128)(2,1)S(1)} %get-tuple-element.326) | copy-start | bytes 3148804
  245.4 6.4 %copy-start.47 = (bf16[1025,1365]{1,0:T(8,128)(2,1)}, bf16[1025,1365]{1,0:T(8,128)(2,1)S(1)}, u32[]{:S(2)}) copy-start(bf16[1025,1365]{1,0:T(8,128)(2,1)S(1)} %get-tuple-element.96) | copy-start | bytes 8394754
  245.4 6.4 %collective-permute-start.6 = (f32[1025]{0:T(1024)S(1)}, f32[1025]{0:T(1024)S(1)}, u32[]{:S(2)}, u32[]{:S(2)}) collective-permute-start(f32[1025]{0:T(1024)S(1)} %get-tuple-element.238), channel_id=1, source_target_pairs={{0,1},{1,0},{2,3},{3,2},{4,5},{5,4},{6,7},{7,6},{8,9},{9,8},{10,11... | collective-permute-start | bytes 12308 | tf_op jit(solution)/shard_map/ppermute | solution.py:74
  245.5 6.3 %collective-permute-start.7 = (f32[1025]{0:T(1024)S(1)}, f32[1025]{0:T(1024)S(1)}, u32[]{:S(2)}, u32[]{:S(2)}) collective-permute-start(f32[1025]{0:T(1024)S(1)} %get-tuple-element.233), channel_id=1, source_target_pairs={{0,1},{1,0},{2,3},{3,2},{4,5},{5,4},{6,7},{7,6},{8,9},{9,8},{10,11... | collective-permute-start | bytes 12308 | tf_op jit(solution)/shard_map/ppermute | solution.py:74
  246.0 5.9 %slice-start = ((s8[5812224]{0:T(1024)(128)(4,1)}), s8[4194304]{0:T(1024)(128)(4,1)S(1)}, s32[]{:S(2)}) async-start(s8[5812224]{0:T(1024)(128)(4,1)} %bitcast.199), calls=%async_computation.6 | async-start | bytes 8388608
  246.0 5.9 %slice-start.6 = ((s8[5812224]{0:T(1024)(128)(4,1)}), s8[4194304]{0:T(1024)(128)(4,1)S(1)}, s32[]{:S(2)}) async-start(s8[5812224]{0:T(1024)(128)(4,1)} %bitcast.214), calls=%async_computation.12 | async-start | bytes 8388608
  246.0 5.9 %slice-start.8 = ((s8[5812224]{0:T(1024)(128)(4,1)}), s8[4194304]{0:T(1024)(128)(4,1)S(1)}, s32[]{:S(2)}) async-start(s8[5812224]{0:T(1024)(128)(4,1)} %bitcast.216), calls=%async_computation.14 | async-start | bytes 8388608
  246.0 6.5 %slice-start.1 = ((s8[5812224]{0:T(1024)(128)(4,1)}), s8[1617920]{0:T(1024)(128)(4,1)S(1)}, s32[]{:S(2)}) async-start(s8[5812224]{0:T(1024)(128)(4,1)} %bitcast.199), calls=%async_computation.7 | async-start | bytes 3235840
  246.0 7.0 %slice-start.7 = ((s8[5812224]{0:T(1024)(128)(4,1)}), s8[1617920]{0:T(1024)(128)(4,1)S(1)}, s32[]{:S(2)}) async-start(s8[5812224]{0:T(1024)(128)(4,1)} %bitcast.214), calls=%async_computation.13 | async-start | bytes 3235840
  246.0 7.4 %slice-start.9 = ((s8[5812224]{0:T(1024)(128)(4,1)}), s8[1617920]{0:T(1024)(128)(4,1)S(1)}, s32[]{:S(2)}) async-start(s8[5812224]{0:T(1024)(128)(4,1)} %bitcast.216), calls=%async_computation.15 | async-start | bytes 3235840
  271.7 13.3 %collective-permute-start.8 = (bf16[1025,1024]{1,0:T(8,128)(2,1)S(1)}, bf16[1025,1024]{1,0:T(8,128)(2,1)}, u32[]{:S(2)}, u32[]{:S(2)}) collective-permute-start(bf16[1025,1024]{1,0:T(8,128)(2,1)S(1)} %fusion.74), channel_id=1, source_target_pairs={{0,1},{1,0},{2,3},{3,2},{4,5},{5,4},{6,7},{7,6},{8,9},{9,8},{10,11... | collective-permute-start | bytes 6297608 | tf_op jit(solution)/shard_map/ppermute | solution.py:74
  285.0 11.8 %copy-start.6 = (bf16[1024,4992]{1,0:T(8,128)(2,1)}, bf16[1024,4992]{1,0:T(8,128)(2,1)S(1)}, u32[]{:S(2)}) copy-start(bf16[1024,4992]{1,0:T(8,128)(2,1)S(1)} %pad_dynamic-update-slice_fusion) | copy-start | bytes 30670852
  285.0 5.6 copy-start.20
  297.1 6.3 %copy-start.28 = (bf16[1025,1024]{1,0:T(8,128)(2,1)S(1)}, bf16[1025,1024]{1,0:T(8,128)(2,1)}, u32[]{:S(2)}) copy-start(bf16[1025,1024]{1,0:T(8,128)(2,1)} %get-tuple-element.97) | copy-start | bytes 6297604
  307.3 263.4 %reduce-scatter.5.cloned.1.call-start = ((), (), s32[]{:S(2)}) async-start(), calls=%async_computation.5 | async-start | bytes 3899392 | tf_op jit(solution)/shard_map/reduce_scatter | solution.py:391
  309.0 100.9 %copy-start.24 = (f32[1025,64]{0,1:T(8,128)S(1)}, f32[1025,64]{0,1:T(8,128)}, u32[]{:S(2)}) copy-start(f32[1025,64]{0,1:T(8,128)} %get-tuple-element.347) | copy-start | bytes 787204
  437.5 14.1 %collective-permute-start.10 = (bf16[1025,1024]{1,0:T(8,128)(2,1)}, bf16[1025,1024]{1,0:T(8,128)(2,1)}, u32[]{:S(2)}, u32[]{:S(2)}) collective-permute-start(bf16[1025,1024]{1,0:T(8,128)(2,1)} %fusion.73), channel_id=1, source_target_pairs={{0,1},{1,0},{2,3},{3,2},{4,5},{5,4},{6,7},{7,6},{8,9},{9,8},{10,11... | collective-permute-start | bytes 6297608 | tf_op jit(solution)/shard_map/ppermute | solution.py:74
  484.5 12.8 %slice-start.4 = ((s8[4227072]{0:T(1024)(128)(4,1)}), s8[32768]{0:T(1024)(128)(4,1)S(1)}, s32[]{:S(2)}) async-start(s8[4227072]{0:T(1024)(128)(4,1)} %bitcast.207), calls=%async_computation.10 | async-start | bytes 65536
  484.6 6.6 %copy-start.30 = (f32[1024,1]{1,0:T(8,128)S(1)}, f32[1024,1]{1,0:T(8,128)}, u32[]{:S(2)}) copy-start(f32[1024,1]{1,0:T(8,128)} %get-tuple-element.336) | copy-start | bytes 12292
  484.6 9.3 %copy-start.36 = (f32[512]{0:T(512)S(1)}, f32[512]{0:T(512)}, u32[]{:S(2)}) copy-start(f32[512]{0:T(512)} %copy-done.35) | copy-start | bytes 6148
  484.6 12.8 %slice-start.5 = ((s8[4227072]{0:T(1024)(128)(4,1)}), s8[4194304]{0:T(1024)(128)(4,1)S(1)}, s32[]{:S(2)}) async-start(s8[4227072]{0:T(1024)(128)(4,1)} %bitcast.207), calls=%async_computation.11 | async-start | bytes 8388608
  491.1 2.7 collective-permute-start.9
  491.2 6.2 %slice-start.2 = ((s8[4227072]{0:T(1024)(128)(4,1)}), s8[4194304]{0:T(1024)(128)(4,1)S(1)}, s32[]{:S(2)}) async-start(s8[4227072]{0:T(1024)(128)(4,1)} %bitcast.205), calls=%async_computation.8 | async-start | bytes 8388608
  491.4 6.0 %slice-start.3 = ((s8[4227072]{0:T(1024)(128)(4,1)}), s8[32768]{0:T(1024)(128)(4,1)S(1)}, s32[]{:S(2)}) async-start(s8[4227072]{0:T(1024)(128)(4,1)} %bitcast.205), calls=%async_computation.9 | async-start | bytes 65536
  (25 other events, 103.4 us)
Sparse Core Ops, SparseCore 0:
  11.4 80.3 all-gather.2
  95.1 113.3 all-gather.4
  307.5 175.8 reduce-scatter.2
  485.5 85.1 reduce-scatter.4
